TPU v7x, 128 devices: a whole 4x4x4 slice. The times are simulated.
128 devices in a mesh: dp: 8 (over y_lo, z), ctx: 16 (over x, y_hi, core).
Axes of the slice: x: 4, y: 4 (y_hi: 2, y_lo: 2; y = y_hi * 2 + y_lo), z: 4, core: 2. Of those that a mesh axis runs over, the one named last changes fastest.
Arguments:
- item_ids: int32 [32, 4096], P('dp', 'ctx'), may hold values from 0 to 131071, as said below
- lengths: int32 [32], P('dp'), may hold values from 512 to 4096
- table: bfloat16 [131072, 512], P('dp'), may hold values from -6 to 6
- w_in: bfloat16 [512, 2048], replicated, may hold values from -0.25 to 0.25
- w_out: bfloat16 [512, 512], replicated, may hold values from -0.25 to 0.25
Outputs:
- layer_out: bfloat16 [32, 4096, 512], P('dp', 'ctx')
Inputs may be any that keep to these rules, and one draw needn't show every extreme that they name: `item_ids`: the owner of an id is id // 16384. In every user's block of 256 positions of one index of ctx, at most 64 ids have one owner; in each such block one owner, the same for all users at that index of ctx, has exactly 64.
All inputs are finite; a program needn't handle non-finite values.
Results may differ from a plain program's by a relative error of at most 0.0054.
Values may be sent and summed in bfloat16 or wider, within the bound.
No kernel may reach another device: no remote copies, remote signals or barrier semaphores. Data moves between devices by JAX's collectives and lax.ppermute only.
A program may use at most 128 MiB of HBM per device.

v0:
```python
import jax, jax.numpy as jnp, functools
from jax import lax
from jax.experimental import pallas as pl
from jax.experimental.pallas import tpu as pltpu
BF=jnp.bfloat16; F32=jnp.float32
BLK=256; D=512

def half_silu(h):
    return h + h*jnp.tanh(h)

def nt(a,b):
    return lax.dot_general(a,b,(((1,),(1,)),((),())),preferred_element_type=F32)
def nn(a,b):
    return jnp.dot(a,b,preferred_element_type=F32)

def kv_kernel(nb, sc_ref, x_ref, wk_ref, wvT_ref, wqT_ref, wgT_ref, k_ref, vT_ref, qT_ref, gT_ref, xq_ref, n_scr, nq_scr):
    def body(i,_):
        place = sc_ref[3+i]
        x = x_ref[pl.ds(pl.multiple_of(i*BLK,BLK),BLK),:].astype(F32)
        mean = jnp.mean(x,axis=1,keepdims=True)
        c = x-mean
        var = jnp.mean(c*c,axis=1,keepdims=True)
        n = (c*lax.rsqrt(var+1e-5)).astype(BF)
        n_scr[...] = n
        row = pl.multiple_of(place*BLK,BLK)
        k_ref[pl.ds(row,BLK),:] = half_silu(nn(n,wk_ref[...])).astype(BF)
        v = half_silu(nt(wvT_ref[...],n))
        pos = sc_ref[2]+place*BLK+lax.broadcasted_iota(jnp.int32,(1,BLK),1)
        vT_ref[:,pl.ds(row,BLK)] = jnp.where(pos<sc_ref[0],v,0.0).astype(BF)
        qo = pl.multiple_of(sc_ref[1],64)
        qrow = pl.multiple_of(place*64,64)
        nq_scr[pl.ds(qrow,64),:] = n_scr[pl.ds(qo,64),:]
        xq_ref[pl.ds(qrow,64),:] = x_ref[pl.ds(pl.multiple_of(i*BLK+qo,64),64),:]
        return 0
    lax.fori_loop(0,nb,body,0)
    nq = nq_scr[...]
    qT_ref[...] = half_silu(nt(wqT_ref[...],nq)).astype(BF)*BF(1/16)
    gT_ref[...] = half_silu(nt(wgT_ref[...],nq)).astype(BF)

def kv_call(nb, sc, x, wk, wvT, wqT, wgT):
    nq=nb*64
    vm=pl.BlockSpec(memory_space=pltpu.VMEM)
    return pl.pallas_call(functools.partial(kv_kernel,nb),
        out_shape=[jax.ShapeDtypeStruct((nb*BLK,D),BF),jax.ShapeDtypeStruct((D,nb*BLK),BF),
                   jax.ShapeDtypeStruct((D,nq),BF),jax.ShapeDtypeStruct((D,nq),BF),jax.ShapeDtypeStruct((nq,D),BF)],
        in_specs=[pl.BlockSpec(memory_space=pltpu.SMEM)]+[vm]*5,
        out_specs=[vm]*5,
        scratch_shapes=[pltpu.VMEM((BLK,D),BF),pltpu.VMEM((nq,D),BF)],
        compiler_params=pltpu.CompilerParams(vmem_limit_bytes=56*1024*1024),
        name="kv",
    )(sc,x,wk,wvT,wqT,wgT)

def attn_kernel(nprev, G, sc_ref, *refs):
    nch=nprev+1
    ks=refs[:nch]; vs=refs[nch:2*nch]
    qT_ref,gT_ref,xq_ref,wo_ref,out_ref,o_scr = refs[2*nch:]
    nb=8
    def head_pair(p,_):
        lane=pl.multiple_of(p*128,128)
        rid=lax.broadcasted_iota(jnp.int32,(128,256),0)
        for t in range(nb//4):
            qT=qT_ref[pl.ds(lane,128),256*t:256*t+256]
            zero=jnp.zeros_like(qT)
            qs=(jnp.where(rid<64,qT,zero),jnp.where(rid<64,zero,qT))
            accs=[None,None]
            for ch in range(nch):
                last = ch==nch-1
                nk = 4*(t+1) if last else nb
                for g in range(0,nk,G):
                    k=ks[ch][g*BLK:(g+G)*BLK,pl.ds(lane,128)]
                    for hh in range(2):
                        s=nn(k,qs[hh])
                        w=s+s*jnp.tanh(s)
                        if last and g+G>4*t:
                            r=lax.broadcasted_iota(jnp.int32,(G*BLK,256),0)+(g-4*t)*BLK
                            cc=lax.broadcasted_iota(jnp.int32,(1,256),1)
                            thr=(cc//64)*256+(cc%64)+sc_ref[1]
                            w=jnp.where(r<=thr,w,0.0)
                        o=nn(vs[ch][pl.ds(pl.multiple_of(lane+64*hh,64),64),g*BLK:(g+G)*BLK],w.astype(BF))
                        accs[hh]=o if accs[hh] is None else accs[hh]+o
            for hh in range(2):
                o_scr[pl.ds(pl.multiple_of(lane+64*hh,64),64),256*t:256*t+256]=accs[hh]
        return 0
    lax.fori_loop(0,4,head_pair,0)
    for t in range(nb//4):
        cs=slice(256*t,256*t+256)
        o=o_scr[:,cs]
        mean=jnp.mean(o,axis=0,keepdims=True)
        c=o-mean
        var=jnp.mean(c*c,axis=0,keepdims=True)
        gated=((c*lax.rsqrt(var+1e-5))*gT_ref[:,cs].astype(F32)).astype(BF)
        mixed=lax.dot_general(gated,wo_ref[...],(((0,),(0,)),((),())),preferred_element_type=F32)
        out_ref[cs,:]=(xq_ref[cs,:].astype(F32)+mixed).astype(BF)

def attn_call(nprev, G, sc, ks, vs, qT, gT, xq, wo):
    vm=pl.BlockSpec(memory_space=pltpu.VMEM)
    n=2*(nprev+1)+4
    return pl.pallas_call(functools.partial(attn_kernel,nprev,G),
        out_shape=jax.ShapeDtypeStruct((512,D),BF),
        in_specs=[pl.BlockSpec(memory_space=pltpu.SMEM)]+[vm]*n,
        out_specs=vm,
        scratch_shapes=[pltpu.VMEM((D,512),F32)],
        compiler_params=pltpu.CompilerParams(vmem_limit_bytes=56*1024*1024),
        name=f"attn{nprev}",
    )(sc,*ks,*vs,qT,gT,xq,wo)


from jax.sharding import Mesh
from jax.sharding import PartitionSpec as P

CTX = ("xh", "xl", "yh", "co")
FLIP = [(0, 1), (1, 0)]


def per_device(item_ids, lengths, table, w_in, w_out):
    owned = table.shape[0]
    me = lax.axis_index("dp")
    xh, xl, yh, co = (lax.axis_index(a) for a in CTX)
    owners = lax.axis_size("dp")
    half = (w_in * 0.5).astype(BF)
    wgT, wvT, wqT = (half[:, D * i : D * (i + 1)].T for i in range(3))
    wk = half[:, 3 * D :]

    send = jnp.broadcast_to(item_ids[None], (owners, 4, BLK)).reshape(owners * 4, BLK)
    wanted = lax.all_to_all(send, ("dp", "xh", "yh"), 0, 0, tiled=True).reshape(owners, 4, BLK)
    mine = lax.dynamic_index_in_dim(wanted, me, 0, keepdims=False)
    length = lax.dynamic_index_in_dim(lengths, 2 * xh + yh, 0, keepdims=False)
    upto = jnp.triu(jnp.ones((2 * BLK, 2 * BLK), BF))

    def ranks(member):
        return nn(member.astype(BF), upto).astype(jnp.int32) - 1

    cap = 2 * 64
    places = []
    for xx, cc in ((xl, co), (1 - xl, co), (xl, 1 - co), (1 - xl, 1 - co)):
        places += [4 * xx + cc, 4 * xx + cc + 2]

    def fetch(c):
        ids = wanted[:, 2 * c : 2 * c + 2].reshape(owners, 2 * BLK)
        local = ids - me * owned
        here = (local >= 0) & (local < owned)
        rank = jnp.where(here, ranks(here), -1)
        slot = lax.broadcasted_iota(jnp.int32, (owners, cap, 2 * BLK), 1)
        rows = jnp.sum(jnp.where(rank[:, None, :] == slot, local[:, None, :], 0), axis=2)
        picked = jnp.take(table, rows.reshape(-1), axis=0, mode="clip").reshape(owners, cap, D)
        got = lax.all_to_all(picked, "dp", 0, 0, tiled=True).reshape(owners * cap, D)
        own_ids = mine[2 * c : 2 * c + 2].reshape(2 * BLK)
        owner = own_ids // owned
        member = owner[None, :] == lax.broadcasted_iota(jnp.int32, (owners, 2 * BLK), 0)
        at = jnp.sum(jnp.where(member, ranks(member), 0), axis=0) + owner * cap
        pick = (at[:, None] == lax.broadcasted_iota(jnp.int32, (2 * BLK, owners * cap), 1)).astype(BF)
        return nn(pick, got).astype(BF)

    def exchange(own):
        far = lax.ppermute(own, "xl", FLIP)
        near = lax.ppermute(own, "co", FLIP)
        diag = lax.ppermute(far, "co", FLIP)
        return jnp.concatenate([own, far, near, diag], axis=0)

    ks, vs, outs = [], [], []
    for c in range(2):
        x = exchange(fetch(c))
        sc = jnp.stack([length, 64 * (2 * xl + co), jnp.int32(8 * BLK * c)] + places).astype(jnp.int32)
        k, v, q, g, xq = kv_call(8, sc, x, wk, wvT, wqT, wgT)
        ks.append(k)
        vs.append(v)
        outs.append(attn_call(c, 4, sc, ks, vs, q, g, xq, w_out))
    out = jnp.concatenate(outs, axis=0).reshape(16, 64, D)
    back = lax.all_to_all(out, CTX, 0, 0, tiled=True)
    back = back.reshape(2, 2, 2, 2, 64, D).transpose(0, 2, 1, 3, 4, 5)
    return back.reshape(4, BLK, D)


def solution(mesh):
    finer = Mesh(mesh.devices.reshape(mesh.shape["dp"], 2, 2, 2, 2), ("dp",) + CTX)
    return jax.shard_map(
        per_device,
        mesh=finer,
        in_specs=(P("dp", CTX), P("dp"), P("dp", None), P(), P()),
        out_specs=P("dp", CTX, None),
        check_vma=False,
    )
```

profile of v0, /device:TPU:8, one launch (start us, length us, event | category | flops | bytes accessed | tf_op | source)
XLA Modules:
  0.0 182.4 jit_solution(9704894883142397905)
XLA Ops:
  1.4 11.0 %all-to-all-start = ((s32[32,1,256]{2,1,0:T(1,128)}), s32[32,1,256]{2,1,0:T(1,128)S(1)}, u32[]{:S(2)}, u32[]{:S(2)}) async-start(s32[32,1,256]{2,1,0:T(1,128)} %all_to_all.15), calls=%async_computation | async-start | bytes 65536 | tf_op jit(solution)/shard_map/all_to_all | solution.py:125
  12.4 2.9 %copy.18 = bf16[512,2048]{0,1:T(8,128)(2,1)S(1)} copy(bf16[512,2048]{1,0:T(8,128)(2,1)} %param.8) | data formatting | bytes 4194304 | tf_op args[3]
  15.3 5.8 %all-to-all-done = s32[32,1,256]{2,1,0:T(1,128)S(1)} async-done(((s32[32,1,256]{2,1,0:T(1,128)}), s32[32,1,256]{2,1,0:T(1,128)S(1)}, u32[]{:S(2)}, u32[]{:S(2)}) %all-to-all-start) | async-done | bytes 32800 | tf_op jit(solution)/shard_map/all_to_all | solution.py:125
  21.8 13.0 %gather_fusion = bf16[1024,512]{1,0:T(8,128)(2,1)} fusion(bf16[16384,512]{1,0:T(8,128)(2,1)} %param.7, s32[1024]{0:T(1024)S(1)} %bitcast_clamp_fusion.1), kind=kCustom, calls=%fused_computation | custom fusion | bytes 2101248 | tf_op jit(solution)/shard_map/jit(_take)/gather | solution.py:145
  34.8 4.9 %all-to-all-start.1 = ((bf16[8,128,512]{2,1,0:T(8,128)(2,1)}), bf16[8,128,512]{2,1,0:T(8,128)(2,1)S(1)}, u32[]{:S(2)}, u32[]{:S(2)}) async-start(bf16[8,128,512]{2,1,0:T(8,128)(2,1)} %bitcast.10), calls=%async_computation.1 | async-start | bytes 2097152 | tf_op jit(solution)/shard_map/all_to_all | solution.py:146
  40.3 13.0 %gather_fusion.1 = bf16[1024,512]{1,0:T(8,128)(2,1)} fusion(bf16[16384,512]{1,0:T(8,128)(2,1)} %param.7, s32[1024]{0:T(1024)S(1)} %bitcast_clamp_fusion), kind=kCustom, calls=%fused_computation.1 | custom fusion | bytes 2101248 | tf_op jit(solution)/shard_map/jit(_take)/gather | solution.py:145
  53.4 5.7 %all-to-all-start.2 = ((bf16[8,128,512]{2,1,0:T(8,128)(2,1)}), bf16[8,128,512]{2,1,0:T(8,128)(2,1)}, u32[]{:S(2)}, u32[]{:S(2)}) async-start(bf16[8,128,512]{2,1,0:T(8,128)(2,1)} %bitcast.16), calls=%async_computation.2 | async-start | bytes 2097152 | tf_op jit(solution)/shard_map/all_to_all | solution.py:146
  59.4 1.6 fusion.3
  61.9 9.8 %all-to-all-done.2 = bf16[8,128,512]{2,1,0:T(8,128)(2,1)} async-done(((bf16[8,128,512]{2,1,0:T(8,128)(2,1)}), bf16[8,128,512]{2,1,0:T(8,128)(2,1)}, u32[]{:S(2)}, u32[]{:S(2)}) %all-to-all-start.2) | async-done | bytes 1048608 | tf_op jit(solution)/shard_map/all_to_all | solution.py:146
  71.8 2.0 %fusion.2 = bf16[512,512]{1,0:T(8,128)(2,1)S(1)} fusion(bf16[1024,512]{1,0:T(8,128)(2,1)} %bitcast.17, s32[512]{0:T(512)S(1)} %multiply_add_fusion), kind=kOutput, calls=%fused_computation.12 | convolution fusion | flops 537657344 | bytes 1574912 | tf_op jit(solution)/shard_map/dot_general | solution.py:14
  74.4 1.5 broadcast_multiply_fusion
  76.4 11.0 %collective-permute-done.3 = bf16[512,512]{1,0:T(8,128)(2,1)} collective-permute-done((bf16[512,512]{1,0:T(8,128)(2,1)S(1)}, bf16[512,512]{1,0:T(8,128)(2,1)}, u32[]{:S(2)}, u32[]{:S(2)}) %collective-permute-start.3) | collective-permute-done | bytes 524320 | tf_op jit(solution)/shard_map/ppermute | solution.py:155
  87.5 2.7 %slice_bitcast_fusion = (bf16[512,512]{1,0:T(8,128)(2,1)}, bf16[512,512]{1,0:T(8,128)(2,1)}, bf16[512,512]{1,0:T(8,128)(2,1)}, bf16[512,512]{0,1:T(8,128)(2,1)S(1)}) fusion(bf16[512,2048]{0,1:T(8,128)(2,1)} %broadcast_multiply_fusion), kind=kLoop, calls=%fused_computation.34 | loop fusion | bytes 4194304 | tf_op jit(solution)/shard_map/transpose | solution.py:121
  91.8 1.2 stack.53.sc_ref
  93.0 1.3 stack.54.sc_ref
  94.3 2.8 %pad_maximum_fusion.x_ref = bf16[2048,512]{1,0:T(8,128)(2,1)} fusion(bf16[512,512]{1,0:T(8,128)(2,1)} %collective-permute-done.2, bf16[512,512]{1,0:T(8,128)(2,1)} %collective-permute-done.1, bf16[512,512]{1,0:T(8,128)(2,1)S(1)} %collective-permute-done, bf16[512,512]{1,0:T(8,128)(2,1)} %fusion.3), kind=kLoop, calls=%fused_computation.2 | loop fusion | flops 8388608 | bytes 4194304 | tf_op jit(solution)/shard_map/concatenate | solution.py:158
  97.1 9.6 %kv.2 = (bf16[2048,512]{1,0:T(8,128)(2,1)}, bf16[512,2048]{1,0:T(8,128)(2,1)}, bf16[512,512]{1,0:T(8,128)(2,1)}, bf16[512,512]{1,0:T(8,128)(2,1)}, bf16[512,512]{1,0:T(8,128)(2,1)}) custom-call(s32[11]{0:T(128)} %stack.53.sc_ref, bf16[2048,512]{1,0:T(8,128)(2,1)} %pad_maximum_fusion.x_ref, bf16[512,512]{1,0:T(8,128)(2,1)} %copy.19.wk_ref, ...), custom_call_target="tpu_custom_call" | custom-call | tf_op jit(solution)/shard_map/kv/pallas_call | solution.py:43
  106.8 2.5 %pad_maximum_fusion.1.x_ref = bf16[2048,512]{1,0:T(8,128)(2,1)} fusion(bf16[512,512]{1,0:T(8,128)(2,1)S(1)} %collective-permute-done.5, bf16[512,512]{1,0:T(8,128)(2,1)S(1)} %collective-permute-done.4, bf16[512,512]{1,0:T(8,128)(2,1)} %collective-permute-done.3, bf16[512,512]{1,0:T(8,128)(2,1)S(1)} %fusion.2), kind=kLoop, calls=%fused_computation.3 | loop fusion | flops 8388608 | bytes 4194304 | tf_op jit(solution)/shard_map/concatenate | solution.py:158
  109.3 9.5 %kv.3 = (bf16[2048,512]{1,0:T(8,128)(2,1)}, bf16[512,2048]{1,0:T(8,128)(2,1)}, bf16[512,512]{1,0:T(8,128)(2,1)}, bf16[512,512]{1,0:T(8,128)(2,1)}, bf16[512,512]{1,0:T(8,128)(2,1)}) custom-call(s32[11]{0:T(128)} %stack.54.sc_ref, bf16[2048,512]{1,0:T(8,128)(2,1)} %pad_maximum_fusion.1.x_ref, bf16[512,512]{1,0:T(8,128)(2,1)} %copy.19.wk_ref, ...), custom_call_target="tpu_custom_call" | custom-call | tf_op jit(solution)/shard_map/kv/pallas_call | solution.py:43
  118.8 13.2 %attn0.1 = bf16[512,512]{1,0:T(8,128)(2,1)} custom-call(s32[11]{0:T(128)} %stack.53.sc_ref, bf16[2048,512]{1,0:T(8,128)(2,1)} %get-tuple-element.15.refs_0_, bf16[512,2048]{1,0:T(8,128)(2,1)} %get-tuple-element.16.refs_1_.refs_2_, bf16[512,512]{1,0:T(8,128)(2,1)} %get-tuple-element.17.refs_2_, bf16[512,512]{1,0:T(8,128)(2,1)} %get-tuple-element.18.refs_3_, ...), custom_call_target="tpu_custom_call" | custom-call | tf_op jit(solution)/shard_map/attn0/pallas_call | solution.py:98
  132.0 27.6 %attn1.1 = bf16[512,512]{1,0:T(8,128)(2,1)} custom-call(s32[11]{0:T(128)} %stack.54.sc_ref, bf16[2048,512]{1,0:T(8,128)(2,1)} %get-tuple-element.15.refs_0_, bf16[2048,512]{1,0:T(8,128)(2,1)} %get-tuple-element.20.refs_1_, bf16[512,2048]{1,0:T(8,128)(2,1)} %get-tuple-element.16.refs_1_.refs_2_, bf16[512,2048]{1,0:T(8,128)(2,1)} %get-tuple-element.21.refs_3_, ...), custom_call_target="tpu_custom_call" | custom-call | tf_op jit(solution)/shard_map/attn1/pallas_call | solution.py:98
  159.6 1.1 pad_maximum_fusion.2
  160.7 20.6 %all_to_all.24 = bf16[16,64,512]{2,1,0:T(8,128)(2,1)S(1)} all-to-all(bf16[16,64,512]{2,1,0:T(8,128)(2,1)S(1)} %bitcast.42), channel_id=1, replica_groups=mesh['dp'=8,'xh'=2,'xl'=2,'yh'=2,'co'=2] {'xh','xl','yh','co'}, dimensions={0} | all-to-all | bytes 2097152 | tf_op jit(solution)/shard_map/all_to_all | solution.py:169
  181.3 1.1 copy.21
  (41 shorter events, 6.6 us)
Async XLA Ops:
  1.4 19.8 %all-to-all-start = ((s32[32,1,256]{2,1,0:T(1,128)}), s32[32,1,256]{2,1,0:T(1,128)S(1)}, u32[]{:S(2)}, u32[]{:S(2)}) async-start(s32[32,1,256]{2,1,0:T(1,128)} %all_to_all.15), calls=%async_computation | async-start | bytes 65536 | tf_op jit(solution)/shard_map/all_to_all | solution.py:125
  34.8 18.5 %all-to-all-start.1 = ((bf16[8,128,512]{2,1,0:T(8,128)(2,1)}), bf16[8,128,512]{2,1,0:T(8,128)(2,1)S(1)}, u32[]{:S(2)}, u32[]{:S(2)}) async-start(bf16[8,128,512]{2,1,0:T(8,128)(2,1)} %bitcast.10), calls=%async_computation.1 | async-start | bytes 2097152 | tf_op jit(solution)/shard_map/all_to_all | solution.py:146
  53.4 18.4 %all-to-all-start.2 = ((bf16[8,128,512]{2,1,0:T(8,128)(2,1)}), bf16[8,128,512]{2,1,0:T(8,128)(2,1)}, u32[]{:S(2)}, u32[]{:S(2)}) async-start(bf16[8,128,512]{2,1,0:T(8,128)(2,1)} %bitcast.16), calls=%async_computation.2 | async-start | bytes 2097152 | tf_op jit(solution)/shard_map/all_to_all | solution.py:146
  61.0 13.4 %collective-permute-start = (bf16[512,512]{1,0:T(8,128)(2,1)}, bf16[512,512]{1,0:T(8,128)(2,1)S(1)}, u32[]{:S(2)}, u32[]{:S(2)}) collective-permute-start(bf16[512,512]{1,0:T(8,128)(2,1)} %fusion.3), channel_id=1, source_target_pairs={{0,4},{4,0},{1,5},{5,1},{2,6},{6,2},{3,7},{7,3},{8,12},{12,8},{9,1... | collective-permute-start | bytes 1572872 | tf_op jit(solution)/shard_map/ppermute | solution.py:155
  61.8 32.4 %collective-permute-start.1 = (bf16[512,512]{1,0:T(8,128)(2,1)}, bf16[512,512]{1,0:T(8,128)(2,1)}, u32[]{:S(2)}, u32[]{:S(2)}) collective-permute-start(bf16[512,512]{1,0:T(8,128)(2,1)} %fusion.3), channel_id=1, source_target_pairs={{0,1},{1,0},{2,3},{3,2},{4,5},{5,4},{6,7},{7,6},{8,9},{9,8},{10,11... | collective-permute-start | bytes 1572872 | tf_op jit(solution)/shard_map/ppermute | solution.py:156
  73.7 13.7 %collective-permute-start.3 = (bf16[512,512]{1,0:T(8,128)(2,1)S(1)}, bf16[512,512]{1,0:T(8,128)(2,1)}, u32[]{:S(2)}, u32[]{:S(2)}) collective-permute-start(bf16[512,512]{1,0:T(8,128)(2,1)S(1)} %fusion.2), channel_id=1, source_target_pairs={{0,4},{4,0},{1,5},{5,1},{2,6},{6,2},{3,7},{7,3},{8,12},{12,8},{9,1... | collective-permute-start | bytes 1572872 | tf_op jit(solution)/shard_map/ppermute | solution.py:155
  74.4 19.9 %collective-permute-start.2 = (bf16[512,512]{1,0:T(8,128)(2,1)S(1)}, bf16[512,512]{1,0:T(8,128)(2,1)}, u32[]{:S(2)}, u32[]{:S(2)}) collective-permute-start(bf16[512,512]{1,0:T(8,128)(2,1)S(1)} %collective-permute-done), channel_id=1, source_target_pairs={{0,1},{1,0},{2,3},{3,2},{4,5},{5,4},{6,7},{7,6},{8,9},{9,8},{10,11... | collective-permute-start | bytes 1572872 | tf_op jit(solution)/shard_map/ppermute | solution.py:157
  75.9 15.3 %copy-start.1 = (s32[4]{0:T(128)S(1)}, s32[4]{0:T(128)}, u32[]{:S(2)}) copy-start(s32[4]{0:T(128)} %param.6) | copy-start | bytes 52
  75.9 30.8 %collective-permute-start.4 = (bf16[512,512]{1,0:T(8,128)(2,1)S(1)}, bf16[512,512]{1,0:T(8,128)(2,1)S(1)}, u32[]{:S(2)}, u32[]{:S(2)}) collective-permute-start(bf16[512,512]{1,0:T(8,128)(2,1)S(1)} %fusion.2), channel_id=1, source_target_pairs={{0,1},{1,0},{2,3},{3,2},{4,5},{5,4},{6,7},{7,6},{8,9},{9,8},{10,11... | collective-permute-start | bytes 1572872 | tf_op jit(solution)/shard_map/ppermute | solution.py:156
  87.5 19.3 %collective-permute-start.5 = (bf16[512,512]{1,0:T(8,128)(2,1)}, bf16[512,512]{1,0:T(8,128)(2,1)S(1)}, u32[]{:S(2)}, u32[]{:S(2)}) collective-permute-start(bf16[512,512]{1,0:T(8,128)(2,1)} %collective-permute-done.3), channel_id=1, source_target_pairs={{0,1},{1,0},{2,3},{3,2},{4,5},{5,4},{6,7},{7,6},{8,9},{9,8},{10,11... | collective-permute-start | bytes 1572872 | tf_op jit(solution)/shard_map/ppermute | solution.py:157
  132.0 27.6 %copy-start = (bf16[512,512]{1,0:T(8,128)(2,1)S(1)}, bf16[512,512]{1,0:T(8,128)(2,1)}, u32[]{:S(2)}) copy-start(bf16[512,512]{1,0:T(8,128)(2,1)} %attn0.1) | copy-start | bytes 1572868
where the time goes:
time: 183 us; the launch traced here: 182 us
  Pallas kernels  60 us (33%)
  local copies, waits for them, and re-layouts  38.2 us (21%)
  waiting for transfers between devices  26.7 us (15%)
  starting transfers between devices  23.5 us (13%)
  blocking collectives  20.6 us (11%)
  other arithmetic  8.67 us (5%)
  matrix products  4.56 us (2%)
    pallas_call x2, Pallas kernels, attn_call(): pl.pallas_call(functools.partial(attn_kernel, nprev, G), out_shape=jax.Sh...  40.8 us
    gather x2, local copies, waits for them, and re-layouts, fetch(): jnp.take(table, rows.reshape(-1), axis=0, mode='clip')  26.1 us
    all_to_all x1, blocking collectives, per_device(): back = lax.all_to_all(out, CTX, 0, 0, tiled=True)  20.6 us
    pallas_call x2, Pallas kernels, kv_call(): pl.pallas_call(functools.partial(kv_kernel, nb), out_shape=[jax.ShapeDtyp...  19.2 us
    ppermute x2, waiting for transfers between devices, exchange(): far = lax.ppermute(own, 'xl', FLIP)  11 us
    all_to_all x1, starting transfers between devices, per_device(): lax.all_to_all(send, ('dp', 'xh', 'yh'), 0, 0, tiled=True)  11 us
    all_to_all x2, starting transfers between devices, fetch(): lax.all_to_all(picked, 'dp', 0, 0, tiled=True).reshape(owners * cap, D)  10.6 us
    all_to_all x2, waiting for transfers between devices, fetch(): lax.all_to_all(picked, 'dp', 0, 0, tiled=True).reshape(owners * cap, D)  9.82 us
  transfers between devices with their start and end apart: 9, of which 3 were waited for; matrix products, arithmetic and copies ran while one was open for 17% of the time, Pallas kernels for 5%

commit v1 on v0

v1 whole, which is shorter than its diff:
```python
import functools

import jax
import jax.numpy as jnp
from jax import lax
from jax.experimental import pallas as pl
from jax.experimental.pallas import tpu as pltpu

BF = jnp.bfloat16
F32 = jnp.float32
BLK = 256
D = 512
GRP = 1024
PART = 64
CAP = 128
VM = pl.BlockSpec(memory_space=pltpu.VMEM)
SM = pl.BlockSpec(memory_space=pltpu.SMEM)
ANY = pl.BlockSpec(memory_space=pl.ANY)
PARAMS = pltpu.CompilerParams(vmem_limit_bytes=56 * 1024 * 1024)
BUNCH = 32


def twice_silu(h):
    return h + h * jnp.tanh(h)


def nt(a, b):
    return lax.dot_general(a, b, (((1,), (1,)), ((), ())), preferred_element_type=F32)


def nn(a, b):
    return jnp.dot(a, b, preferred_element_type=F32)


def gather_kernel(owners, rows_ref, count_ref, low_ref, table_ref, out_ref, buf, sems):
    bunches = CAP // BUNCH

    def real(o, b):
        return b * BUNCH < count_ref[o]

    def copy(o, b, i):
        at = o * CAP + b * BUNCH + i
        return pltpu.make_async_copy(
            table_ref.at[lax.shift_right_logical(rows_ref[o, b * BUNCH + i], 3)],
            buf.at[at],
            sems.at[o * bunches + b],
        )

    def start(k, _):
        o = k // bunches
        b = k % bunches

        @pl.when(real(o, b))
        def _():
            for i in range(BUNCH):
                copy(o, b, i).start()

        return 0

    lax.fori_loop(0, owners * bunches, start, 0)
    width = BUNCH * 8
    lane = lax.broadcasted_iota(jnp.int32, (BUNCH, width), 1)
    base = 8 * lax.broadcasted_iota(jnp.int32, (BUNCH, 1), 0)
    for o in range(owners):
        for b in range(bunches):
            dst = slice(o * CAP + b * BUNCH, o * CAP + (b + 1) * BUNCH)

            @pl.when(real(o, b))
            def _():
                pltpu.make_async_copy(buf.at[dst], buf.at[dst], sems.at[o * bunches + b]).wait()
                want = base + low_ref[b * BUNCH : (b + 1) * BUNCH, o : o + 1]
                pick = (lane == want).astype(F32).astype(BF)
                got = buf[dst].reshape(width, D)
                out_ref[dst, :] = nn(pick, got).astype(BF)

            @pl.when(jnp.logical_not(real(o, b)))
            def _():
                out_ref[dst, :] = jnp.zeros((BUNCH, D), BF)


def gather_call(rows, count, low, table):
    owners = rows.shape[0]
    return pl.pallas_call(
        functools.partial(gather_kernel, owners),
        out_shape=jax.ShapeDtypeStruct((owners * CAP, D), BF),
        in_specs=[SM, SM, VM, ANY],
        out_specs=VM,
        scratch_shapes=[
            pltpu.VMEM((owners * CAP, 8, D), BF),
            pltpu.SemaphoreType.DMA((owners * CAP // BUNCH,)),
        ],
        compiler_params=PARAMS,
        name="gather",
    )(rows, count, low, table.reshape(-1, 8, D))


def kv_kernel(
    first, group_at, sc_ref, p1_ref, p2_ref, wk_ref, wv_ref, wq_ref, wg_ref, k_ref, v_ref, q_ref, g_ref, xq_ref, n_scr, nq_scr
):
    co = sc_ref[2]
    base = first + GRP * sc_ref[group_at]
    qo = pl.multiple_of(sc_ref[1], PART)
    for s, ref in enumerate((p1_ref, p2_ref)):
        x = ref[...].astype(F32)
        c = x - jnp.mean(x, axis=1, keepdims=True)
        var = jnp.mean(c * c, axis=1, keepdims=True)
        n_scr[s] = (c * lax.rsqrt(var + 1e-5)).astype(BF)
    for s, ref in enumerate((p1_ref, p2_ref)):
        edge = co if s == 0 else 1 - co
        n = n_scr[s]
        k = twice_silu(0.5 * nn(n, wk_ref[...])).astype(BF)
        v = twice_silu(0.5 * nt(wv_ref[...], n))
        for j in range(2):
            at = pl.multiple_of((edge + 2 * j) * BLK, BLK)
            k_ref[pl.ds(at, BLK), :] = k[j * BLK : (j + 1) * BLK]
            pos = base + at + lax.broadcasted_iota(jnp.int32, (1, BLK), 1)
            v_ref[:, pl.ds(at, BLK)] = jnp.where(pos < sc_ref[0], v[:, j * BLK : (j + 1) * BLK], 0.0).astype(BF)
            to = pl.multiple_of((edge + 2 * j) * PART, PART)
            nq_scr[pl.ds(to, PART), :] = n_scr[s, pl.ds(j * BLK + qo, PART), :]
            xq_ref[pl.ds(to, PART), :] = ref[pl.ds(j * BLK + qo, PART), :]
    nq = nq_scr[...]
    q_ref[...] = twice_silu(0.5 * nt(wq_ref[...], nq)).astype(BF) * BF(1 / 16)
    g_ref[...] = twice_silu(0.5 * nt(wg_ref[...], nq)).astype(BF)


def kv_call(first, group_at, sc, p1, p2, w_in, w_turned):
    def part(i):
        return pl.BlockSpec((D, D), lambda _: (i, 0))

    def whole(shape):
        return pl.BlockSpec(shape, lambda _: (0,) * len(shape))

    quarter = GRP // 4
    shapes = [(GRP, D), (D, GRP), (D, quarter), (D, quarter), (quarter, D)]
    return pl.pallas_call(
        functools.partial(kv_kernel, first, group_at),
        grid=(1,),
        out_shape=[jax.ShapeDtypeStruct(s, BF) for s in shapes],
        in_specs=[SM, whole((D, D)), whole((D, D)), pl.BlockSpec((D, D), lambda _: (0, 3)), part(1), part(2), part(0)],
        out_specs=[whole(s) for s in shapes],
        scratch_shapes=[pltpu.VMEM((2, D, D), BF), pltpu.VMEM((quarter, D), BF)],
        compiler_params=PARAMS,
        name="kv",
    )(sc, p1, p2, w_in, w_turned, w_turned, w_turned)


def attn_kernel(chunk, sc_ref, *refs):
    halves = 2 * (chunk + 1)
    k_in, v_in = refs[:halves], refs[halves : 2 * halves]
    q_in, g_in, x_in = (refs[2 * halves + 2 * i : 2 * halves + 2 * i + 2] for i in range(3))
    w_ref = refs[2 * halves + 6]
    out_ref, k_scr, v_scr, q_scr, g_scr, x_scr, o_scr, r_scr, sems, out_sem = refs[-10:]
    copies = []
    for i in range(halves):
        grp = 2 * (i // 2) + sc_ref[3 + i % 2]
        pairs = [(k_in[i], k_scr, grp), (v_in[i], v_scr, grp)]
        if i >= halves - 2:
            side = sc_ref[3 + i % 2]
            pairs += [(a[i % 2], s, side) for a, s in ((q_in, q_scr), (g_in, g_scr), (x_in, x_scr))]
        for src, dst, to in pairs:
            copies.append(pltpu.make_async_copy(src, dst.at[to], sems.at[len(copies)]))
    for c in copies:
        c.start()
    for c in copies:
        c.wait()
    rid = lax.broadcasted_iota(jnp.int32, (128, 256), 0)
    col = lax.broadcasted_iota(jnp.int32, (1, 512), 1) & 255
    last_key = (col // PART) * BLK + (col % PART) + sc_ref[1]
    key = lax.broadcasted_iota(jnp.int32, (BLK, 512), 0)

    def head_pair(p, _):
        lane = pl.multiple_of(p * 128, 128)
        steps = [(t, g, i) for t in range(2) for g in range(2 * chunk + t + 1) for i in range(4)]
        queries = []
        for t in range(2):
            q = q_scr[t, pl.ds(lane, 128), :]
            zero = jnp.zeros_like(q)
            queries.append(jnp.concatenate([jnp.where(rid < 64, q, zero), jnp.where(rid < 64, zero, q)], axis=1))

        def scores(step):
            t, g, i = step
            return nn(k_scr[g, i * BLK : (i + 1) * BLK, pl.ds(lane, 128)], queries[t])

        def weights(step, s):
            t, g, i = step
            w = s + s * jnp.tanh(s)
            if g == 2 * chunk + t:
                w = jnp.where(key + i * BLK <= last_key, w, 0.0)
            return w.astype(BF)

        sums = [None, None]

        def gather_values(step, w):
            t, g, i = step
            o = nn(v_scr[g, pl.ds(lane, 128), i * BLK : (i + 1) * BLK], w)
            o = (o[:64, :256], o[64:, 256:])
            sums[t] = o if sums[t] is None else (sums[t][0] + o[0], sums[t][1] + o[1])

        s = scores(steps[0])
        before = None
        for n, step in enumerate(steps):
            ahead = scores(steps[n + 1]) if n + 1 < len(steps) else None
            w = weights(step, s)
            if before is not None:
                gather_values(steps[n - 1], before)
            before, s = w, ahead
        gather_values(steps[-1], before)
        for t in range(2):
            for hh in range(2):
                o_scr[t, pl.ds(pl.multiple_of(lane + 64 * hh, 64), 64), :] = sums[t][hh]
        return 0

    lax.fori_loop(0, 4, head_pair, 0)
    for t in range(2):
        o = o_scr[t]
        c = o - jnp.mean(o, axis=0, keepdims=True)
        var = jnp.mean(c * c, axis=0, keepdims=True)
        gated = ((c * lax.rsqrt(var + 1e-5)) * g_scr[t].astype(F32)).astype(BF)
        mixed = lax.dot_general(gated, w_ref[...], (((0,), (0,)), ((), ())), preferred_element_type=F32)
        r_scr[t * 256 : (t + 1) * 256, :] = (x_scr[t].astype(F32) + mixed).astype(BF)
    done = pltpu.make_async_copy(r_scr, out_ref.at[pl.ds(chunk * 512, 512)], out_sem)
    done.start()
    done.wait()


def attn_call(chunk, sc, ks, vs, qs, gs, xs, w_out, previous):
    halves = 2 * (chunk + 1)
    inputs = [sc, *ks, *vs, *qs, *gs, *xs, w_out]
    specs = [SM] + [ANY] * (2 * halves + 6) + [VM]
    alias = {}
    if previous is not None:
        alias = {len(inputs): 0}
        inputs.append(previous)
        specs.append(ANY)
    return pl.pallas_call(
        functools.partial(attn_kernel, chunk),
        out_shape=jax.ShapeDtypeStruct((1024, D), BF),
        in_specs=specs,
        out_specs=ANY,
        input_output_aliases=alias,
        scratch_shapes=[
            pltpu.VMEM((halves, GRP, D), BF),
            pltpu.VMEM((halves, D, GRP), BF),
            pltpu.VMEM((2, D, 256), BF),
            pltpu.VMEM((2, D, 256), BF),
            pltpu.VMEM((2, 256, D), BF),
            pltpu.VMEM((2, D, 256), F32),
            pltpu.VMEM((512, D), BF),
            pltpu.SemaphoreType.DMA((2 * halves + 6,)),
            pltpu.SemaphoreType.DMA,
        ],
        compiler_params=PARAMS,
        name="attend" + str(chunk),
    )(*inputs)


from jax.sharding import Mesh
from jax.sharding import PartitionSpec as P

CTX = ("xh", "xl", "yh", "co")
FLIP = [(0, 1), (1, 0)]


def per_device(item_ids, lengths, table, w_in, w_out):
    owned = table.shape[0]
    me = lax.axis_index("dp")
    xh, xl, yh, co = (lax.axis_index(a) for a in CTX)
    owners = lax.axis_size("dp")
    w_turned = w_in.T

    send = jnp.broadcast_to(item_ids[None], (owners, 4, BLK)).reshape(owners * 4, BLK)
    wanted = lax.all_to_all(send, ("dp", "xh", "yh"), 0, 0, tiled=True).reshape(owners, 4, BLK)
    mine = lax.dynamic_index_in_dim(wanted, me, 0, keepdims=False)
    user = 2 * xh + yh
    length = jnp.sum(jnp.where(lax.iota(jnp.int32, 4) == user, lengths, 0))
    upto = jnp.triu(jnp.ones((2 * BLK, 2 * BLK), BF))
    slots = lax.iota(jnp.int32, 8)
    sc = jnp.zeros((8,), jnp.int32)
    for i, value in enumerate((length, PART * (2 * xl + co), co, xl, 1 - xl)):
        sc = jnp.where(slots == i, value, sc)

    def ranks(member):
        return nn(member.astype(BF), upto).astype(jnp.int32) - 1

    def fetch(c):
        ids = wanted[:, 2 * c : 2 * c + 2].reshape(owners, 2 * BLK)
        local = ids - me * owned
        here = (local >= 0) & (local < owned)
        rank = jnp.where(here, ranks(here), -1)
        slot = lax.broadcasted_iota(jnp.int32, (owners, CAP, 2 * BLK), 1)
        rows = jnp.sum(jnp.where(rank[:, None, :] == slot, local[:, None, :], 0), axis=2)
        count = jnp.sum(here.astype(jnp.int32), axis=1)
        picked = gather_call(rows, count, (rows & 7).T, table).reshape(owners, CAP, D)
        return lax.all_to_all(picked, "dp", 0, 0, tiled=True).reshape(owners * CAP, D)

    def place(c, got):
        own_ids = mine[2 * c : 2 * c + 2].reshape(2 * BLK)
        owner = own_ids // owned
        member = owner[None, :] == lax.broadcasted_iota(jnp.int32, (owners, 2 * BLK), 0)
        at = jnp.sum(jnp.where(member, ranks(member), 0), axis=0) + owner * CAP
        pick = (at[:, None] == lax.broadcasted_iota(jnp.int32, (2 * BLK, owners * CAP), 1)).astype(BF)
        return nn(pick, got).astype(BF)

    ks, vs, out = [], [], None
    for c in range(2):
        own = place(c, fetch(c))
        far = lax.ppermute(own, "xl", FLIP)
        near = lax.ppermute(own, "co", FLIP)
        diag = lax.ppermute(far, "co", FLIP)
        first = 2 * GRP * c
        k0, v0, q0, g0, x0 = kv_call(first, 3, sc, own, near, w_in, w_turned)
        k1, v1, q1, g1, x1 = kv_call(first, 4, sc, far, diag, w_in, w_turned)
        ks += [k0, k1]
        vs += [v0, v1]
        out = attn_call(c, sc, ks, vs, (q0, q1), (g0, g1), (x0, x1), w_out, out)
    back = lax.all_to_all(out.reshape(16, PART, D), CTX, 0, 0, tiled=True)
    back = back.reshape(2, 2, 2, 2, PART, D).transpose(0, 2, 1, 3, 4, 5)
    return back.reshape(4, BLK, D)


def solution(mesh):
    finer = Mesh(mesh.devices.reshape(mesh.shape["dp"], 2, 2, 2, 2), ("dp",) + CTX)
    return jax.shard_map(
        per_device,
        mesh=finer,
        in_specs=(P("dp", CTX), P("dp"), P("dp", None), P(), P()),
        out_specs=P("dp", CTX, None),
        check_vma=False,
    )
```

time: 183 us -> 167 us (0.913)
  local copies, waits for them, and re-layouts: 38.2 us -> 6 us
  Pallas kernels: 60 us -> 72.1 us
  waiting for transfers between devices: 26.7 us -> 34.6 us
  other arithmetic: 8.67 us -> 4.63 us
    gather x2 -> x0, local copies, waits for them, and re-layouts: 26.1 us -> none  [fetch(): jnp.take(table, rows.reshape(-1), axis=0, mode='clip')]
    pallas_call x4 -> x8, Pallas kernels: 60 us -> 72.1 us  [the longest x2 31.8 us: attn_call(): pl.pallas_call(functools.partial(attn_kernel, chunk), out_shape=jax.Shape...]
    concatenate x3 -> x0, other arithmetic: 6.46 us -> none  [the longest x2 5.35 us: exchange(): return jnp.concatenate([own, far, near, diag], axis=0)]
    all_to_all x1, waiting for transfers between devices: 5.85 us -> 8.72 us  [per_device(): lax.all_to_all(send, ('dp', 'xh', 'yh'), 0, 0, tiled=True)]
    all_to_all x2, waiting for transfers between devices: 9.82 us -> 12.6 us  [fetch(): lax.all_to_all(picked, 'dp', 0, 0, tiled=True).reshape(owners * CAP, D)]
    transpose x1 -> x0, local copies, waits for them, and re-layouts: 2.69 us -> none  [per_device(): wgT, wvT, wqT = (half[:, D * i:D * (i + 1)].T for i in range(3))]
    another operation x2 -> x0, local copies, waits for them, and re-layouts: 2.51 us -> none  [per_device(): jnp.stack([length, 64 * (2 * xl + co), jnp.int32(8 * BLK * c)] + places)]
    ppermute x6, waiting for transfers between devices: 11.1 us -> 13.3 us  [the longest x2 13.2 us: per_device(): far = lax.ppermute(own, 'xl', FLIP)]
  transfers between devices with their start and end apart: 9 -> 9, of which waited for: 3 -> 4; matrix products, arithmetic and copies ran while one was open for 17% -> 6% of each run, Pallas kernels for 5% -> 23%
where the time goes in v1:
time: 167 us; the launch traced here: 166 us
  Pallas kernels  72.1 us (43%)
  waiting for transfers between devices  34.6 us (21%)
  starting transfers between devices  22.9 us (14%)
  blocking collectives  21.6 us (13%)
  local copies, waits for them, and re-layouts  6 us (4%)
  other arithmetic  4.63 us (3%)
  matrix products  4.16 us (2%)
    pallas_call x2, Pallas kernels, attn_call(): pl.pallas_call(functools.partial(attn_kernel, chunk), out_shape=jax.Shape...  31.8 us
    pallas_call x4, Pallas kernels, kv_call(): pl.pallas_call(functools.partial(kv_kernel, first, group_at), grid=(1,),...  21.9 us
    all_to_all x1, blocking collectives, per_device(): back = lax.all_to_all(out.reshape(16, PART, D), CTX, 0, 0, tiled=True)  21.6 us
    pallas_call x2, Pallas kernels, gather_call(): pl.pallas_call(functools.partial(gather_kernel, owners), out_shape=jax.Sh...  18.4 us
    ppermute x2, waiting for transfers between devices, per_device(): far = lax.ppermute(own, 'xl', FLIP)  13.2 us
    all_to_all x2, waiting for transfers between devices, fetch(): lax.all_to_all(picked, 'dp', 0, 0, tiled=True).reshape(owners * CAP, D)  12.6 us
    all_to_all x1, starting transfers between devices, per_device(): lax.all_to_all(send, ('dp', 'xh', 'yh'), 0, 0, tiled=True)  11 us
    all_to_all x2, starting transfers between devices, fetch(): lax.all_to_all(picked, 'dp', 0, 0, tiled=True).reshape(owners * CAP, D)  10.2 us
  transfers between devices with their start and end apart: 9, of which 4 were waited for; matrix products, arithmetic and copies ran while one was open for 6% of the time, Pallas kernels for 23%

profile of v1, /device:TPU:8, one launch (start us, length us, event | category | flops | bytes accessed | tf_op | source)
XLA Modules:
  0.0 166.2 jit_solution(5569707059148843246)
XLA Ops:
  1.4 11.0 %all-to-all-start = ((s32[32,1,256]{2,1,0:T(1,128)}), s32[32,1,256]{2,1,0:T(1,128)S(1)}, u32[]{:S(2)}, u32[]{:S(2)}) async-start(s32[32,1,256]{2,1,0:T(1,128)} %all_to_all.15), calls=%async_computation | async-start | bytes 65536 | tf_op jit(solution)/shard_map/all_to_all | solution.py:272
  12.4 8.7 %all-to-all-done = s32[32,1,256]{2,1,0:T(1,128)S(1)} async-done(((s32[32,1,256]{2,1,0:T(1,128)}), s32[32,1,256]{2,1,0:T(1,128)S(1)}, u32[]{:S(2)}, u32[]{:S(2)}) %all-to-all-start) | async-done | bytes 32800 | tf_op jit(solution)/shard_map/all_to_all | solution.py:272
  21.2 0.9 fusion.34
  23.4 8.1 %gather.2 = bf16[1024,512]{1,0:T(8,128)(2,1)} custom-call(s32[8,128]{1,0:T(8,128)} %copy-done.4, s32[8]{0:T(128)} %get-tuple-element.46.count_ref, s32[128,8]{1,0:T(8,128)} %and_bitcast_fusion.1.low_ref, bf16[2048,8,512]{2,1,0:T(8,128)(2,1)} %bitcast.41), custom_call_target="tpu_custom_call" | custom-call | tf_op jit(solution)/shard_map/gather/pallas_call | solution.py:83
  31.5 6.0 %all-to-all-start.1 = ((bf16[8,128,512]{2,1,0:T(8,128)(2,1)}), bf16[8,128,512]{2,1,0:T(8,128)(2,1)S(1)}, u32[]{:S(2)}, u32[]{:S(2)}) async-start(bf16[8,128,512]{2,1,0:T(8,128)(2,1)} %bitcast.44), calls=%async_computation.1 | async-start | bytes 2097152 | tf_op jit(solution)/shard_map/all_to_all | solution.py:294
  38.9 10.3 %gather.3 = bf16[1024,512]{1,0:T(8,128)(2,1)} custom-call(s32[8,128]{1,0:T(8,128)} %copy-done.3, s32[8]{0:T(128)} %get-tuple-element.45.count_ref, s32[128,8]{1,0:T(8,128)} %and_bitcast_fusion.low_ref, bf16[2048,8,512]{2,1,0:T(8,128)(2,1)} %bitcast.42), custom_call_target="tpu_custom_call" | custom-call | tf_op jit(solution)/shard_map/gather/pallas_call | solution.py:83
  49.2 1.5 all-to-all-done.1
  50.7 4.2 %all-to-all-start.2 = ((bf16[8,128,512]{2,1,0:T(8,128)(2,1)}), bf16[8,128,512]{2,1,0:T(8,128)(2,1)S(1)}, u32[]{:S(2)}, u32[]{:S(2)}) async-start(bf16[8,128,512]{2,1,0:T(8,128)(2,1)} %bitcast.45), calls=%async_computation.2 | async-start | bytes 2097152 | tf_op jit(solution)/shard_map/all_to_all | solution.py:294
  55.4 1.5 fusion.3.p1_ref
  57.0 1.1 collective-permute-start.1
  58.1 11.2 %all-to-all-done.2 = bf16[8,128,512]{2,1,0:T(8,128)(2,1)S(1)} async-done(((bf16[8,128,512]{2,1,0:T(8,128)(2,1)}), bf16[8,128,512]{2,1,0:T(8,128)(2,1)S(1)}, u32[]{:S(2)}, u32[]{:S(2)}) %all-to-all-start.2) | async-done | bytes 1048608 | tf_op jit(solution)/shard_map/all_to_all | solution.py:294
  69.3 1.6 fusion.2.p1_ref
  71.4 13.2 %collective-permute-done.4.p1_ref = bf16[512,512]{1,0:T(8,128)(2,1)S(1)} collective-permute-done((bf16[512,512]{1,0:T(8,128)(2,1)}, bf16[512,512]{1,0:T(8,128)(2,1)S(1)}, u32[]{:S(2)}, u32[]{:S(2)}) %collective-permute-start.4) | collective-permute-done | bytes 524320 | tf_op jit(solution)/shard_map/ppermute | solution.py:307
  84.6 2.5 %copy.25 = bf16[512,2048]{0,1:T(8,128)(2,1)} copy(bf16[512,2048]{1,0:T(8,128)(2,1)S(1)} %copy-done) | data formatting | bytes 4194304 | tf_op args[3]
  87.8 1.2 compare_select_fusion.5.sc_ref
  89.0 5.5 %kv.4 = (bf16[1024,512]{1,0:T(8,128)(2,1)}, bf16[512,1024]{1,0:T(8,128)(2,1)}, bf16[512,256]{1,0:T(8,128)(2,1)}, bf16[512,256]{1,0:T(8,128)(2,1)}, bf16[256,512]{1,0:T(8,128)(2,1)}) custom-call(s32[8]{0:T(128)} %compare_select_fusion.5.sc_ref, bf16[512,512]{1,0:T(8,128)(2,1)} %fusion.3.p1_ref, bf16[512,512]{1,0:T(8,128)(2,1)} %collective-permute-done.p2_ref, ...), custom_call_target="tpu_custom_call" | custom-call | tf_op jit(solution)/shard_map/kv/pallas_call | solution.py:135
  94.4 5.4 %kv.6 = (bf16[1024,512]{1,0:T(8,128)(2,1)}, bf16[512,1024]{1,0:T(8,128)(2,1)}, bf16[512,256]{1,0:T(8,128)(2,1)}, bf16[512,256]{1,0:T(8,128)(2,1)}, bf16[256,512]{1,0:T(8,128)(2,1)}) custom-call(s32[8]{0:T(128)} %compare_select_fusion.5.sc_ref, bf16[512,512]{1,0:T(8,128)(2,1)} %fusion.2.p1_ref, bf16[512,512]{1,0:T(8,128)(2,1)} %collective-permute-done.3.p2_ref, ...), custom_call_target="tpu_custom_call" | custom-call | tf_op jit(solution)/shard_map/kv/pallas_call | solution.py:135
  99.9 5.5 %kv.5 = (bf16[1024,512]{1,0:T(8,128)(2,1)}, bf16[512,1024]{1,0:T(8,128)(2,1)}, bf16[512,256]{1,0:T(8,128)(2,1)}, bf16[512,256]{1,0:T(8,128)(2,1)}, bf16[256,512]{1,0:T(8,128)(2,1)}) custom-call(s32[8]{0:T(128)} %compare_select_fusion.5.sc_ref, bf16[512,512]{1,0:T(8,128)(2,1)} %collective-permute-done.1.p1_ref, ...), custom_call_target="tpu_custom_call" | custom-call | tf_op jit(solution)/shard_map/kv/pallas_call | solution.py:135
  105.4 12.0 %attend0.1.refs_15_ = bf16[1024,512]{1,0:T(8,128)(2,1)} custom-call(s32[8]{0:T(128)} %compare_select_fusion.5.sc_ref, bf16[1024,512]{1,0:T(8,128)(2,1)} %get-tuple-element.25.refs_0_, bf16[1024,512]{1,0:T(8,128)(2,1)} %get-tuple-element.26.refs_1_, bf16[512,1024]{1,0:T(8,128)(2,1)} %get-tuple-element.29.refs_2_.refs_4_, ...), custom_call_target="tpu_custom_call" | custom-call | tf_op jit(solution)/shard_map/attend0/pallas_call | solution.py:235
  117.4 0.8 copy-done.2
  118.2 5.5 %kv.7 = (bf16[1024,512]{1,0:T(8,128)(2,1)}, bf16[512,1024]{1,0:T(8,128)(2,1)}, bf16[512,256]{1,0:T(8,128)(2,1)}, bf16[512,256]{1,0:T(8,128)(2,1)}, bf16[256,512]{1,0:T(8,128)(2,1)}) custom-call(s32[8]{0:T(128)} %compare_select_fusion.5.sc_ref, bf16[512,512]{1,0:T(8,128)(2,1)} %copy-done.1, bf16[512,512]{1,0:T(8,128)(2,1)} %copy-done.2, ...), custom_call_target="tpu_custom_call" | custom-call | tf_op jit(solution)/shard_map/kv/pallas_call | solution.py:135
  123.6 19.9 %attend1.1 = bf16[1024,512]{1,0:T(8,128)(2,1)} custom-call(s32[8]{0:T(128)} %compare_select_fusion.5.sc_ref, bf16[1024,512]{1,0:T(8,128)(2,1)} %get-tuple-element.25.refs_0_, bf16[1024,512]{1,0:T(8,128)(2,1)} %get-tuple-element.26.refs_1_, bf16[1024,512]{1,0:T(8,128)(2,1)} %get-tuple-element.27.refs_2_, ...), custom_call_target="tpu_custom_call", output_to_operand_aliasing={{}: (16, {})} | custom-call | tf_op jit(solution)/shard_map/attend1/pallas_call | solution.py:235
  143.5 21.6 %all_to_all.24 = bf16[16,64,512]{2,1,0:T(8,128)(2,1)S(1)} all-to-all(bf16[16,64,512]{2,1,0:T(8,128)(2,1)} %bitcast.43), channel_id=1, replica_groups=mesh['dp'=8,'xh'=2,'xl'=2,'yh'=2,'co'=2] {'xh','xl','yh','co'}, dimensions={0} | all-to-all | bytes 2097152 | tf_op jit(solution)/shard_map/all_to_all | solution.py:316
  165.1 1.1 copy.28
  (46 shorter events, 5.8 us)
Async XLA Ops:
  1.4 19.8 %all-to-all-start = ((s32[32,1,256]{2,1,0:T(1,128)}), s32[32,1,256]{2,1,0:T(1,128)S(1)}, u32[]{:S(2)}, u32[]{:S(2)}) async-start(s32[32,1,256]{2,1,0:T(1,128)} %all_to_all.15), calls=%async_computation | async-start | bytes 65536 | tf_op jit(solution)/shard_map/all_to_all | solution.py:272
  22.7 0.7 copy-start.4
  31.5 19.2 %all-to-all-start.1 = ((bf16[8,128,512]{2,1,0:T(8,128)(2,1)}), bf16[8,128,512]{2,1,0:T(8,128)(2,1)S(1)}, u32[]{:S(2)}, u32[]{:S(2)}) async-start(bf16[8,128,512]{2,1,0:T(8,128)(2,1)} %bitcast.44), calls=%async_computation.1 | async-start | bytes 2097152 | tf_op jit(solution)/shard_map/all_to_all | solution.py:294
  38.1 0.8 copy-start.3
  50.7 18.6 %all-to-all-start.2 = ((bf16[8,128,512]{2,1,0:T(8,128)(2,1)}), bf16[8,128,512]{2,1,0:T(8,128)(2,1)S(1)}, u32[]{:S(2)}, u32[]{:S(2)}) async-start(bf16[8,128,512]{2,1,0:T(8,128)(2,1)} %bitcast.45), calls=%async_computation.2 | async-start | bytes 2097152 | tf_op jit(solution)/shard_map/all_to_all | solution.py:294
  57.0 27.6 %copy-start = (bf16[512,2048]{1,0:T(8,128)(2,1)S(1)}, bf16[512,2048]{1,0:T(8,128)(2,1)}, u32[]{:S(2)}) copy-start(bf16[512,2048]{1,0:T(8,128)(2,1)} %wk_ref.7) | copy-start | bytes 6291460
  57.0 14.4 %collective-permute-start.1 = (bf16[512,512]{1,0:T(8,128)(2,1)}, bf16[512,512]{1,0:T(8,128)(2,1)}, u32[]{:S(2)}, u32[]{:S(2)}) collective-permute-start(bf16[512,512]{1,0:T(8,128)(2,1)} %fusion.3.p1_ref), channel_id=1, source_target_pairs={{0,4},{4,0},{1,5},{5,1},{2,6},{6,2},{3,7},{7,3},{8,12},{12,8},{9,1... | collective-permute-start | bytes 1572872 | tf_op jit(solution)/shard_map/ppermute | solution.py:307
  70.9 13.8 %collective-permute-start.4 = (bf16[512,512]{1,0:T(8,128)(2,1)}, bf16[512,512]{1,0:T(8,128)(2,1)S(1)}, u32[]{:S(2)}, u32[]{:S(2)}) collective-permute-start(bf16[512,512]{1,0:T(8,128)(2,1)} %fusion.2.p1_ref), channel_id=1, source_target_pairs={{0,4},{4,0},{1,5},{5,1},{2,6},{6,2},{3,7},{7,3},{8,12},{12,8},{9,1... | collective-permute-start | bytes 1572872 | tf_op jit(solution)/shard_map/ppermute | solution.py:307
  70.9 18.1 %collective-permute-start = (bf16[512,512]{1,0:T(8,128)(2,1)}, bf16[512,512]{1,0:T(8,128)(2,1)}, u32[]{:S(2)}, u32[]{:S(2)}) collective-permute-start(bf16[512,512]{1,0:T(8,128)(2,1)} %fusion.3.p1_ref), channel_id=1, source_target_pairs={{0,1},{1,0},{2,3},{3,2},{4,5},{5,4},{6,7},{7,6},{8,9},{9,8},{10,11... | collective-permute-start | bytes 1572872 | tf_op jit(solution)/shard_map/ppermute | solution.py:308
  70.9 23.6 %collective-permute-start.3 = (bf16[512,512]{1,0:T(8,128)(2,1)}, bf16[512,512]{1,0:T(8,128)(2,1)}, u32[]{:S(2)}, u32[]{:S(2)}) collective-permute-start(bf16[512,512]{1,0:T(8,128)(2,1)} %fusion.2.p1_ref), channel_id=1, source_target_pairs={{0,1},{1,0},{2,3},{3,2},{4,5},{5,4},{6,7},{7,6},{8,9},{9,8},{10,11... | collective-permute-start | bytes 1572872 | tf_op jit(solution)/shard_map/ppermute | solution.py:308
  71.4 28.5 %collective-permute-start.2 = (bf16[512,512]{1,0:T(8,128)(2,1)}, bf16[512,512]{1,0:T(8,128)(2,1)}, u32[]{:S(2)}, u32[]{:S(2)}) collective-permute-start(bf16[512,512]{1,0:T(8,128)(2,1)} %collective-permute-done.1.p1_ref), channel_id=1, source_target_pairs={{0,1},{1,0},{2,3},{3,2},{4,5},{5,4},{6,7},{7,6},{8,9},{9,8},{10,11... | collective-permute-start | bytes 1572872 | tf_op jit(solution)/shard_map/ppermute | solution.py:309
  84.6 2.5 %copy-start.1 = (bf16[512,512]{1,0:T(8,128)(2,1)}, bf16[512,512]{1,0:T(8,128)(2,1)S(1)}, u32[]{:S(2)}) copy-start(bf16[512,512]{1,0:T(8,128)(2,1)S(1)} %collective-permute-done.4.p1_ref) | copy-start | bytes 1572868
  84.6 32.7 %collective-permute-start.5 = (bf16[512,512]{1,0:T(8,128)(2,1)S(1)}, bf16[512,512]{1,0:T(8,128)(2,1)S(1)}, u32[]{:S(2)}, u32[]{:S(2)}) collective-permute-start(bf16[512,512]{1,0:T(8,128)(2,1)S(1)} %collective-permute-done.4.p1_ref), channel_id=1, source_target_pairs={{0,1},{1,0},{2,3},{3,2},{4,5},{5,4},{6,7},{7,6},{8,9},{9,8},{10,11... | collective-permute-start | bytes 1572872 | tf_op jit(solution)/shard_map/ppermute | solution.py:309
  84.6 2.5 %copy-start.5 = (s32[4]{0:T(128)S(1)}, s32[4]{0:T(128)}, u32[]{:S(2)}) copy-start(s32[4]{0:T(128)} %param.6) | copy-start | bytes 52
  117.4 0.8 copy-start.2

commit v2 on v1

--- a/solution.py
+++ b/solution.py
@@ -16,6 +16,13 @@
 VM = pl.BlockSpec(memory_space=pltpu.VMEM)
 SM = pl.BlockSpec(memory_space=pltpu.SMEM)
 ANY = pl.BlockSpec(memory_space=pl.ANY)
+
+
+def cost(us):
+    return pl.CostEstimate(flops=int(us * FLOPS_PER_US), bytes_accessed=0, transcendentals=0)
+
+
+FLOPS_PER_US = 4_000_000
 PARAMS = pltpu.CompilerParams(vmem_limit_bytes=56 * 1024 * 1024)
 BUNCH = 32
 
@@ -24,8 +31,8 @@
     return h + h * jnp.tanh(h)
 
 
-def nt(a, b):
-    return lax.dot_general(a, b, (((1,), (1,)), ((), ())), preferred_element_type=F32)
+def tn(a, b):
+    return lax.dot_general(a, b, (((0,), (1,)), ((), ())), preferred_element_type=F32)
 
 
 def nn(a, b):
@@ -90,6 +97,7 @@
             pltpu.SemaphoreType.DMA((owners * CAP // BUNCH,)),
         ],
         compiler_params=PARAMS,
+        cost_estimate=cost(8),
         name="gather",
     )(rows, count, low, table.reshape(-1, 8, D))
 
@@ -109,7 +117,7 @@
         edge = co if s == 0 else 1 - co
         n = n_scr[s]
         k = twice_silu(0.5 * nn(n, wk_ref[...])).astype(BF)
-        v = twice_silu(0.5 * nt(wv_ref[...], n))
+        v = twice_silu(0.5 * tn(wv_ref[...], n))
         for j in range(2):
             at = pl.multiple_of((edge + 2 * j) * BLK, BLK)
             k_ref[pl.ds(at, BLK), :] = k[j * BLK : (j + 1) * BLK]
@@ -119,13 +127,13 @@
             nq_scr[pl.ds(to, PART), :] = n_scr[s, pl.ds(j * BLK + qo, PART), :]
             xq_ref[pl.ds(to, PART), :] = ref[pl.ds(j * BLK + qo, PART), :]
     nq = nq_scr[...]
-    q_ref[...] = twice_silu(0.5 * nt(wq_ref[...], nq)).astype(BF) * BF(1 / 16)
-    g_ref[...] = twice_silu(0.5 * nt(wg_ref[...], nq)).astype(BF)
-
-
-def kv_call(first, group_at, sc, p1, p2, w_in, w_turned):
+    q_ref[...] = twice_silu(0.5 * tn(wq_ref[...], nq)).astype(BF) * BF(1 / 16)
+    g_ref[...] = twice_silu(0.5 * tn(wg_ref[...], nq)).astype(BF)
+
+
+def kv_call(first, group_at, sc, p1, p2, w_in):
     def part(i):
-        return pl.BlockSpec((D, D), lambda _: (i, 0))
+        return pl.BlockSpec((D, D), lambda _: (0, i))
 
     def whole(shape):
         return pl.BlockSpec(shape, lambda _: (0,) * len(shape))
@@ -136,12 +144,13 @@
         functools.partial(kv_kernel, first, group_at),
         grid=(1,),
         out_shape=[jax.ShapeDtypeStruct(s, BF) for s in shapes],
-        in_specs=[SM, whole((D, D)), whole((D, D)), pl.BlockSpec((D, D), lambda _: (0, 3)), part(1), part(2), part(0)],
+        in_specs=[SM, whole((D, D)), whole((D, D)), part(3), part(1), part(2), part(0)],
         out_specs=[whole(s) for s in shapes],
         scratch_shapes=[pltpu.VMEM((2, D, D), BF), pltpu.VMEM((quarter, D), BF)],
         compiler_params=PARAMS,
+        cost_estimate=cost(5.5),
         name="kv",
-    )(sc, p1, p2, w_in, w_turned, w_turned, w_turned)
+    )(sc, p1, p2, w_in, w_in, w_in, w_in)
 
 
 def attn_kernel(chunk, sc_ref, *refs):
@@ -250,7 +259,7 @@
             pltpu.SemaphoreType.DMA,
         ],
         compiler_params=PARAMS,
-        name="attend" + str(chunk),
+        cost_estimate=cost(12 + 8 * chunk),
     )(*inputs)
 
 
@@ -261,12 +270,11 @@
 FLIP = [(0, 1), (1, 0)]
 
 
-def per_device(item_ids, lengths, table, w_in, w_out):
+def layer(item_ids, lengths, table, w_in, w_out):
     owned = table.shape[0]
     me = lax.axis_index("dp")
     xh, xl, yh, co = (lax.axis_index(a) for a in CTX)
     owners = lax.axis_size("dp")
-    w_turned = w_in.T
 
     send = jnp.broadcast_to(item_ids[None], (owners, 4, BLK)).reshape(owners * 4, BLK)
     wanted = lax.all_to_all(send, ("dp", "xh", "yh"), 0, 0, tiled=True).reshape(owners, 4, BLK)
@@ -303,13 +311,14 @@
 
     ks, vs, out = [], [], None
     for c in range(2):
-        own = place(c, fetch(c))
+        got = fetch(c)
+        own = place(c, got)
         far = lax.ppermute(own, "xl", FLIP)
         near = lax.ppermute(own, "co", FLIP)
         diag = lax.ppermute(far, "co", FLIP)
         first = 2 * GRP * c
-        k0, v0, q0, g0, x0 = kv_call(first, 3, sc, own, near, w_in, w_turned)
-        k1, v1, q1, g1, x1 = kv_call(first, 4, sc, far, diag, w_in, w_turned)
+        k0, v0, q0, g0, x0 = kv_call(first, 3, sc, own, near, w_in)
+        k1, v1, q1, g1, x1 = kv_call(first, 4, sc, far, diag, w_in)
         ks += [k0, k1]
         vs += [v0, v1]
         out = attn_call(c, sc, ks, vs, (q0, q1), (g0, g1), (x0, x1), w_out, out)
@@ -321,7 +330,7 @@
 def solution(mesh):
     finer = Mesh(mesh.devices.reshape(mesh.shape["dp"], 2, 2, 2, 2), ("dp",) + CTX)
     return jax.shard_map(
-        per_device,
+        layer,
         mesh=finer,
         in_specs=(P("dp", CTX), P("dp"), P("dp", None), P(), P()),
         out_specs=P("dp", CTX, None),

time: 167 us -> 165 us (0.988)
  waiting for transfers between devices: 34.6 us -> 31.7 us
  starting transfers between devices: 22.9 us -> 25.3 us
  local copies, waits for them, and re-layouts: 6 us -> 4.3 us
    all_to_all x2, starting transfers between devices: 10.2 us -> 12.3 us  [fetch(): lax.all_to_all(picked, 'dp', 0, 0, tiled=True).reshape(owners * CAP, D)]
    unnamed x18 -> x23, local copies, waits for them, and re-layouts: 3.36 us -> 1.67 us
  transfers between devices with their start and end apart: 9 -> 9, of which waited for: 4 -> 3; matrix products, arithmetic and copies ran while one was open for 6% -> 3% of each run, Pallas kernels for 23% -> 25%
where the time goes in v2:
time: 165 us; the launch traced here: 164 us
  Pallas kernels  73.4 us (44%)
  waiting for transfers between devices  31.7 us (19%)
  starting transfers between devices  25.3 us (15%)
  blocking collectives  21.6 us (13%)
  other arithmetic  4.74 us (3%)
  local copies, waits for them, and re-layouts  4.3 us (3%)
  matrix products  2.55 us (2%)
    pallas_call x2, Pallas kernels, attn_call(): pl.pallas_call(functools.partial(attn_kernel, chunk), out_shape=jax.Shape...  31.8 us
    pallas_call x4, Pallas kernels, kv_call(): pl.pallas_call(functools.partial(kv_kernel, first, group_at), grid=(1,),...  22.5 us
    all_to_all x1, blocking collectives, layer(): back = lax.all_to_all(out.reshape(16, PART, D), CTX, 0, 0, tiled=True)  21.6 us
    pallas_call x2, Pallas kernels, gather_call(): pl.pallas_call(functools.partial(gather_kernel, owners), out_shape=jax.Sh...  19 us
    all_to_all x2, starting transfers between devices, fetch(): lax.all_to_all(picked, 'dp', 0, 0, tiled=True).reshape(owners * CAP, D)  12.3 us
    ppermute x2, waiting for transfers between devices, layer(): far = lax.ppermute(own, 'xl', FLIP)  11.7 us
    all_to_all x2, waiting for transfers between devices, fetch(): lax.all_to_all(picked, 'dp', 0, 0, tiled=True).reshape(owners * CAP, D)  11.3 us
    all_to_all x1, starting transfers between devices, layer(): lax.all_to_all(send, ('dp', 'xh', 'yh'), 0, 0, tiled=True)  11 us
  transfers between devices with their start and end apart: 9, of which 3 were waited for; matrix products, arithmetic and copies ran while one was open for 3% of the time, Pallas kernels for 25%

profile of v2, /device:TPU:8, one launch (start us, length us, event | category | flops | bytes accessed | tf_op | source)
XLA Modules:
  0.0 163.9 jit_solution(17887178690795019428)
XLA Ops:
  0.0 0.7 broadcast_in_dim.74
  1.4 11.0 %all-to-all-start = ((s32[32,1,256]{2,1,0:T(1,128)}), s32[32,1,256]{2,1,0:T(1,128)S(1)}, u32[]{:S(2)}, u32[]{:S(2)}) async-start(s32[32,1,256]{2,1,0:T(1,128)} %all_to_all.15), calls=%async_computation | async-start | bytes 65536 | tf_op jit(solution)/shard_map/all_to_all | solution.py:280
  12.4 8.7 %all-to-all-done = s32[32,1,256]{2,1,0:T(1,128)S(1)} async-done(((s32[32,1,256]{2,1,0:T(1,128)}), s32[32,1,256]{2,1,0:T(1,128)S(1)}, u32[]{:S(2)}, u32[]{:S(2)}) %all-to-all-start) | async-done | bytes 32800 | tf_op jit(solution)/shard_map/all_to_all | solution.py:280
  21.2 1.0 fusion.34
  23.7 7.8 %gather.2 = bf16[1024,512]{1,0:T(8,128)(2,1)} custom-call(s32[8,128]{1,0:T(8,128)} %copy-done.7, s32[8]{0:T(128)} %get-tuple-element.46.count_ref, s32[128,8]{1,0:T(8,128)} %and_bitcast_fusion.1.low_ref, bf16[2048,8,512]{2,1,0:T(8,128)(2,1)} %bitcast.28), custom_call_target="tpu_custom_call" | custom-call | flops 32000000 | tf_op jit(solution)/shard_map/gather/pallas_call | solution.py:90
  31.5 8.7 %all-to-all-start.1 = ((bf16[8,128,512]{2,1,0:T(8,128)(2,1)}), bf16[8,128,512]{2,1,0:T(8,128)(2,1)S(1)}, u32[]{:S(2)}, u32[]{:S(2)}) async-start(bf16[8,128,512]{2,1,0:T(8,128)(2,1)} %bitcast.32), calls=%async_computation.1 | async-start | bytes 2097152 | tf_op jit(solution)/shard_map/all_to_all | solution.py:302
  41.3 11.2 %gather.3 = bf16[1024,512]{1,0:T(8,128)(2,1)} custom-call(s32[8,128]{1,0:T(8,128)} %copy-done.6, s32[8]{0:T(128)} %get-tuple-element.45.count_ref, s32[128,8]{1,0:T(8,128)} %and_bitcast_fusion.low_ref, bf16[2048,8,512]{2,1,0:T(8,128)(2,1)} %bitcast.29), custom_call_target="tpu_custom_call" | custom-call | flops 32000000 | tf_op jit(solution)/shard_map/gather/pallas_call | solution.py:90
  52.6 3.5 %all-to-all-start.2 = ((bf16[8,128,512]{2,1,0:T(8,128)(2,1)}), bf16[8,128,512]{2,1,0:T(8,128)(2,1)S(1)}, u32[]{:S(2)}, u32[]{:S(2)}) async-start(bf16[8,128,512]{2,1,0:T(8,128)(2,1)} %bitcast.31), calls=%async_computation.2 | async-start | bytes 2097152 | tf_op jit(solution)/shard_map/all_to_all | solution.py:302
  56.7 0.8 fusion.3.p1_ref
  57.6 11.3 %all-to-all-done.2 = bf16[8,128,512]{2,1,0:T(8,128)(2,1)S(1)} async-done(((bf16[8,128,512]{2,1,0:T(8,128)(2,1)}), bf16[8,128,512]{2,1,0:T(8,128)(2,1)S(1)}, u32[]{:S(2)}, u32[]{:S(2)}) %all-to-all-start.2) | async-done | bytes 1048608 | tf_op jit(solution)/shard_map/all_to_all | solution.py:302
  68.9 0.8 fusion.2.p1_ref
  69.7 1.4 collective-permute-start.4
  71.6 11.7 %collective-permute-done.4.p1_ref = bf16[512,512]{1,0:T(8,128)(2,1)S(1)} collective-permute-done((bf16[512,512]{1,0:T(8,128)(2,1)S(1)}, bf16[512,512]{1,0:T(8,128)(2,1)S(1)}, u32[]{:S(2)}, u32[]{:S(2)}) %collective-permute-start.4) | collective-permute-done | bytes 524320 | tf_op jit(solution)/shard_map/ppermute | solution.py:316
  84.0 1.2 compare_select_fusion.5.sc_ref
  85.2 5.6 %kv.4 = (bf16[1024,512]{1,0:T(8,128)(2,1)}, bf16[512,1024]{1,0:T(8,128)(2,1)}, bf16[512,256]{1,0:T(8,128)(2,1)}, bf16[512,256]{1,0:T(8,128)(2,1)}, bf16[256,512]{1,0:T(8,128)(2,1)}) custom-call(s32[8]{0:T(128)} %compare_select_fusion.5.sc_ref, bf16[512,512]{1,0:T(8,128)(2,1)} %copy-done.3, bf16[512,512]{1,0:T(8,128)(2,1)} %collective-permute-done.p2_ref, ...), custom_call_target="tpu_custom_call" | custom-call | flops 22000000 | tf_op jit(solution)/shard_map/kv/pallas_call | solution.py:143
  90.8 5.6 %kv.6 = (bf16[1024,512]{1,0:T(8,128)(2,1)}, bf16[512,1024]{1,0:T(8,128)(2,1)}, bf16[512,256]{1,0:T(8,128)(2,1)}, bf16[512,256]{1,0:T(8,128)(2,1)}, bf16[256,512]{1,0:T(8,128)(2,1)}) custom-call(s32[8]{0:T(128)} %compare_select_fusion.5.sc_ref, bf16[512,512]{1,0:T(8,128)(2,1)} %copy-done.4, bf16[512,512]{1,0:T(8,128)(2,1)} %collective-permute-done.3.p2_ref, ...), custom_call_target="tpu_custom_call" | custom-call | flops 22000000 | tf_op jit(solution)/shard_map/kv/pallas_call | solution.py:143
  96.5 0.8 copy-done.5
  97.2 5.6 %kv.5 = (bf16[1024,512]{1,0:T(8,128)(2,1)}, bf16[512,1024]{1,0:T(8,128)(2,1)}, bf16[512,256]{1,0:T(8,128)(2,1)}, bf16[512,256]{1,0:T(8,128)(2,1)}, bf16[256,512]{1,0:T(8,128)(2,1)}) custom-call(s32[8]{0:T(128)} %compare_select_fusion.5.sc_ref, bf16[512,512]{1,0:T(8,128)(2,1)} %copy-done.1, bf16[512,512]{1,0:T(8,128)(2,1)} %copy-done.5, ...), custom_call_target="tpu_custom_call" | custom-call | flops 22000000 | tf_op jit(solution)/shard_map/kv/pallas_call | solution.py:143
  102.9 12.1 %shard_map.55.refs_15_ = bf16[1024,512]{1,0:T(8,128)(2,1)} custom-call(s32[8]{0:T(128)} %compare_select_fusion.5.sc_ref, bf16[1024,512]{1,0:T(8,128)(2,1)} %get-tuple-element.25.refs_0_, bf16[1024,512]{1,0:T(8,128)(2,1)} %get-tuple-element.26.refs_1_, bf16[512,1024]{1,0:T(8,128)(2,1)} %get-tuple-element.29.refs_2_.refs_4_, ...), custom_call_target="tpu_custom_call" | custom-call | flops 48000000 | tf_op jit(solution)/shard_map/pallas_call | solution.py:244
  115.0 0.8 copy-done.2
  115.8 5.7 %kv.7 = (bf16[1024,512]{1,0:T(8,128)(2,1)}, bf16[512,1024]{1,0:T(8,128)(2,1)}, bf16[512,256]{1,0:T(8,128)(2,1)}, bf16[512,256]{1,0:T(8,128)(2,1)}, bf16[256,512]{1,0:T(8,128)(2,1)}) custom-call(s32[8]{0:T(128)} %compare_select_fusion.5.sc_ref, bf16[512,512]{1,0:T(8,128)(2,1)} %copy-done, bf16[512,512]{1,0:T(8,128)(2,1)} %copy-done.2, ...), custom_call_target="tpu_custom_call" | custom-call | flops 22000000 | tf_op jit(solution)/shard_map/kv/pallas_call | solution.py:143
  121.5 19.7 %shard_map.56 = bf16[1024,512]{1,0:T(8,128)(2,1)} custom-call(s32[8]{0:T(128)} %compare_select_fusion.5.sc_ref, bf16[1024,512]{1,0:T(8,128)(2,1)} %get-tuple-element.25.refs_0_, bf16[1024,512]{1,0:T(8,128)(2,1)} %get-tuple-element.26.refs_1_, bf16[1024,512]{1,0:T(8,128)(2,1)} %get-tuple-element.27.refs_2_, ...), custom_call_target="tpu_custom_call", output_to_operand_aliasing={{}: (16, {})} | custom-call | flops 80000000 | tf_op jit(solution)/shard_map/pallas_call | solution.py:244
  141.2 21.6 %all_to_all.24 = bf16[16,64,512]{2,1,0:T(8,128)(2,1)S(1)} all-to-all(bf16[16,64,512]{2,1,0:T(8,128)(2,1)} %bitcast.30), channel_id=1, replica_groups=mesh['dp'=8,'xh'=2,'xl'=2,'yh'=2,'co'=2] {'xh','xl','yh','co'}, dimensions={0} | all-to-all | bytes 2097152 | tf_op jit(solution)/shard_map/all_to_all | solution.py:325
  162.8 1.1 copy.23
  (51 shorter events, 5.3 us)
Async XLA Ops:
  1.4 19.8 %all-to-all-start = ((s32[32,1,256]{2,1,0:T(1,128)}), s32[32,1,256]{2,1,0:T(1,128)S(1)}, u32[]{:S(2)}, u32[]{:S(2)}) async-start(s32[32,1,256]{2,1,0:T(1,128)} %all_to_all.15), calls=%async_computation | async-start | bytes 65536 | tf_op jit(solution)/shard_map/all_to_all | solution.py:280
  23.0 0.7 copy-start.7
  31.5 21.0 %all-to-all-start.1 = ((bf16[8,128,512]{2,1,0:T(8,128)(2,1)}), bf16[8,128,512]{2,1,0:T(8,128)(2,1)S(1)}, u32[]{:S(2)}, u32[]{:S(2)}) async-start(bf16[8,128,512]{2,1,0:T(8,128)(2,1)} %bitcast.32), calls=%async_computation.1 | async-start | bytes 2097152 | tf_op jit(solution)/shard_map/all_to_all | solution.py:302
  40.6 0.7 copy-start.6
  52.6 16.3 %all-to-all-start.2 = ((bf16[8,128,512]{2,1,0:T(8,128)(2,1)}), bf16[8,128,512]{2,1,0:T(8,128)(2,1)S(1)}, u32[]{:S(2)}, u32[]{:S(2)}) async-start(bf16[8,128,512]{2,1,0:T(8,128)(2,1)} %bitcast.31), calls=%async_computation.2 | async-start | bytes 2097152 | tf_op jit(solution)/shard_map/all_to_all | solution.py:302
  57.5 27.7 %copy-start.3 = (bf16[512,512]{1,0:T(8,128)(2,1)}, bf16[512,512]{1,0:T(8,128)(2,1)S(1)}, u32[]{:S(2)}) copy-start(bf16[512,512]{1,0:T(8,128)(2,1)S(1)} %fusion.3.p1_ref) | copy-start | bytes 1572868
  57.5 25.8 %copy-start.8 = (s32[4]{0:T(128)S(1)}, s32[4]{0:T(128)}, u32[]{:S(2)}) copy-start(s32[4]{0:T(128)} %param.6) | copy-start | bytes 52
  57.5 14.1 %collective-permute-start.1 = (bf16[512,512]{1,0:T(8,128)(2,1)S(1)}, bf16[512,512]{1,0:T(8,128)(2,1)S(1)}, u32[]{:S(2)}, u32[]{:S(2)}) collective-permute-start(bf16[512,512]{1,0:T(8,128)(2,1)S(1)} %fusion.3.p1_ref), channel_id=1, source_target_pairs={{0,4},{4,0},{1,5},{5,1},{2,6},{6,2},{3,7},{7,3},{8,12},{12,8},{9,1... | collective-permute-start | bytes 1572872 | tf_op jit(solution)/shard_map/ppermute | solution.py:316
  69.7 21.1 %copy-start.4 = (bf16[512,512]{1,0:T(8,128)(2,1)}, bf16[512,512]{1,0:T(8,128)(2,1)S(1)}, u32[]{:S(2)}) copy-start(bf16[512,512]{1,0:T(8,128)(2,1)S(1)} %fusion.2.p1_ref) | copy-start | bytes 1572868
  69.7 13.6 %collective-permute-start.4 = (bf16[512,512]{1,0:T(8,128)(2,1)S(1)}, bf16[512,512]{1,0:T(8,128)(2,1)S(1)}, u32[]{:S(2)}, u32[]{:S(2)}) collective-permute-start(bf16[512,512]{1,0:T(8,128)(2,1)S(1)} %fusion.2.p1_ref), channel_id=1, source_target_pairs={{0,4},{4,0},{1,5},{5,1},{2,6},{6,2},{3,7},{7,3},{8,12},{12,8},{9,1... | collective-permute-start | bytes 1572872 | tf_op jit(solution)/shard_map/ppermute | solution.py:316
  71.0 14.1 %collective-permute-start = (bf16[512,512]{1,0:T(8,128)(2,1)S(1)}, bf16[512,512]{1,0:T(8,128)(2,1)}, u32[]{:S(2)}, u32[]{:S(2)}) collective-permute-start(bf16[512,512]{1,0:T(8,128)(2,1)S(1)} %fusion.3.p1_ref), channel_id=1, source_target_pairs={{0,1},{1,0},{2,3},{3,2},{4,5},{5,4},{6,7},{7,6},{8,9},{9,8},{10,11... | collective-permute-start | bytes 1572872 | tf_op jit(solution)/shard_map/ppermute | solution.py:317
  71.1 19.8 %collective-permute-start.3 = (bf16[512,512]{1,0:T(8,128)(2,1)S(1)}, bf16[512,512]{1,0:T(8,128)(2,1)}, u32[]{:S(2)}, u32[]{:S(2)}) collective-permute-start(bf16[512,512]{1,0:T(8,128)(2,1)S(1)} %fusion.2.p1_ref), channel_id=1, source_target_pairs={{0,1},{1,0},{2,3},{3,2},{4,5},{5,4},{6,7},{7,6},{8,9},{9,8},{10,11... | collective-permute-start | bytes 1572872 | tf_op jit(solution)/shard_map/ppermute | solution.py:317
  71.6 19.2 %copy-start.1 = (bf16[512,512]{1,0:T(8,128)(2,1)}, bf16[512,512]{1,0:T(8,128)(2,1)S(1)}, u32[]{:S(2)}) copy-start(bf16[512,512]{1,0:T(8,128)(2,1)S(1)} %collective-permute-done.1.p1_ref) | copy-start | bytes 1572868
  71.6 24.9 %collective-permute-start.2 = (bf16[512,512]{1,0:T(8,128)(2,1)S(1)}, bf16[512,512]{1,0:T(8,128)(2,1)S(1)}, u32[]{:S(2)}, u32[]{:S(2)}) collective-permute-start(bf16[512,512]{1,0:T(8,128)(2,1)S(1)} %collective-permute-done.1.p1_ref), channel_id=1, source_target_pairs={{0,1},{1,0},{2,3},{3,2},{4,5},{5,4},{6,7},{7,6},{8,9},{9,8},{10,11... | collective-permute-start | bytes 1572872 | tf_op jit(solution)/shard_map/ppermute | solution.py:318
  83.3 7.5 %copy-start = (bf16[512,512]{1,0:T(8,128)(2,1)}, bf16[512,512]{1,0:T(8,128)(2,1)S(1)}, u32[]{:S(2)}) copy-start(bf16[512,512]{1,0:T(8,128)(2,1)S(1)} %collective-permute-done.4.p1_ref) | copy-start | bytes 1572868
  83.3 31.7 %collective-permute-start.5 = (bf16[512,512]{1,0:T(8,128)(2,1)S(1)}, bf16[512,512]{1,0:T(8,128)(2,1)S(1)}, u32[]{:S(2)}, u32[]{:S(2)}) collective-permute-start(bf16[512,512]{1,0:T(8,128)(2,1)S(1)} %collective-permute-done.4.p1_ref), channel_id=1, source_target_pairs={{0,1},{1,0},{2,3},{3,2},{4,5},{5,4},{6,7},{7,6},{8,9},{9,8},{10,11... | collective-permute-start | bytes 1572872 | tf_op jit(solution)/shard_map/ppermute | solution.py:318
  96.5 0.8 copy-start.5
  115.0 0.8 copy-start.2

commit v3 on v2

v3 whole, which is shorter than its diff:
```python
import functools

import jax
import jax.numpy as jnp
from jax import lax
from jax.experimental import pallas as pl
from jax.experimental.pallas import tpu as pltpu

BF = jnp.bfloat16
F32 = jnp.float32
BLK = 256
D = 512
GRP = 1024
PART = 64
CAP = 128
ROW8 = 8
BUNCH = 32
VM = pl.BlockSpec(memory_space=pltpu.VMEM)
SM = pl.BlockSpec(memory_space=pltpu.SMEM)
ANY = pl.BlockSpec(memory_space=pl.ANY)
PARAMS = pltpu.CompilerParams(vmem_limit_bytes=16 * 1024 * 1024)


def cost(us):
    return pl.CostEstimate(flops=int(us * 4_000_000), bytes_accessed=0, transcendentals=0)


def in_vmem(x):
    return pltpu.with_memory_space_constraint(x, pltpu.VMEM)


def twice_silu(h):
    return h + h * jnp.tanh(h)


def tn(a, b):
    return lax.dot_general(a, b, (((0,), (1,)), ((), ())), preferred_element_type=F32)


def nn(a, b):
    return jnp.dot(a, b, preferred_element_type=F32)


def gather_kernel(owners, rows_ref, count_ref, ids_ref, table_ref, out_ref, buf, sems):
    def eights(o):
        return (count_ref[o] + ROW8 - 1) // ROW8

    for o in range(owners):

        def start(j, _, o=o):
            for i in range(ROW8):
                s = j * ROW8 + i
                pltpu.make_async_copy(
                    table_ref.at[lax.shift_right_logical(rows_ref[o, s], 3)], buf.at[o * CAP + s], sems.at[o]
                ).start()
            return 0

        def clear(j, _, o=o):
            buf[pl.ds(o * CAP + j * ROW8, ROW8)] = jnp.zeros((ROW8, 8, D), BF)
            return 0

        lax.fori_loop(0, eights(o), start, 0)
        full = BUNCH // ROW8
        lax.fori_loop(eights(o), (eights(o) + full - 1) // full * full, clear, 0)
    low = (ids_ref[...] & 7).astype(F32).T
    width = BUNCH * 8
    lane = lax.broadcasted_iota(jnp.int32, (BUNCH, width), 1).astype(F32)
    slot = lax.broadcasted_iota(jnp.int32, (BUNCH, 1), 0)
    for o in range(owners):
        eight = buf.at[pl.ds(o * CAP, ROW8)]

        def wait(j, _, o=o, eight=eight):
            pltpu.make_async_copy(eight, eight, sems.at[o]).wait()
            return 0

        lax.fori_loop(0, eights(o), wait, 0)
        for b in range(CAP // BUNCH):
            dst = slice(o * CAP + b * BUNCH, o * CAP + (b + 1) * BUNCH)
            want = (8 * slot).astype(F32) + low[b * BUNCH : (b + 1) * BUNCH, o : o + 1]
            pick = (lane == want).astype(F32).astype(BF)
            got = nn(pick, buf[dst].reshape(width, D))
            out_ref[dst, :] = jnp.where(slot + b * BUNCH < count_ref[o], got, 0.0).astype(BF)


def gather_call(rows, count, groups):
    owners = rows.shape[0]
    return pl.pallas_call(
        functools.partial(gather_kernel, owners),
        out_shape=jax.ShapeDtypeStruct((owners * CAP, D), BF),
        in_specs=[SM, SM, VM, pl.BlockSpec(memory_space=pltpu.HBM)],
        out_specs=VM,
        scratch_shapes=[pltpu.VMEM((owners * CAP, 8, D), BF), pltpu.SemaphoreType.DMA((owners,))],
        compiler_params=pltpu.CompilerParams(vmem_limit_bytes=56 * 1024 * 1024),
        cost_estimate=cost(7),
        name="gather",
    )(rows, count, rows, groups)


def project(first, side, sc_ref, pieces, w_ref, k_ref, v_ref, q_ref, g_ref, x_ref, n_scr, nq_scr):
    co = sc_ref[2]
    base = first + GRP * sc_ref[3 + side]
    qo = pl.multiple_of(sc_ref[1], PART)
    wg, wv, wq, wk = (slice(D * i, D * (i + 1)) for i in range(4))
    for s, ref in enumerate(pieces):
        x = ref[...].astype(F32)
        c = x - jnp.mean(x, axis=1, keepdims=True)
        var = jnp.mean(c * c, axis=1, keepdims=True)
        n_scr[s] = (c * lax.rsqrt(var + 1e-5)).astype(BF)
    for s, ref in enumerate(pieces):
        edge = co if s == 0 else 1 - co
        n = n_scr[s]
        k = twice_silu(0.5 * nn(n, w_ref[:, wk])).astype(BF)
        v = twice_silu(0.5 * tn(w_ref[:, wv], n))
        for j in range(2):
            at = pl.multiple_of((edge + 2 * j) * BLK, BLK)
            k_ref[pl.ds(at, BLK), :] = k[j * BLK : (j + 1) * BLK]
            pos = base + at + lax.broadcasted_iota(jnp.int32, (1, BLK), 1)
            v_ref[:, pl.ds(at, BLK)] = jnp.where(pos < sc_ref[0], v[:, j * BLK : (j + 1) * BLK], 0.0).astype(BF)
            to = pl.multiple_of((edge + 2 * j) * PART, PART)
            nq_scr[pl.ds(to, PART), :] = n_scr[s, pl.ds(j * BLK + qo, PART), :]
            x_ref[pl.ds(to, PART), :] = ref[pl.ds(j * BLK + qo, PART), :]
    nq = nq_scr[...]
    q_ref[...] = twice_silu(0.5 * tn(w_ref[:, wq], nq)).astype(BF) * BF(1 / 16)
    g_ref[...] = twice_silu(0.5 * tn(w_ref[:, wg], nq)).astype(BF)


def attend(sc_ref, tiles, together):
    rid = lax.broadcasted_iota(jnp.int32, (128, 256), 0)
    col = lax.broadcasted_iota(jnp.int32, (1, 512), 1) & 255
    last_key = (col // PART) * BLK + (col % PART) + sc_ref[1]
    key = lax.broadcasted_iota(jnp.int32, (BLK, 512), 0)

    def heads(pp, _):
        steps = [
            (u, t, m, i)
            for u in range(together)
            for t in range(len(tiles))
            for m in range(len(tiles[t][2]))
            for i in range(GRP // BLK)
        ]
        queries = {}
        sums = {}

        def lanes(u):
            return pl.multiple_of((pp * together + u) * 128, 128)

        def scores(step):
            u, t, m, i = step
            if (u, t) not in queries:
                q = tiles[t][0][pl.ds(lanes(u), 128), :]
                zero = jnp.zeros_like(q)
                queries[u, t] = jnp.concatenate([jnp.where(rid < 64, q, zero), jnp.where(rid < 64, zero, q)], axis=1)
            return nn(tiles[t][2][m][0][i * BLK : (i + 1) * BLK, pl.ds(lanes(u), 128)], queries[u, t])

        def weights(step, s):
            _, t, m, i = step
            w = s + s * jnp.tanh(s)
            if tiles[t][2][m][2]:
                w = jnp.where(key + i * BLK <= last_key, w, 0.0)
            return w.astype(BF)

        def add_values(step, w):
            u, t, m, i = step
            o = nn(tiles[t][2][m][1][pl.ds(lanes(u), 128), i * BLK : (i + 1) * BLK], w)
            o = (o[:64, :256], o[64:, 256:])
            old = sums.get((u, t))
            sums[u, t] = o if old is None else (old[0] + o[0], old[1] + o[1])

        s = scores(steps[0])
        before = None
        for n, step in enumerate(steps):
            ahead = scores(steps[n + 1]) if n + 1 < len(steps) else None
            w = weights(step, s)
            if before is not None:
                add_values(steps[n - 1], before)
            before, s = w, ahead
        add_values(steps[-1], before)
        for (u, t), pair in sums.items():
            for hh in range(2):
                tiles[t][1][pl.ds(pl.multiple_of(lanes(u) + 64 * hh, 64), 64), :] = pair[hh]
        return 0

    lax.fori_loop(0, 4 // together, heads, 0)


def near_kernel(chunk, sc_ref, *refs):
    past = refs[: 4 * chunk]
    p1, p2, w_ref, k_ref, v_ref, q_ref, g_ref, x_ref, o_ref, n_scr, nq_scr = refs[4 * chunk :]
    project(2 * GRP * chunk, 0, sc_ref, (p1, p2), w_ref, k_ref, v_ref, q_ref, g_ref, x_ref, n_scr, nq_scr)
    seen = [(past[2 * i], past[2 * i + 1], False) for i in range(2 * chunk)]
    attend(sc_ref, [(q_ref, o_ref, seen + [(k_ref, v_ref, True)])], 2)


def far_kernel(chunk, sc_ref, *refs):
    past = refs[: 4 * chunk]
    p1, p2, w_ref, wo_ref, kn, vn, qn, gn, xn, on = refs[4 * chunk : 4 * chunk + 10]
    rest = refs[4 * chunk + 10 :]
    if chunk:
        first_ref, rest = rest[0], rest[1:]
        out_ref, rest = rest[0], rest[1:]
        kf, vf = rest[-2:]
    else:
        out_ref, kf, vf = rest[:3]
        rest = rest[3:]
    n_scr, nq_scr, qf, gf, xf, of, qx, kx, vx, ox = rest[:10]
    project(2 * GRP * chunk, 1, sc_ref, (p1, p2), w_ref, kf, vf, qf, gf, xf, n_scr, nq_scr)
    low = sc_ref[3] == 0

    @pl.when(low)
    def _():
        qx[...], kx[...], vx[...] = qf[...], kn[...], vn[...]

    @pl.when(jnp.logical_not(low))
    def _():
        qx[...], kx[...], vx[...] = qn[...], kf[...], vf[...]

    seen = [(past[2 * i], past[2 * i + 1], False) for i in range(2 * chunk)]
    attend(sc_ref, [(qf, of, seen + [(kf, vf, True)]), (qx, ox, [(kx, vx, False)])], 2 - chunk)
    if chunk:
        out_ref[:512, :] = first_ref[...]
    for side, (o_ref, g_ref, x_ref) in enumerate(((on, gn, xn), (of, gf, xf))):
        o = o_ref[...] + jnp.where(sc_ref[3 + side] == 1, ox[...], 0.0)
        c = o - jnp.mean(o, axis=0, keepdims=True)
        var = jnp.mean(c * c, axis=0, keepdims=True)
        gated = ((c * lax.rsqrt(var + 1e-5)) * g_ref[...].astype(F32)).astype(BF)
        mixed = lax.dot_general(gated, wo_ref[...], (((0,), (0,)), ((), ())), preferred_element_type=F32)
        at = pl.multiple_of(512 * chunk + 256 * sc_ref[3 + side], 256)
        out_ref[pl.ds(at, 256), :] = (x_ref[...].astype(F32) + mixed).astype(BF)


SIZES = [(GRP, D), (D, GRP), (D, 256), (D, 256), (256, D)]


def near_call(chunk, sc, past, own, near, w_in):
    inputs = [*past, own, near, w_in]
    outs = pl.pallas_call(
        functools.partial(near_kernel, chunk),
        out_shape=[pltpu.VMEM(s, BF) for s in SIZES] + [pltpu.VMEM((D, 256), F32)],
        in_specs=[SM] + [VM] * len(inputs),
        out_specs=[VM] * 6,
        scratch_shapes=[pltpu.VMEM((2, D, D), BF), pltpu.VMEM((256, D), BF)],
        compiler_params=PARAMS,
        cost_estimate=cost(6 + 6 * chunk),
    )(sc, *inputs)
    return outs


def far_call(chunk, sc, past, far, diag, w_in, w_out, kept, first):
    inputs = [*past, far, diag, w_in, w_out, *kept]
    scratch = [
        pltpu.VMEM((2, D, D), BF),
        pltpu.VMEM((256, D), BF),
        pltpu.VMEM((D, 256), BF),
        pltpu.VMEM((D, 256), BF),
        pltpu.VMEM((256, D), BF),
        pltpu.VMEM((D, 256), F32),
        pltpu.VMEM((D, 256), BF),
        pltpu.VMEM((GRP, D), BF),
        pltpu.VMEM((D, GRP), BF),
        pltpu.VMEM((D, 256), F32),
    ]
    held = [pltpu.VMEM(s, BF) for s in SIZES[:2]]
    if chunk:
        inputs.append(first)
        shapes, scratch = [jax.ShapeDtypeStruct((1024, D), BF)], scratch + held
    else:
        shapes = [pltpu.VMEM((512, D), BF)] + held
    return pl.pallas_call(
        functools.partial(far_kernel, chunk),
        out_shape=shapes,
        in_specs=[SM] + [VM] * len(inputs),
        out_specs=[VM] * len(shapes),
        scratch_shapes=scratch,
        compiler_params=PARAMS,
        cost_estimate=cost(9 + 5 * chunk),
    )(sc, *inputs)


from jax.sharding import Mesh
from jax.sharding import PartitionSpec as P

CTX = ("xh", "xl", "yh", "co")
FLIP = [(0, 1), (1, 0)]


def layer(item_ids, lengths, table, w_in, w_out):
    owned = table.shape[0]
    me = lax.axis_index("dp")
    xh, xl, yh, co = (lax.axis_index(a) for a in CTX)
    owners = lax.axis_size("dp")
    w_in, w_out = in_vmem(w_in), in_vmem(w_out)
    groups = table.reshape(-1, 8, D)

    send = jnp.broadcast_to(item_ids[None], (owners, 4, BLK)).reshape(owners * 4, BLK)
    wanted = lax.all_to_all(send, ("dp", "xh", "yh"), 0, 0, tiled=True).reshape(owners, 4, BLK)
    mine = lax.dynamic_index_in_dim(wanted, me, 0, keepdims=False)
    user = 2 * xh + yh
    length = jnp.sum(jnp.where(lax.iota(jnp.int32, 4) == user, lengths, 0))
    upto = jnp.triu(jnp.ones((2 * BLK, 2 * BLK), BF))
    slots = lax.iota(jnp.int32, 8)
    sc = jnp.zeros((8,), jnp.int32)
    for i, value in enumerate((length, PART * (2 * xl + co), co, xl, 1 - xl)):
        sc = jnp.where(slots == i, value, sc)

    def ranks(member):
        return nn(member.astype(BF), upto).astype(jnp.int32) - 1

    def fetch(c):
        ids = wanted[:, 2 * c : 2 * c + 2].reshape(owners, 2 * BLK)
        local = ids - me * owned
        here = (local >= 0) & (local < owned)
        rank = jnp.where(here, ranks(here), -1)
        slot = lax.broadcasted_iota(jnp.int32, (owners, CAP, 2 * BLK), 1)
        rows = jnp.sum(jnp.where(rank[:, None, :] == slot, local[:, None, :], 0), axis=2)
        count = jnp.sum(here.astype(jnp.int32), axis=1)
        picked = gather_call(rows, count, groups).reshape(owners, CAP, D)
        return lax.all_to_all(picked, "dp", 0, 0, tiled=True).reshape(owners * CAP, D)

    def place(c, got):
        own_ids = mine[2 * c : 2 * c + 2].reshape(2 * BLK)
        owner = own_ids // owned
        member = owner[None, :] == lax.broadcasted_iota(jnp.int32, (owners, 2 * BLK), 0)
        at = jnp.sum(jnp.where(member, ranks(member), 0), axis=0) + owner * CAP
        pick = (at[:, None] == lax.broadcasted_iota(jnp.int32, (2 * BLK, owners * CAP), 1)).astype(BF)
        return nn(pick, got).astype(BF)

    past, first = [], None
    for c in range(2):
        got = fetch(c)
        own = place(c, got)
        far = lax.ppermute(own, "xl", FLIP)
        near = lax.ppermute(own, "co", FLIP)
        diag = lax.ppermute(far, "co", FLIP)
        pieces = [in_vmem(a) for a in (own, near, far, diag)]
        kept = near_call(c, sc, past, *pieces[:2], w_in)
        kept = [in_vmem(a) for a in kept]
        done = far_call(c, sc, past, *pieces[2:], w_in, w_out, kept, first)
        if c == 0:
            first, k1, v1 = (in_vmem(a) for a in done)
            past = [*kept[:2], k1, v1]
    back = lax.all_to_all(done[0].reshape(16, PART, D), CTX, 0, 0, tiled=True)
    back = back.reshape(2, 2, 2, 2, PART, D).transpose(0, 2, 1, 3, 4, 5)
    return back.reshape(4, BLK, D)


def solution(mesh):
    finer = Mesh(mesh.devices.reshape(mesh.shape["dp"], 2, 2, 2, 2), ("dp",) + CTX)
    return jax.shard_map(
        layer,
        mesh=finer,
        in_specs=(P("dp", CTX), P("dp"), P("dp", None), P(), P()),
        out_specs=P("dp", CTX, None),
        check_vma=False,
    )
```

time: 165 us -> 146 us (0.88)
  Pallas kernels: 73.4 us -> 53.2 us
  matrix products: 2.55 us -> 5.36 us
  local copies, waits for them, and re-layouts: 4.3 us -> 2.46 us
    pallas_call x6 -> x4, Pallas kernels: 54.4 us -> 37.9 us  [the longest x2 22 us: far_call(): pl.pallas_call(functools.partial(far_kernel, chunk), out_shape=shapes, in...]
    pallas_call x2, Pallas kernels: 19 us -> 15.3 us  [gather_call(): pl.pallas_call(functools.partial(gather_kernel, owners), out_shape=jax.Sh...]
    dot_general x6, matrix products: 2.55 us -> 5.36 us  [nn(): return jnp.dot(a, b, preferred_element_type=F32)]
  transfers between devices with their start and end apart: 9 -> 9, of which waited for: 3 -> 4; matrix products, arithmetic and copies ran while one was open for 3% -> 5% of each run, Pallas kernels for 25% -> 23%
where the time goes in v3:
time: 146 us; the launch traced here: 144 us
  Pallas kernels  53.2 us (36%)
  waiting for transfers between devices  33.3 us (23%)
  starting transfers between devices  24.5 us (17%)
  blocking collectives  21.6 us (15%)
  matrix products  5.36 us (4%)
  other arithmetic  3.91 us (3%)
  local copies, waits for them, and re-layouts  2.46 us (2%)
    pallas_call x2, Pallas kernels, far_call(): pl.pallas_call(functools.partial(far_kernel, chunk), out_shape=shapes, in...  22 us
    all_to_all x1, blocking collectives, layer(): back = lax.all_to_all(done[0].reshape(16, PART, D), CTX, 0, 0, tiled=True)  21.6 us
    pallas_call x2, Pallas kernels, near_call(): pl.pallas_call(functools.partial(near_kernel, chunk), out_shape=[pltpu.VM...  15.9 us
    pallas_call x2, Pallas kernels, gather_call(): pl.pallas_call(functools.partial(gather_kernel, owners), out_shape=jax.Sh...  15.3 us
    all_to_all x2, waiting for transfers between devices, fetch(): lax.all_to_all(picked, 'dp', 0, 0, tiled=True).reshape(owners * CAP, D)  12.6 us
    ppermute x2, waiting for transfers between devices, layer(): far = lax.ppermute(own, 'xl', FLIP)  11.9 us
    all_to_all x2, starting transfers between devices, fetch(): lax.all_to_all(picked, 'dp', 0, 0, tiled=True).reshape(owners * CAP, D)  11 us
    all_to_all x1, starting transfers between devices, layer(): lax.all_to_all(send, ('dp', 'xh', 'yh'), 0, 0, tiled=True)  11 us
  transfers between devices with their start and end apart: 9, of which 4 were waited for; matrix products, arithmetic and copies ran while one was open for 5% of the time, Pallas kernels for 23%

profile of v3, /device:TPU:8, one launch (start us, length us, event | category | flops | bytes accessed | tf_op | source)
XLA Modules:
  0.0 144.4 jit_solution(2521314526655690308)
XLA Ops:
  0.0 0.7 broadcast_in_dim.74
  0.7 0.7 all_to_all.15
  1.4 11.0 %all-to-all-start = ((s32[32,1,256]{2,1,0:T(1,128)}), s32[32,1,256]{2,1,0:T(1,128)S(1)}, u32[]{:S(2)}, u32[]{:S(2)}) async-start(s32[32,1,256]{2,1,0:T(1,128)} %all_to_all.15), calls=%async_computation | async-start | bytes 65536 | tf_op jit(solution)/shard_map/all_to_all | solution.py:295
  12.4 8.7 %all-to-all-done = s32[32,1,256]{2,1,0:T(1,128)S(1)} async-done(((s32[32,1,256]{2,1,0:T(1,128)}), s32[32,1,256]{2,1,0:T(1,128)S(1)}, u32[]{:S(2)}, u32[]{:S(2)}) %all-to-all-start) | async-done | bytes 32800 | tf_op jit(solution)/shard_map/all_to_all | solution.py:295
  21.2 0.9 fusion.34
  22.4 0.9 select_reduce_fusion.1.rows_ref.ids_ref
  23.2 6.9 %gather.2 = bf16[1024,512]{1,0:T(8,128)(2,1)} custom-call(s32[8,128]{1,0:T(8,128)} %select_reduce_fusion.1.rows_ref.ids_ref, s32[8]{0:T(128)} %get-tuple-element.36.count_ref, s32[8,128]{1,0:T(8,128)} %select_reduce_fusion.1.rows_ref.ids_ref, bf16[2048,8,512]{2,1,0:T(8,128)(2,1)} %bitcast.25), custom_call_target="tpu_custom_call" | custom-call | flops 28000000 | tf_op jit(solution)/shard_map/gather/pallas_call | solution.py:87
  30.2 6.3 %all-to-all-start.1 = ((bf16[8,128,512]{2,1,0:T(8,128)(2,1)}), bf16[8,128,512]{2,1,0:T(8,128)(2,1)S(1)}, u32[]{:S(2)}, u32[]{:S(2)}) async-start(bf16[8,128,512]{2,1,0:T(8,128)(2,1)} %bitcast.28), calls=%async_computation.1 | async-start | bytes 2097152 | tf_op jit(solution)/shard_map/all_to_all | solution.py:317
  36.8 0.9 select_reduce_fusion.rows_ref.ids_ref
  37.7 8.4 %gather.3 = bf16[1024,512]{1,0:T(8,128)(2,1)} custom-call(s32[8,128]{1,0:T(8,128)} %select_reduce_fusion.rows_ref.ids_ref, s32[8]{0:T(128)} %get-tuple-element.35.count_ref, s32[8,128]{1,0:T(8,128)} %select_reduce_fusion.rows_ref.ids_ref, bf16[2048,8,512]{2,1,0:T(8,128)(2,1)} %bitcast.26), custom_call_target="tpu_custom_call" | custom-call | flops 28000000 | tf_op jit(solution)/shard_map/gather/pallas_call | solution.py:87
  46.1 2.1 %all-to-all-done.1 = bf16[8,128,512]{2,1,0:T(8,128)(2,1)S(1)} async-done(((bf16[8,128,512]{2,1,0:T(8,128)(2,1)}), bf16[8,128,512]{2,1,0:T(8,128)(2,1)S(1)}, u32[]{:S(2)}, u32[]{:S(2)}) %all-to-all-start.1) | async-done | bytes 1048608 | tf_op jit(solution)/shard_map/all_to_all | solution.py:317
  48.2 4.7 %all-to-all-start.2 = ((bf16[8,128,512]{2,1,0:T(8,128)(2,1)}), bf16[8,128,512]{2,1,0:T(8,128)(2,1)}, u32[]{:S(2)}, u32[]{:S(2)}) async-start(bf16[8,128,512]{2,1,0:T(8,128)(2,1)} %bitcast.27), calls=%async_computation.2 | async-start | bytes 2097152 | tf_op jit(solution)/shard_map/all_to_all | solution.py:317
  53.4 1.5 %fusion.3.refs_0_ = bf16[512,512]{1,0:T(8,128)(2,1)} fusion(bf16[1024,512]{1,0:T(8,128)(2,1)S(1)} %bitcast.30, s32[512]{0:T(512)S(1)} %multiply_add_fusion.1), kind=kOutput, calls=%fused_computation.9 | convolution fusion | flops 537657344 | bytes 1574912 | tf_op jit(solution)/shard_map/dot_general | solution.py:41
  55.5 10.5 %all-to-all-done.2 = bf16[8,128,512]{2,1,0:T(8,128)(2,1)} async-done(((bf16[8,128,512]{2,1,0:T(8,128)(2,1)}), bf16[8,128,512]{2,1,0:T(8,128)(2,1)}, u32[]{:S(2)}, u32[]{:S(2)}) %all-to-all-start.2) | async-done | bytes 1048608 | tf_op jit(solution)/shard_map/all_to_all | solution.py:317
  66.0 2.8 %fusion.2.refs_4_ = bf16[512,512]{1,0:T(8,128)(2,1)} fusion(bf16[1024,512]{1,0:T(8,128)(2,1)} %bitcast.4, s32[512]{0:T(512)S(1)} %multiply_add_fusion), kind=kOutput, calls=%fused_computation.8 | convolution fusion | flops 537657344 | bytes 1574912 | tf_op jit(solution)/shard_map/dot_general | solution.py:41
  68.8 1.4 collective-permute-start.3
  70.7 11.9 %collective-permute-done.3.refs_4_ = bf16[512,512]{1,0:T(8,128)(2,1)} collective-permute-done((bf16[512,512]{1,0:T(8,128)(2,1)}, bf16[512,512]{1,0:T(8,128)(2,1)}, u32[]{:S(2)}, u32[]{:S(2)}) %collective-permute-start.3) | collective-permute-done | bytes 524320 | tf_op jit(solution)/shard_map/ppermute | solution.py:331
  82.7 0.6 fusion.53
  83.8 6.3 %shard_map.55 = (bf16[1024,512]{1,0:T(8,128)(2,1)S(1)}, bf16[512,1024]{1,0:T(8,128)(2,1)S(1)}, bf16[512,256]{1,0:T(8,128)(2,1)S(1)}, bf16[512,256]{1,0:T(8,128)(...) custom-call(s32[8]{0:T(128)S(1)} %compare_select_fusion.5.sc_ref, bf16[512,512]{1,0:T(8,128)(2,1)} %fusion.3.refs_0_, ...), custom_call_target="tpu_custom_call" | custom-call | flops 24000000 | tf_op jit(solution)/shard_map/pallas_call | solution.py:236
  90.1 9.0 %shard_map.56 = (bf16[512,512]{1,0:T(8,128)(2,1)S(1)}, bf16[1024,512]{1,0:T(8,128)(2,1)S(1)}, bf16[512,1024]{1,0:T(8,128)(2,1)S(1)}) custom-call(s32[8]{0:T(128)S(1)} %compare_select_fusion.5.sc_ref, bf16[512,512]{1,0:T(8,128)(2,1)S(1)} %collective-permute-done.1.refs_0_, bf16[512,512]{1,0:T(8,128)(2,1)} %collective-permute-done.2.refs_1_, ...), custom_call_target="tpu_custom_call" | custom-call | flops 36000000 | tf_op jit(solution)/shard_map/pallas_call | solution.py:268
  99.2 9.6 %shard_map.57 = (bf16[1024,512]{1,0:T(8,128)(2,1)S(1)}, bf16[512,1024]{1,0:T(8,128)(2,1)S(1)}, bf16[512,256]{1,0:T(8,128)(2,1)S(1)}, bf16[512,256]{1,0:T(8,128)(...) custom-call(s32[8]{0:T(128)S(1)} %compare_select_fusion.5.sc_ref, ...), custom_call_target="tpu_custom_call" | custom-call | flops 48000000 | tf_op jit(solution)/shard_map/pallas_call | solution.py:236
  108.8 13.0 %shard_map.58 = bf16[1024,512]{1,0:T(8,128)(2,1)S(1)} custom-call(s32[8]{0:T(128)S(1)} %compare_select_fusion.5.sc_ref, bf16[1024,512]{1,0:T(8,128)(2,1)S(1)} %get-tuple-element.20.refs_4_.refs_0_, bf16[512,1024]{1,0:T(8,128)(2,1)S(1)} %get-tuple-element.21.refs_5_.refs_1_, bf16[1024,512]{1,0:T(8,128)(2,1)S(1)} %get-tuple-element.26.refs_2_, ...), custom_call_target="tpu_custom_call" | custom-call | flops 56000000 | tf_op jit(solution)/shard_map/pallas_call | solution.py:268
  121.8 21.6 %all_to_all.24 = bf16[16,64,512]{2,1,0:T(8,128)(2,1)S(1)} all-to-all(bf16[16,64,512]{2,1,0:T(8,128)(2,1)S(1)} %bitcast.24), channel_id=1, replica_groups=mesh['dp'=8,'xh'=2,'xl'=2,'yh'=2,'co'=2] {'xh','xl','yh','co'}, dimensions={0} | all-to-all | bytes 2097152 | tf_op jit(solution)/shard_map/all_to_all | solution.py:341
  143.3 1.1 copy.9
  (33 shorter events, 2.8 us)
Async XLA Ops:
  1.4 19.8 %all-to-all-start = ((s32[32,1,256]{2,1,0:T(1,128)}), s32[32,1,256]{2,1,0:T(1,128)S(1)}, u32[]{:S(2)}, u32[]{:S(2)}) async-start(s32[32,1,256]{2,1,0:T(1,128)} %all_to_all.15), calls=%async_computation | async-start | bytes 65536 | tf_op jit(solution)/shard_map/all_to_all | solution.py:295
  30.2 18.0 %all-to-all-start.1 = ((bf16[8,128,512]{2,1,0:T(8,128)(2,1)}), bf16[8,128,512]{2,1,0:T(8,128)(2,1)S(1)}, u32[]{:S(2)}, u32[]{:S(2)}) async-start(bf16[8,128,512]{2,1,0:T(8,128)(2,1)} %bitcast.28), calls=%async_computation.1 | async-start | bytes 2097152 | tf_op jit(solution)/shard_map/all_to_all | solution.py:317
  48.2 17.8 %all-to-all-start.2 = ((bf16[8,128,512]{2,1,0:T(8,128)(2,1)}), bf16[8,128,512]{2,1,0:T(8,128)(2,1)}, u32[]{:S(2)}, u32[]{:S(2)}) async-start(bf16[8,128,512]{2,1,0:T(8,128)(2,1)} %bitcast.27), calls=%async_computation.2 | async-start | bytes 2097152 | tf_op jit(solution)/shard_map/all_to_all | solution.py:317
  55.0 27.7 %copy-start.2 = (s32[4]{0:T(128)S(1)}, s32[4]{0:T(128)}, u32[]{:S(2)}) copy-start(s32[4]{0:T(128)} %param.6) | copy-start | bytes 52
  55.0 28.8 %copy-start = (bf16[512,2048]{1,0:T(8,128)(2,1)S(1)}, bf16[512,2048]{1,0:T(8,128)(2,1)}, u32[]{:S(2)}) copy-start(bf16[512,2048]{1,0:T(8,128)(2,1)} %refs_6_.3) | copy-start | bytes 6291460
  55.0 15.2 %collective-permute-start.1 = (bf16[512,512]{1,0:T(8,128)(2,1)}, bf16[512,512]{1,0:T(8,128)(2,1)S(1)}, u32[]{:S(2)}, u32[]{:S(2)}) collective-permute-start(bf16[512,512]{1,0:T(8,128)(2,1)} %fusion.3.refs_0_), channel_id=1, source_target_pairs={{0,4},{4,0},{1,5},{5,1},{2,6},{6,2},{3,7},{7,3},{8,12},{12,8},{9,1... | collective-permute-start | bytes 1572872 | tf_op jit(solution)/shard_map/ppermute | solution.py:331
  68.8 21.4 %copy-start.1 = (bf16[512,512]{1,0:T(8,128)(2,1)S(1)}, bf16[512,512]{1,0:T(8,128)(2,1)}, u32[]{:S(2)}) copy-start(bf16[512,512]{1,0:T(8,128)(2,1)} %refs_7_.1) | copy-start | bytes 1572868
  68.8 13.9 %collective-permute-start.3 = (bf16[512,512]{1,0:T(8,128)(2,1)}, bf16[512,512]{1,0:T(8,128)(2,1)}, u32[]{:S(2)}, u32[]{:S(2)}) collective-permute-start(bf16[512,512]{1,0:T(8,128)(2,1)} %fusion.2.refs_4_), channel_id=1, source_target_pairs={{0,4},{4,0},{1,5},{5,1},{2,6},{6,2},{3,7},{7,3},{8,12},{12,8},{9,1... | collective-permute-start | bytes 1572872 | tf_op jit(solution)/shard_map/ppermute | solution.py:331
  70.2 13.6 %collective-permute-start = (bf16[512,512]{1,0:T(8,128)(2,1)}, bf16[512,512]{1,0:T(8,128)(2,1)}, u32[]{:S(2)}, u32[]{:S(2)}) collective-permute-start(bf16[512,512]{1,0:T(8,128)(2,1)} %fusion.3.refs_0_), channel_id=1, source_target_pairs={{0,1},{1,0},{2,3},{3,2},{4,5},{5,4},{6,7},{7,6},{8,9},{9,8},{10,11... | collective-permute-start | bytes 1572872 | tf_op jit(solution)/shard_map/ppermute | solution.py:332
  70.2 19.9 %collective-permute-start.2 = (bf16[512,512]{1,0:T(8,128)(2,1)S(1)}, bf16[512,512]{1,0:T(8,128)(2,1)}, u32[]{:S(2)}, u32[]{:S(2)}) collective-permute-start(bf16[512,512]{1,0:T(8,128)(2,1)S(1)} %collective-permute-done.1.refs_0_), channel_id=1, source_target_pairs={{0,1},{1,0},{2,3},{3,2},{4,5},{5,4},{6,7},{7,6},{8,9},{9,8},{10,11... | collective-permute-start | bytes 1572872 | tf_op jit(solution)/shard_map/ppermute | solution.py:333
  70.7 28.5 %collective-permute-start.5 = (bf16[512,512]{1,0:T(8,128)(2,1)}, bf16[512,512]{1,0:T(8,128)(2,1)}, u32[]{:S(2)}, u32[]{:S(2)}) collective-permute-start(bf16[512,512]{1,0:T(8,128)(2,1)} %fusion.2.refs_4_), channel_id=1, source_target_pairs={{0,1},{1,0},{2,3},{3,2},{4,5},{5,4},{6,7},{7,6},{8,9},{9,8},{10,11... | collective-permute-start | bytes 1572872 | tf_op jit(solution)/shard_map/ppermute | solution.py:332
  82.6 26.2 %collective-permute-start.4 = (bf16[512,512]{1,0:T(8,128)(2,1)}, bf16[512,512]{1,0:T(8,128)(2,1)}, u32[]{:S(2)}, u32[]{:S(2)}) collective-permute-start(bf16[512,512]{1,0:T(8,128)(2,1)} %collective-permute-done.3.refs_4_), channel_id=1, source_target_pairs={{0,1},{1,0},{2,3},{3,2},{4,5},{5,4},{6,7},{7,6},{8,9},{9,8},{10,11... | collective-permute-start | bytes 1572872 | tf_op jit(solution)/shard_map/ppermute | solution.py:333

commit v4 on v3

--- a/solution.py
+++ b/solution.py
@@ -94,6 +94,25 @@
         cost_estimate=cost(7),
         name="gather",
     )(rows, count, rows, groups)
+
+
+def place_kernel(at_ref, got_ref, own_ref):
+    rows, slots = own_ref.shape[0], got_ref.shape[0]
+    at = jnp.broadcast_to(at_ref[...].astype(F32), (8, rows)).T[:, :1]
+    slot = lax.broadcasted_iota(jnp.int32, (rows, slots), 1).astype(F32)
+    own_ref[...] = nn((slot == at).astype(F32).astype(BF), got_ref[...]).astype(BF)
+
+
+def place_call(at, got):
+    return pl.pallas_call(
+        place_kernel,
+        out_shape=pltpu.VMEM((at.shape[1], D), BF),
+        in_specs=[VM, VM],
+        out_specs=VM,
+        compiler_params=PARAMS,
+        cost_estimate=cost(1.5),
+        name="place",
+    )(at, got)
 
 
 def project(first, side, sc_ref, pieces, w_ref, k_ref, v_ref, q_ref, g_ref, x_ref, n_scr, nq_scr):
@@ -161,8 +180,13 @@
 
         def add_values(step, w):
             u, t, m, i = step
-            o = nn(tiles[t][2][m][1][pl.ds(lanes(u), 128), i * BLK : (i + 1) * BLK], w)
-            o = (o[:64, :256], o[64:, 256:])
+            o = [
+                nn(
+                    tiles[t][2][m][1][pl.ds(pl.multiple_of(lanes(u) + 64 * hh, 64), 64), i * BLK : (i + 1) * BLK],
+                    w[:, 256 * hh : 256 * (hh + 1)],
+                )
+                for hh in range(2)
+            ]
             old = sums.get((u, t))
             sums[u, t] = o if old is None else (old[0] + o[0], old[1] + o[1])
 
@@ -215,7 +239,7 @@
         qx[...], kx[...], vx[...] = qn[...], kf[...], vf[...]
 
     seen = [(past[2 * i], past[2 * i + 1], False) for i in range(2 * chunk)]
-    attend(sc_ref, [(qf, of, seen + [(kf, vf, True)]), (qx, ox, [(kx, vx, False)])], 2 - chunk)
+    attend(sc_ref, [(qf, of, seen + [(kf, vf, True)]), (qx, ox, [(kx, vx, False)])], 2)
     if chunk:
         out_ref[:512, :] = first_ref[...]
     for side, (o_ref, g_ref, x_ref) in enumerate(((on, gn, xn), (of, gf, xf))):
@@ -224,8 +248,10 @@
         var = jnp.mean(c * c, axis=0, keepdims=True)
         gated = ((c * lax.rsqrt(var + 1e-5)) * g_ref[...].astype(F32)).astype(BF)
         mixed = lax.dot_general(gated, wo_ref[...], (((0,), (0,)), ((), ())), preferred_element_type=F32)
-        at = pl.multiple_of(512 * chunk + 256 * sc_ref[3 + side], 256)
-        out_ref[pl.ds(at, 256), :] = (x_ref[...].astype(F32) + mixed).astype(BF)
+        out = (x_ref[...].astype(F32) + mixed).astype(BF)
+        for j in range(2):
+            at = pl.multiple_of(512 * chunk + 256 * j + 128 * sc_ref[3 + side], 128)
+            out_ref[pl.ds(at, 128), :] = out[128 * j : 128 * (j + 1)]
 
 
 SIZES = [(GRP, D), (D, GRP), (D, 256), (D, 256), (256, D)]
@@ -291,7 +317,7 @@
     w_in, w_out = in_vmem(w_in), in_vmem(w_out)
     groups = table.reshape(-1, 8, D)
 
-    send = jnp.broadcast_to(item_ids[None], (owners, 4, BLK)).reshape(owners * 4, BLK)
+    send = jnp.broadcast_to(item_ids[None, :, None], (owners, 4, 1, BLK)).reshape(owners * 4, 1, BLK)
     wanted = lax.all_to_all(send, ("dp", "xh", "yh"), 0, 0, tiled=True).reshape(owners, 4, BLK)
     mine = lax.dynamic_index_in_dim(wanted, me, 0, keepdims=False)
     user = 2 * xh + yh
@@ -321,8 +347,7 @@
         owner = own_ids // owned
         member = owner[None, :] == lax.broadcasted_iota(jnp.int32, (owners, 2 * BLK), 0)
         at = jnp.sum(jnp.where(member, ranks(member), 0), axis=0) + owner * CAP
-        pick = (at[:, None] == lax.broadcasted_iota(jnp.int32, (2 * BLK, owners * CAP), 1)).astype(BF)
-        return nn(pick, got).astype(BF)
+        return in_vmem(place_call(at[None], got))
 
     past, first = [], None
     for c in range(2):
@@ -338,8 +363,7 @@
         if c == 0:
             first, k1, v1 = (in_vmem(a) for a in done)
             past = [*kept[:2], k1, v1]
-    back = lax.all_to_all(done[0].reshape(16, PART, D), CTX, 0, 0, tiled=True)
-    back = back.reshape(2, 2, 2, 2, PART, D).transpose(0, 2, 1, 3, 4, 5)
+    back = lax.all_to_all(done[0].reshape(16, PART, D), ("xh", "yh", "xl", "co"), 0, 0, tiled=True)
     return back.reshape(4, BLK, D)
 
 

time: 146 us -> 144 us (0.986)
  matrix products: 5.36 us -> 1.04 us
  Pallas kernels: 53.2 us -> 55.4 us
    dot_general x6 -> x4, matrix products: 5.36 us -> 1.04 us  [nn(): return jnp.dot(a, b, preferred_element_type=F32)]
    pallas_call x0 -> x2, Pallas kernels: none -> 4.04 us  [place_call(): pl.pallas_call(place_kernel, out_shape=pltpu.VMEM((at.shape[1], D), BF),...]
  transfers between devices with their start and end apart: 9 -> 9, of which waited for: 4 -> 4; matrix products, arithmetic and copies ran while one was open for 5% -> 2% of each run, Pallas kernels for 23% -> 26%
where the time goes in v4:
time: 144 us; the launch traced here: 142 us
  Pallas kernels  55.4 us (38%)
  waiting for transfers between devices  32.8 us (23%)
  starting transfers between devices  24.6 us (17%)
  blocking collectives  21.5 us (15%)
  other arithmetic  3.92 us (3%)
  local copies, waits for them, and re-layouts  2.38 us (2%)
    all_to_all x1, blocking collectives, layer(): lax.all_to_all(done[0].reshape(16, PART, D), ('xh', 'yh', 'xl', 'co'), 0,...  21.5 us
    pallas_call x2, Pallas kernels, far_call(): pl.pallas_call(functools.partial(far_kernel, chunk), out_shape=shapes, in...  21 us
    pallas_call x2, Pallas kernels, gather_call(): pl.pallas_call(functools.partial(gather_kernel, owners), out_shape=jax.Sh...  15.3 us
    pallas_call x2, Pallas kernels, near_call(): pl.pallas_call(functools.partial(near_kernel, chunk), out_shape=[pltpu.VM...  15.1 us
    all_to_all x2, waiting for transfers between devices, fetch(): lax.all_to_all(picked, 'dp', 0, 0, tiled=True).reshape(owners * CAP, D)  12.3 us
    ppermute x2, waiting for transfers between devices, layer(): far = lax.ppermute(own, 'xl', FLIP)  11.7 us
    all_to_all x2, starting transfers between devices, fetch(): lax.all_to_all(picked, 'dp', 0, 0, tiled=True).reshape(owners * CAP, D)  11 us
    all_to_all x1, starting transfers between devices, layer(): lax.all_to_all(send, ('dp', 'xh', 'yh'), 0, 0, tiled=True)  11 us
  transfers between devices with their start and end apart: 9, of which 4 were waited for; matrix products, arithmetic and copies ran while one was open for 2% of the time, Pallas kernels for 26%

profile of v4, /device:TPU:8, one launch (start us, length us, event | category | flops | bytes accessed | tf_op | source)
XLA Modules:
  0.0 141.9 jit_solution(1159896521301537804)
XLA Ops:
  0.0 0.7 broadcast_in_dim.76
  0.7 0.7 broadcast_in_dim.77
  1.4 11.0 %all-to-all-start = ((s32[32,1,256]{2,1,0:T(1,128)}), s32[32,1,256]{2,1,0:T(1,128)S(1)}, u32[]{:S(2)}, u32[]{:S(2)}) async-start(s32[32,1,256]{2,1,0:T(1,128)} %broadcast_in_dim.77), calls=%async_computation | async-start | bytes 65536 | tf_op jit(solution)/shard_map/all_to_all | solution.py:321
  12.4 8.7 %all-to-all-done = s32[32,1,256]{2,1,0:T(1,128)S(1)} async-done(((s32[32,1,256]{2,1,0:T(1,128)}), s32[32,1,256]{2,1,0:T(1,128)S(1)}, u32[]{:S(2)}, u32[]{:S(2)}) %all-to-all-start) | async-done | bytes 32800 | tf_op jit(solution)/shard_map/all_to_all | solution.py:321
  21.3 0.9 fusion.28
  22.4 0.9 select_reduce_fusion.1.rows_ref.ids_ref
  23.3 6.9 %gather.2 = bf16[1024,512]{1,0:T(8,128)(2,1)} custom-call(s32[8,128]{1,0:T(8,128)} %select_reduce_fusion.1.rows_ref.ids_ref, s32[8]{0:T(128)} %get-tuple-element.36.count_ref, s32[8,128]{1,0:T(8,128)} %select_reduce_fusion.1.rows_ref.ids_ref, bf16[2048,8,512]{2,1,0:T(8,128)(2,1)} %bitcast.29), custom_call_target="tpu_custom_call" | custom-call | flops 28000000 | tf_op jit(solution)/shard_map/gather/pallas_call | solution.py:87
  30.2 6.3 %all-to-all-start.1 = ((bf16[8,128,512]{2,1,0:T(8,128)(2,1)}), bf16[8,128,512]{2,1,0:T(8,128)(2,1)S(1)}, u32[]{:S(2)}, u32[]{:S(2)}) async-start(bf16[8,128,512]{2,1,0:T(8,128)(2,1)} %bitcast.32), calls=%async_computation.1 | async-start | bytes 2097152 | tf_op jit(solution)/shard_map/all_to_all | solution.py:343
  36.8 0.9 select_reduce_fusion.rows_ref.ids_ref
  37.7 8.4 %gather.3 = bf16[1024,512]{1,0:T(8,128)(2,1)} custom-call(s32[8,128]{1,0:T(8,128)} %select_reduce_fusion.rows_ref.ids_ref, s32[8]{0:T(128)} %get-tuple-element.35.count_ref, s32[8,128]{1,0:T(8,128)} %select_reduce_fusion.rows_ref.ids_ref, bf16[2048,8,512]{2,1,0:T(8,128)(2,1)} %bitcast.30), custom_call_target="tpu_custom_call" | custom-call | flops 28000000 | tf_op jit(solution)/shard_map/gather/pallas_call | solution.py:87
  46.1 2.1 %all-to-all-done.1 = bf16[8,128,512]{2,1,0:T(8,128)(2,1)S(1)} async-done(((bf16[8,128,512]{2,1,0:T(8,128)(2,1)}), bf16[8,128,512]{2,1,0:T(8,128)(2,1)S(1)}, u32[]{:S(2)}, u32[]{:S(2)}) %all-to-all-start.1) | async-done | bytes 1048608 | tf_op jit(solution)/shard_map/all_to_all | solution.py:343
  48.2 4.7 %all-to-all-start.2 = ((bf16[8,128,512]{2,1,0:T(8,128)(2,1)}), bf16[8,128,512]{2,1,0:T(8,128)(2,1)}, u32[]{:S(2)}, u32[]{:S(2)}) async-start(bf16[8,128,512]{2,1,0:T(8,128)(2,1)} %bitcast.31), calls=%async_computation.2 | async-start | bytes 2097152 | tf_op jit(solution)/shard_map/all_to_all | solution.py:343
  53.5 1.8 %place.2.refs_0_ = bf16[512,512]{1,0:T(8,128)(2,1)} custom-call(s32[1,512]{1,0:T(1,128)S(1)} %multiply_add_fusion.1.at_ref, bf16[1024,512]{1,0:T(8,128)(2,1)S(1)} %bitcast.28), custom_call_target="tpu_custom_call" | custom-call | flops 6000000 | tf_op jit(solution)/shard_map/place/pallas_call | solution.py:107
  55.8 10.2 %all-to-all-done.2 = bf16[8,128,512]{2,1,0:T(8,128)(2,1)} async-done(((bf16[8,128,512]{2,1,0:T(8,128)(2,1)}), bf16[8,128,512]{2,1,0:T(8,128)(2,1)}, u32[]{:S(2)}, u32[]{:S(2)}) %all-to-all-start.2) | async-done | bytes 1048608 | tf_op jit(solution)/shard_map/all_to_all | solution.py:343
  66.1 2.3 %place.3.refs_4_ = bf16[512,512]{1,0:T(8,128)(2,1)S(1)} custom-call(s32[1,512]{1,0:T(1,128)S(1)} %multiply_add_fusion.at_ref, bf16[1024,512]{1,0:T(8,128)(2,1)} %bitcast.6.got_ref), custom_call_target="tpu_custom_call" | custom-call | flops 6000000 | tf_op jit(solution)/shard_map/place/pallas_call | solution.py:107
  68.3 1.5 %collective-permute-start.3 = (bf16[512,512]{1,0:T(8,128)(2,1)S(1)}, bf16[512,512]{1,0:T(8,128)(2,1)}, u32[]{:S(2)}, u32[]{:S(2)}) collective-permute-start(bf16[512,512]{1,0:T(8,128)(2,1)S(1)} %place.3.refs_4_), channel_id=1, source_target_pairs={{0,4},{4,0},{1,5},{5,1},{2,6},{6,2},{3,7},{7,3},{8,12},{12,8},{9,1... | collective-permute-start | bytes 1572872 | tf_op jit(solution)/shard_map/ppermute | solution.py:356
  70.3 11.7 %collective-permute-done.3.refs_4_ = bf16[512,512]{1,0:T(8,128)(2,1)} collective-permute-done((bf16[512,512]{1,0:T(8,128)(2,1)S(1)}, bf16[512,512]{1,0:T(8,128)(2,1)}, u32[]{:S(2)}, u32[]{:S(2)}) %collective-permute-start.3) | collective-permute-done | bytes 524320 | tf_op jit(solution)/shard_map/ppermute | solution.py:356
  82.1 0.6 fusion.47
  83.2 6.1 %shard_map.55 = (bf16[1024,512]{1,0:T(8,128)(2,1)S(1)}, bf16[512,1024]{1,0:T(8,128)(2,1)S(1)}, bf16[512,256]{1,0:T(8,128)(2,1)S(1)}, bf16[512,256]{1,0:T(8,128)(...) custom-call(s32[8]{0:T(128)S(1)} %compare_select_fusion.11.sc_ref, bf16[512,512]{1,0:T(8,128)(2,1)} %place.2.refs_0_, ...), custom_call_target="tpu_custom_call" | custom-call | flops 24000000 | tf_op jit(solution)/shard_map/pallas_call | solution.py:262
  89.4 9.0 %shard_map.56 = (bf16[512,512]{1,0:T(8,128)(2,1)S(1)}, bf16[1024,512]{1,0:T(8,128)(2,1)S(1)}, bf16[512,1024]{1,0:T(8,128)(2,1)S(1)}) custom-call(s32[8]{0:T(128)S(1)} %compare_select_fusion.11.sc_ref, bf16[512,512]{1,0:T(8,128)(2,1)} %collective-permute-done.1.refs_0_, bf16[512,512]{1,0:T(8,128)(2,1)} %collective-permute-done.2.refs_1_, ...), custom_call_target="tpu_custom_call" | custom-call | flops 36000000 | tf_op jit(solution)/shard_map/pallas_call | solution.py:294
  98.5 8.9 %shard_map.57 = (bf16[1024,512]{1,0:T(8,128)(2,1)S(1)}, bf16[512,1024]{1,0:T(8,128)(2,1)S(1)}, bf16[512,256]{1,0:T(8,128)(2,1)S(1)}, bf16[512,256]{1,0:T(8,128)(...) custom-call(s32[8]{0:T(128)S(1)} %compare_select_fusion.11.sc_ref, ...), custom_call_target="tpu_custom_call" | custom-call | flops 48000000 | tf_op jit(solution)/shard_map/pallas_call | solution.py:262
  107.4 11.9 %shard_map.58 = bf16[1024,512]{1,0:T(8,128)(2,1)S(1)} custom-call(s32[8]{0:T(128)S(1)} %compare_select_fusion.11.sc_ref, bf16[1024,512]{1,0:T(8,128)(2,1)S(1)} %get-tuple-element.20.refs_4_.refs_0_, bf16[512,1024]{1,0:T(8,128)(2,1)S(1)} %get-tuple-element.21.refs_5_.refs_1_, bf16[1024,512]{1,0:T(8,128)(2,1)S(1)} %get-tuple-element.26.refs_2_, ...), custom_call_target="tpu_custom_call" | custom-call | flops 56000000 | tf_op jit(solution)/shard_map/pallas_call | solution.py:294
  119.3 21.5 %all_to_all.20 = bf16[16,64,512]{2,1,0:T(8,128)(2,1)S(1)} all-to-all(bf16[16,64,512]{2,1,0:T(8,128)(2,1)S(1)} %bitcast.27), channel_id=1, replica_groups=mesh['dp'=8,'xh'=2,'xl'=2,'yh'=2,'co'=2] {'xh','yh','xl','co'}, dimensions={0} | all-to-all | bytes 2097152 | tf_op jit(solution)/shard_map/all_to_all | solution.py:366
  140.9 1.0 copy.14
  (34 shorter events, 2.8 us)
Async XLA Ops:
  1.4 19.8 %all-to-all-start = ((s32[32,1,256]{2,1,0:T(1,128)}), s32[32,1,256]{2,1,0:T(1,128)S(1)}, u32[]{:S(2)}, u32[]{:S(2)}) async-start(s32[32,1,256]{2,1,0:T(1,128)} %broadcast_in_dim.77), calls=%async_computation | async-start | bytes 65536 | tf_op jit(solution)/shard_map/all_to_all | solution.py:321
  30.2 18.0 %all-to-all-start.1 = ((bf16[8,128,512]{2,1,0:T(8,128)(2,1)}), bf16[8,128,512]{2,1,0:T(8,128)(2,1)S(1)}, u32[]{:S(2)}, u32[]{:S(2)}) async-start(bf16[8,128,512]{2,1,0:T(8,128)(2,1)} %bitcast.32), calls=%async_computation.1 | async-start | bytes 2097152 | tf_op jit(solution)/shard_map/all_to_all | solution.py:343
  48.2 17.8 %all-to-all-start.2 = ((bf16[8,128,512]{2,1,0:T(8,128)(2,1)}), bf16[8,128,512]{2,1,0:T(8,128)(2,1)}, u32[]{:S(2)}, u32[]{:S(2)}) async-start(bf16[8,128,512]{2,1,0:T(8,128)(2,1)} %bitcast.31), calls=%async_computation.2 | async-start | bytes 2097152 | tf_op jit(solution)/shard_map/all_to_all | solution.py:343
  53.2 28.9 %copy-start.2 = (s32[4]{0:T(128)S(1)}, s32[4]{0:T(128)}, u32[]{:S(2)}) copy-start(s32[4]{0:T(128)} %param.6) | copy-start | bytes 52
  53.2 30.0 %copy-start = (bf16[512,2048]{1,0:T(8,128)(2,1)S(1)}, bf16[512,2048]{1,0:T(8,128)(2,1)}, u32[]{:S(2)}) copy-start(bf16[512,2048]{1,0:T(8,128)(2,1)} %refs_6_.3) | copy-start | bytes 6291460
  55.3 14.5 %collective-permute-start.1 = (bf16[512,512]{1,0:T(8,128)(2,1)}, bf16[512,512]{1,0:T(8,128)(2,1)}, u32[]{:S(2)}, u32[]{:S(2)}) collective-permute-start(bf16[512,512]{1,0:T(8,128)(2,1)} %place.2.refs_0_), channel_id=1, source_target_pairs={{0,4},{4,0},{1,5},{5,1},{2,6},{6,2},{3,7},{7,3},{8,12},{12,8},{9,1... | collective-permute-start | bytes 1572872 | tf_op jit(solution)/shard_map/ppermute | solution.py:356
  66.1 23.3 %copy-start.1 = (bf16[512,512]{1,0:T(8,128)(2,1)S(1)}, bf16[512,512]{1,0:T(8,128)(2,1)}, u32[]{:S(2)}) copy-start(bf16[512,512]{1,0:T(8,128)(2,1)} %refs_7_.1) | copy-start | bytes 1572868
  68.3 13.7 %collective-permute-start.3 = (bf16[512,512]{1,0:T(8,128)(2,1)S(1)}, bf16[512,512]{1,0:T(8,128)(2,1)}, u32[]{:S(2)}, u32[]{:S(2)}) collective-permute-start(bf16[512,512]{1,0:T(8,128)(2,1)S(1)} %place.3.refs_4_), channel_id=1, source_target_pairs={{0,4},{4,0},{1,5},{5,1},{2,6},{6,2},{3,7},{7,3},{8,12},{12,8},{9,1... | collective-permute-start | bytes 1572872 | tf_op jit(solution)/shard_map/ppermute | solution.py:356
  69.8 13.4 %collective-permute-start = (bf16[512,512]{1,0:T(8,128)(2,1)}, bf16[512,512]{1,0:T(8,128)(2,1)}, u32[]{:S(2)}, u32[]{:S(2)}) collective-permute-start(bf16[512,512]{1,0:T(8,128)(2,1)} %place.2.refs_0_), channel_id=1, source_target_pairs={{0,1},{1,0},{2,3},{3,2},{4,5},{5,4},{6,7},{7,6},{8,9},{9,8},{10,11... | collective-permute-start | bytes 1572872 | tf_op jit(solution)/shard_map/ppermute | solution.py:357
  69.8 19.6 %collective-permute-start.2 = (bf16[512,512]{1,0:T(8,128)(2,1)}, bf16[512,512]{1,0:T(8,128)(2,1)}, u32[]{:S(2)}, u32[]{:S(2)}) collective-permute-start(bf16[512,512]{1,0:T(8,128)(2,1)} %collective-permute-done.1.refs_0_), channel_id=1, source_target_pairs={{0,1},{1,0},{2,3},{3,2},{4,5},{5,4},{6,7},{7,6},{8,9},{9,8},{10,11... | collective-permute-start | bytes 1572872 | tf_op jit(solution)/shard_map/ppermute | solution.py:358
  70.3 28.1 %collective-permute-start.5 = (bf16[512,512]{1,0:T(8,128)(2,1)S(1)}, bf16[512,512]{1,0:T(8,128)(2,1)}, u32[]{:S(2)}, u32[]{:S(2)}) collective-permute-start(bf16[512,512]{1,0:T(8,128)(2,1)S(1)} %place.3.refs_4_), channel_id=1, source_target_pairs={{0,1},{1,0},{2,3},{3,2},{4,5},{5,4},{6,7},{7,6},{8,9},{9,8},{10,11... | collective-permute-start | bytes 1572872 | tf_op jit(solution)/shard_map/ppermute | solution.py:357
  82.1 25.4 %collective-permute-start.4 = (bf16[512,512]{1,0:T(8,128)(2,1)}, bf16[512,512]{1,0:T(8,128)(2,1)}, u32[]{:S(2)}, u32[]{:S(2)}) collective-permute-start(bf16[512,512]{1,0:T(8,128)(2,1)} %collective-permute-done.3.refs_4_), channel_id=1, source_target_pairs={{0,1},{1,0},{2,3},{3,2},{4,5},{5,4},{6,7},{7,6},{8,9},{9,8},{10,11... | collective-permute-start | bytes 1572872 | tf_op jit(solution)/shard_map/ppermute | solution.py:358

commit v5 on v4

--- a/solution.py
+++ b/solution.py
@@ -41,78 +41,96 @@
     return jnp.dot(a, b, preferred_element_type=F32)
 
 
-def gather_kernel(owners, rows_ref, count_ref, ids_ref, table_ref, out_ref, buf, sems):
-    def eights(o):
-        return (count_ref[o] + ROW8 - 1) // ROW8
-
-    for o in range(owners):
-
-        def start(j, _, o=o):
+def gather_kernel(owners, outs, rows_ref, count_ref, ids_ref, table_ref, *refs):
+    out_refs, (buf, sems) = refs[:outs], refs[outs:]
+    me = lax.axis_index("dp") if outs > 1 else 0
+
+    def who(k):
+        return jnp.bitwise_xor(me, k) if outs > 1 else k
+
+    def eights(k):
+        return (count_ref[who(k)] + ROW8 - 1) // ROW8
+
+    for k in range(owners):
+        o = who(k)
+
+        def start(j, _, k=k, o=o):
             for i in range(ROW8):
                 s = j * ROW8 + i
                 pltpu.make_async_copy(
-                    table_ref.at[lax.shift_right_logical(rows_ref[o, s], 3)], buf.at[o * CAP + s], sems.at[o]
+                    table_ref.at[lax.shift_right_logical(rows_ref[o, s], 3)], buf.at[k * CAP + s], sems.at[k]
                 ).start()
             return 0
 
-        def clear(j, _, o=o):
-            buf[pl.ds(o * CAP + j * ROW8, ROW8)] = jnp.zeros((ROW8, 8, D), BF)
+        def clear(j, _, k=k):
+            buf[pl.ds(k * CAP + j * ROW8, ROW8)] = jnp.zeros((ROW8, 8, D), BF)
             return 0
 
-        lax.fori_loop(0, eights(o), start, 0)
+        lax.fori_loop(0, eights(k), start, 0)
         full = BUNCH // ROW8
-        lax.fori_loop(eights(o), (eights(o) + full - 1) // full * full, clear, 0)
-    low = (ids_ref[...] & 7).astype(F32).T
+        lax.fori_loop(eights(k), (eights(k) + full - 1) // full * full, clear, 0)
     width = BUNCH * 8
     lane = lax.broadcasted_iota(jnp.int32, (BUNCH, width), 1).astype(F32)
     slot = lax.broadcasted_iota(jnp.int32, (BUNCH, 1), 0)
-    for o in range(owners):
-        eight = buf.at[pl.ds(o * CAP, ROW8)]
-
-        def wait(j, _, o=o, eight=eight):
-            pltpu.make_async_copy(eight, eight, sems.at[o]).wait()
+    for k in range(owners):
+        o = who(k)
+        eight = buf.at[pl.ds(k * CAP, ROW8)]
+        low = jnp.broadcast_to((ids_ref[pl.ds(o, 1), :] & 7).astype(F32), (8, CAP)).T[:, :1]
+
+        def wait(j, _, k=k, eight=eight):
+            pltpu.make_async_copy(eight, eight, sems.at[k]).wait()
             return 0
 
-        lax.fori_loop(0, eights(o), wait, 0)
+        lax.fori_loop(0, eights(k), wait, 0)
         for b in range(CAP // BUNCH):
-            dst = slice(o * CAP + b * BUNCH, o * CAP + (b + 1) * BUNCH)
-            want = (8 * slot).astype(F32) + low[b * BUNCH : (b + 1) * BUNCH, o : o + 1]
+            want = (8 * slot).astype(F32) + low[b * BUNCH : (b + 1) * BUNCH]
             pick = (lane == want).astype(F32).astype(BF)
-            got = nn(pick, buf[dst].reshape(width, D))
-            out_ref[dst, :] = jnp.where(slot + b * BUNCH < count_ref[o], got, 0.0).astype(BF)
-
-
-def gather_call(rows, count, groups):
+            at = k * CAP + b * BUNCH
+            got = nn(pick, buf[at : at + BUNCH].reshape(width, D))
+            got = jnp.where(slot + b * BUNCH < count_ref[o], got, 0.0).astype(BF)
+            if outs > 1:
+                out_refs[k][b * BUNCH : (b + 1) * BUNCH, :] = got
+            else:
+                out_refs[0][at : at + BUNCH, :] = got
+
+
+def gather_call(rows, count, groups, outs):
     owners = rows.shape[0]
+    shape = jax.ShapeDtypeStruct((owners // outs * CAP, D), BF)
     return pl.pallas_call(
-        functools.partial(gather_kernel, owners),
-        out_shape=jax.ShapeDtypeStruct((owners * CAP, D), BF),
+        functools.partial(gather_kernel, owners, outs),
+        out_shape=[shape] * outs,
         in_specs=[SM, SM, VM, pl.BlockSpec(memory_space=pltpu.HBM)],
-        out_specs=VM,
+        out_specs=[VM] * outs,
         scratch_shapes=[pltpu.VMEM((owners * CAP, 8, D), BF), pltpu.SemaphoreType.DMA((owners,))],
         compiler_params=pltpu.CompilerParams(vmem_limit_bytes=56 * 1024 * 1024),
         cost_estimate=cost(7),
-        name="gather",
     )(rows, count, rows, groups)
 
 
-def place_kernel(at_ref, got_ref, own_ref):
-    rows, slots = own_ref.shape[0], got_ref.shape[0]
+def place_kernel(at_ref, *refs):
+    pieces, own_ref = refs[:-1], refs[-1]
+    rows = own_ref.shape[0]
     at = jnp.broadcast_to(at_ref[...].astype(F32), (8, rows)).T[:, :1]
-    slot = lax.broadcasted_iota(jnp.int32, (rows, slots), 1).astype(F32)
-    own_ref[...] = nn((slot == at).astype(F32).astype(BF), got_ref[...]).astype(BF)
-
-
-def place_call(at, got):
+    lane = lax.broadcasted_iota(jnp.int32, (rows, 2 * CAP), 1).astype(F32)
+    own = None
+    for j in range(len(pieces) // 2):
+        got = jnp.concatenate([pieces[2 * j][...], pieces[2 * j + 1][...]], axis=0)
+        part = nn((lane + 2.0 * CAP * j == at).astype(F32).astype(BF), got)
+        own = part if own is None else own + part
+    own_ref[...] = own.astype(BF)
+
+
+def place_call(at, pieces):
     return pl.pallas_call(
         place_kernel,
         out_shape=pltpu.VMEM((at.shape[1], D), BF),
-        in_specs=[VM, VM],
+        in_specs=[VM] * (1 + len(pieces)),
         out_specs=VM,
         compiler_params=PARAMS,
         cost_estimate=cost(1.5),
         name="place",
-    )(at, got)
+    )(at, *pieces)
 
 
 def project(first, side, sc_ref, pieces, w_ref, k_ref, v_ref, q_ref, g_ref, x_ref, n_scr, nq_scr):
@@ -307,6 +325,7 @@
 
 CTX = ("xh", "xl", "yh", "co")
 FLIP = [(0, 1), (1, 0)]
+EARLY, LATE = (7, 6, 5), (4, 2, 3, 1)
 
 
 def layer(item_ids, lengths, table, w_in, w_out):
@@ -339,19 +358,38 @@
         slot = lax.broadcasted_iota(jnp.int32, (owners, CAP, 2 * BLK), 1)
         rows = jnp.sum(jnp.where(rank[:, None, :] == slot, local[:, None, :], 0), axis=2)
         count = jnp.sum(here.astype(jnp.int32), axis=1)
-        picked = gather_call(rows, count, groups).reshape(owners, CAP, D)
-        return lax.all_to_all(picked, "dp", 0, 0, tiled=True).reshape(owners * CAP, D)
-
-    def place(c, got):
+        if c == 0:
+            picked = gather_call(rows, count, groups, 1)[0].reshape(owners, CAP, D)
+            return lax.all_to_all(picked, "dp", 0, 0, tiled=True).reshape(owners * CAP, D)
+        picked = gather_call(rows, count, groups, owners)
+        return picked
+
+    def swap(picked, k):
+        return lax.ppermute(picked[k], "dp", [(i, i ^ k) for i in range(owners)])
+
+    def places(c):
         own_ids = mine[2 * c : 2 * c + 2].reshape(2 * BLK)
         owner = own_ids // owned
         member = owner[None, :] == lax.broadcasted_iota(jnp.int32, (owners, 2 * BLK), 0)
-        at = jnp.sum(jnp.where(member, ranks(member), 0), axis=0) + owner * CAP
-        return in_vmem(place_call(at[None], got))
+        rank = jnp.sum(jnp.where(member, ranks(member), 0), axis=0)
+        return rank + (owner if c == 0 else owner ^ me) * CAP
+
+    def place(c, got):
+        at = places(c)
+        if c:
+            return in_vmem(place_call(at[None], got))
+        pick = (at[:, None] == lax.broadcasted_iota(jnp.int32, (2 * BLK, owners * CAP), 1)).astype(BF)
+        return nn(pick, got).astype(BF)
 
     past, first = [], None
     for c in range(2):
         got = fetch(c)
+        if c:
+            early = [swap(got, k) for k in EARLY]
+            late = [swap(got, k) for k in LATE]
+            received = dict(zip(EARLY + LATE, early + late))
+            got = [got[0]] + [received[k] for k in range(1, owners)]
+            got = [in_vmem(a) for a in got]
         own = place(c, got)
         far = lax.ppermute(own, "xl", FLIP)
         near = lax.ppermute(own, "co", FLIP)

time: 144 us -> 146 us (1.014)
  waiting for transfers between devices: 32.8 us -> 23.7 us
  local copies, waits for them, and re-layouts: 2.38 us -> 8 us
  starting transfers between devices: 24.6 us -> 29.9 us
  Pallas kernels: 55.4 us -> 52.2 us
  matrix products: 1.04 us -> 3.97 us
    all_to_all x2 -> x1, waiting for transfers between devices: 12.3 us -> 0.01 us  [fetch(): lax.all_to_all(picked, 'dp', 0, 0, tiled=True).reshape(owners * CAP, D)]
    ppermute x0 -> x7, starting transfers between devices: none -> 11.8 us  [swap(): return lax.ppermute(picked[k], 'dp', [(i, i ^ k) for i in range(owners)])]
    unnamed x14 -> x33, local copies, waits for them, and re-layouts: 1.02 us -> 6.63 us
    all_to_all x2 -> x1, starting transfers between devices: 11 us -> 6.32 us  [fetch(): lax.all_to_all(picked, 'dp', 0, 0, tiled=True).reshape(owners * CAP, D)]
    pallas_call x2 -> x1, Pallas kernels: 4.04 us -> 1.01 us  [place_call(): pl.pallas_call(place_kernel, out_shape=pltpu.VMEM((at.shape[1], D), BF),...]
    dot_general x4 -> x5, matrix products: 1.04 us -> 3.97 us  [nn(): return jnp.dot(a, b, preferred_element_type=F32)]
    ppermute x0 -> x7, waiting for transfers between devices: none -> 2.36 us  [swap(): return lax.ppermute(picked[k], 'dp', [(i, i ^ k) for i in range(owners)])]
    ppermute x2, starting transfers between devices: 2.01 us -> 0.09 us  [layer(): far = lax.ppermute(own, 'xl', FLIP)]
  transfers between devices with their start and end apart: 9 -> 15, of which waited for: 4 -> 4; matrix products, arithmetic and copies ran while one was open for 2% -> 4% of each run, Pallas kernels for 26% -> 23%
where the time goes in v5:
time: 146 us; the launch traced here: 143 us
  Pallas kernels  52.2 us (36%)
  starting transfers between devices  29.9 us (20%)
  waiting for transfers between devices  23.7 us (16%)
  blocking collectives  20.6 us (14%)
  local copies, waits for them, and re-layouts  8 us (5%)
  other arithmetic  4.11 us (3%)
  matrix products  3.97 us (3%)
    pallas_call x2, Pallas kernels, far_call(): pl.pallas_call(functools.partial(far_kernel, chunk), out_shape=shapes, in...  21 us
    all_to_all x1, blocking collectives, layer(): lax.all_to_all(done[0].reshape(16, PART, D), ('xh', 'yh', 'xl', 'co'), 0,...  20.6 us
    pallas_call x2, Pallas kernels, gather_call(): pl.pallas_call(functools.partial(gather_kernel, owners, outs), out_shape=...  15.2 us
    pallas_call x2, Pallas kernels, near_call(): pl.pallas_call(functools.partial(near_kernel, chunk), out_shape=[pltpu.VM...  15.1 us
    ppermute x2, waiting for transfers between devices, layer(): far = lax.ppermute(own, 'xl', FLIP)  12.6 us
    ppermute x7, starting transfers between devices, swap(): return lax.ppermute(picked[k], 'dp', [(i, i ^ k) for i in range(owners)])  11.8 us
    all_to_all x1, starting transfers between devices, layer(): lax.all_to_all(send, ('dp', 'xh', 'yh'), 0, 0, tiled=True)  11 us
    all_to_all x1, waiting for transfers between devices, layer(): lax.all_to_all(send, ('dp', 'xh', 'yh'), 0, 0, tiled=True)  8.74 us
  transfers between devices with their start and end apart: 15, of which 4 were waited for; matrix products, arithmetic and copies ran while one was open for 4% of the time, Pallas kernels for 23%

profile of v5, /device:TPU:8, one launch (start us, length us, event | category | flops | bytes accessed | tf_op | source)
XLA Modules:
  0.0 142.8 jit_solution(3894219664862689363)
XLA Ops:
  1.4 11.0 %all-to-all-start = ((s32[32,1,256]{2,1,0:T(1,128)}), s32[32,1,256]{2,1,0:T(1,128)S(1)}, u32[]{:S(2)}, u32[]{:S(2)}) async-start(s32[32,1,256]{2,1,0:T(1,128)} %broadcast_in_dim.77), calls=%async_computation | async-start | bytes 65536 | tf_op jit(solution)/shard_map/all_to_all | solution.py:340
  12.4 8.7 %all-to-all-done = s32[32,1,256]{2,1,0:T(1,128)S(1)} async-done(((s32[32,1,256]{2,1,0:T(1,128)}), s32[32,1,256]{2,1,0:T(1,128)S(1)}, u32[]{:S(2)}, u32[]{:S(2)}) %all-to-all-start) | async-done | bytes 32800 | tf_op jit(solution)/shard_map/all_to_all | solution.py:340
  21.3 1.0 fusion.31
  23.4 6.9 %shard_map.55 = bf16[1024,512]{1,0:T(8,128)(2,1)} custom-call(s32[8,128]{1,0:T(8,128)} %select_reduce_fusion.1.rows_ref.ids_ref, s32[8]{0:T(128)} %get-tuple-element.52.count_ref, s32[8,128]{1,0:T(8,128)} %select_reduce_fusion.1.rows_ref.ids_ref, bf16[2048,8,512]{2,1,0:T(8,128)(2,1)} %bitcast.23), custom_call_target="tpu_custom_call" | custom-call | flops 28000000 | tf_op jit(solution)/shard_map/pallas_call | solution.py:100
  30.3 6.3 %all-to-all-start.1 = ((bf16[8,128,512]{2,1,0:T(8,128)(2,1)}), bf16[8,128,512]{2,1,0:T(8,128)(2,1)S(1)}, u32[]{:S(2)}, u32[]{:S(2)}) async-start(bf16[8,128,512]{2,1,0:T(8,128)(2,1)} %bitcast.25), calls=%async_computation.1 | async-start | bytes 2097152 | tf_op jit(solution)/shard_map/all_to_all | solution.py:363
  37.8 8.3 %shard_map.58 = (bf16[128,512]{1,0:T(8,128)(2,1)}, bf16[128,512]{1,0:T(8,128)(2,1)}, bf16[128,512]{1,0:T(8,128)(2,1)}, bf16[128,512]{1,0:T(8,128)(2,1)}, bf16[12...) custom-call(s32[8,128]{1,0:T(8,128)} %select_reduce_fusion.rows_ref.ids_ref, ...), custom_call_target="tpu_custom_call" | custom-call | flops 28000000 | tf_op jit(solution)/shard_map/pallas_call | solution.py:100
  46.1 2.5 %collective-permute-start.4 = (bf16[128,512]{1,0:T(8,128)(2,1)}, bf16[128,512]{1,0:T(8,128)(2,1)S(1)}, u32[]{:S(2)}, u32[]{:S(2)}) collective-permute-start(bf16[128,512]{1,0:T(8,128)(2,1)} %get-tuple-element.38), channel_id=1, source_target_pairs={{0,32},{16,48},{32,0},{48,16},{64,96},{80,112},{96,64},{112,80},{1... | collective-permute-start | bytes 393224 | tf_op jit(solution)/shard_map/ppermute | solution.py:368
  48.6 2.2 %collective-permute-start.5 = (bf16[128,512]{1,0:T(8,128)(2,1)}, bf16[128,512]{1,0:T(8,128)(2,1)S(1)}, u32[]{:S(2)}, u32[]{:S(2)}) collective-permute-start(bf16[128,512]{1,0:T(8,128)(2,1)} %get-tuple-element.39), channel_id=1, source_target_pairs={{0,48},{16,32},{32,16},{48,0},{64,112},{80,96},{96,80},{112,64},{1... | collective-permute-start | bytes 393224 | tf_op jit(solution)/shard_map/ppermute | solution.py:368
  51.8 1.0 copy-done.9
  52.7 2.9 %fusion.1.refs_0_ = bf16[512,512]{1,0:T(8,128)(2,1)} fusion(bf16[1024,512]{1,0:T(8,128)(2,1)} %bitcast.27, s32[512]{0:T(512)S(1)} %multiply_add_fusion.1), kind=kOutput, calls=%fused_computation.6 | convolution fusion | flops 537657344 | bytes 1574912 | tf_op jit(solution)/shard_map/dot_general | solution.py:41
  55.7 3.5 %collective-permute-start.8 = (bf16[128,512]{1,0:T(8,128)(2,1)S(1)}, bf16[128,512]{1,0:T(8,128)(2,1)S(1)}, u32[]{:S(2)}, u32[]{:S(2)}) collective-permute-start(bf16[128,512]{1,0:T(8,128)(2,1)S(1)} %copy-done.11), channel_id=1, source_target_pairs={{0,96},{16,112},{32,64},{48,80},{64,32},{80,48},{96,0},{112,16},{1... | collective-permute-start | bytes 393224 | tf_op jit(solution)/shard_map/ppermute | solution.py:368
  59.2 3.2 %collective-permute-start.9 = (bf16[128,512]{1,0:T(8,128)(2,1)S(1)}, bf16[128,512]{1,0:T(8,128)(2,1)S(1)}, u32[]{:S(2)}, u32[]{:S(2)}) collective-permute-start(bf16[128,512]{1,0:T(8,128)(2,1)S(1)} %copy-done.10), channel_id=1, source_target_pairs={{0,112},{16,96},{32,80},{48,64},{64,48},{80,32},{96,16},{112,0},{1... | collective-permute-start | bytes 393224 | tf_op jit(solution)/shard_map/ppermute | solution.py:368
  64.4 2.3 %collective-permute-done.9.refs_7_ = bf16[128,512]{1,0:T(8,128)(2,1)S(1)} collective-permute-done((bf16[128,512]{1,0:T(8,128)(2,1)S(1)}, bf16[128,512]{1,0:T(8,128)(2,1)S(1)}, u32[]{:S(2)}, u32[]{:S(2)}) %collective-permute-start.9) | collective-permute-done | bytes 131104 | tf_op jit(solution)/shard_map/ppermute | solution.py:368
  66.7 0.9 copy-done.4
  67.6 0.9 copy-done.6
  69.5 1.0 place.1.refs_4_
  70.7 6.1 %collective-permute-done.1.refs_0_ = bf16[512,512]{1,0:T(8,128)(2,1)} collective-permute-done((bf16[512,512]{1,0:T(8,128)(2,1)}, bf16[512,512]{1,0:T(8,128)(2,1)}, u32[]{:S(2)}, u32[]{:S(2)}) %collective-permute-start.1) | collective-permute-done | bytes 524320 | tf_op jit(solution)/shard_map/ppermute | solution.py:394
  77.3 6.5 %collective-permute-done.10.refs_4_ = bf16[512,512]{1,0:T(8,128)(2,1)} collective-permute-done((bf16[512,512]{1,0:T(8,128)(2,1)S(1)}, bf16[512,512]{1,0:T(8,128)(2,1)}, u32[]{:S(2)}, u32[]{:S(2)}) %collective-permute-start.10) | collective-permute-done | bytes 524320 | tf_op jit(solution)/shard_map/ppermute | solution.py:394
  85.1 6.1 %shard_map.56 = (bf16[1024,512]{1,0:T(8,128)(2,1)S(1)}, bf16[512,1024]{1,0:T(8,128)(2,1)S(1)}, bf16[512,256]{1,0:T(8,128)(2,1)S(1)}, bf16[512,256]{1,0:T(8,128)(...) custom-call(s32[8]{0:T(128)S(1)} %compare_select_fusion.8.sc_ref, bf16[512,512]{1,0:T(8,128)(2,1)} %fusion.1.refs_0_, ...), custom_call_target="tpu_custom_call" | custom-call | flops 24000000 | tf_op jit(solution)/shard_map/pallas_call | solution.py:280
  91.3 9.0 %shard_map.57 = (bf16[512,512]{1,0:T(8,128)(2,1)S(1)}, bf16[1024,512]{1,0:T(8,128)(2,1)S(1)}, bf16[512,1024]{1,0:T(8,128)(2,1)S(1)}) custom-call(s32[8]{0:T(128)S(1)} %compare_select_fusion.8.sc_ref, bf16[512,512]{1,0:T(8,128)(2,1)} %collective-permute-done.1.refs_0_, bf16[512,512]{1,0:T(8,128)(2,1)} %collective-permute-done.2.refs_1_, ...), custom_call_target="tpu_custom_call" | custom-call | flops 36000000 | tf_op jit(solution)/shard_map/pallas_call | solution.py:312
  100.3 8.9 %shard_map.59 = (bf16[1024,512]{1,0:T(8,128)(2,1)S(1)}, bf16[512,1024]{1,0:T(8,128)(2,1)S(1)}, bf16[512,256]{1,0:T(8,128)(2,1)S(1)}, bf16[512,256]{1,0:T(8,128)(...) custom-call(s32[8]{0:T(128)S(1)} %compare_select_fusion.8.sc_ref, ...), custom_call_target="tpu_custom_call" | custom-call | flops 48000000 | tf_op jit(solution)/shard_map/pallas_call | solution.py:280
  109.3 11.9 %shard_map.60 = bf16[1024,512]{1,0:T(8,128)(2,1)S(1)} custom-call(s32[8]{0:T(128)S(1)} %compare_select_fusion.8.sc_ref, bf16[1024,512]{1,0:T(8,128)(2,1)S(1)} %get-tuple-element.28.refs_4_.refs_0_, bf16[512,1024]{1,0:T(8,128)(2,1)S(1)} %get-tuple-element.29.refs_5_.refs_1_, bf16[1024,512]{1,0:T(8,128)(2,1)S(1)} %get-tuple-element.34.refs_2_, ...), custom_call_target="tpu_custom_call" | custom-call | flops 56000000 | tf_op jit(solution)/shard_map/pallas_call | solution.py:312
  121.2 20.6 %all_to_all.15 = bf16[16,64,512]{2,1,0:T(8,128)(2,1)S(1)} all-to-all(bf16[16,64,512]{2,1,0:T(8,128)(2,1)S(1)} %bitcast.22), channel_id=1, replica_groups=mesh['dp'=8,'xh'=2,'xl'=2,'yh'=2,'co'=2] {'xh','yh','xl','co'}, dimensions={0} | all-to-all | bytes 2097152 | tf_op jit(solution)/shard_map/all_to_all | solution.py:404
  141.8 1.0 copy.13
  (65 shorter events, 9.6 us)
Async XLA Ops:
  1.4 19.8 %all-to-all-start = ((s32[32,1,256]{2,1,0:T(1,128)}), s32[32,1,256]{2,1,0:T(1,128)S(1)}, u32[]{:S(2)}, u32[]{:S(2)}) async-start(s32[32,1,256]{2,1,0:T(1,128)} %broadcast_in_dim.77), calls=%async_computation | async-start | bytes 65536 | tf_op jit(solution)/shard_map/all_to_all | solution.py:340
  30.3 21.4 %all-to-all-start.1 = ((bf16[8,128,512]{2,1,0:T(8,128)(2,1)}), bf16[8,128,512]{2,1,0:T(8,128)(2,1)S(1)}, u32[]{:S(2)}, u32[]{:S(2)}) async-start(bf16[8,128,512]{2,1,0:T(8,128)(2,1)} %bitcast.25), calls=%async_computation.1 | async-start | bytes 2097152 | tf_op jit(solution)/shard_map/all_to_all | solution.py:363
  46.0 9.7 %collective-permute-start.3 = (bf16[128,512]{1,0:T(8,128)(2,1)}, bf16[128,512]{1,0:T(8,128)(2,1)S(1)}, u32[]{:S(2)}, u32[]{:S(2)}) collective-permute-start(bf16[128,512]{1,0:T(8,128)(2,1)} %get-tuple-element.37), channel_id=1, source_target_pairs={{0,16},{16,0},{32,48},{48,32},{64,80},{80,64},{96,112},{112,96},{1... | collective-permute-start | bytes 393224 | tf_op jit(solution)/shard_map/ppermute | solution.py:368
  46.1 13.1 %collective-permute-start.4 = (bf16[128,512]{1,0:T(8,128)(2,1)}, bf16[128,512]{1,0:T(8,128)(2,1)S(1)}, u32[]{:S(2)}, u32[]{:S(2)}) collective-permute-start(bf16[128,512]{1,0:T(8,128)(2,1)} %get-tuple-element.38), channel_id=1, source_target_pairs={{0,32},{16,48},{32,0},{48,16},{64,96},{80,112},{96,64},{112,80},{1... | collective-permute-start | bytes 393224 | tf_op jit(solution)/shard_map/ppermute | solution.py:368
  48.6 13.8 %collective-permute-start.5 = (bf16[128,512]{1,0:T(8,128)(2,1)}, bf16[128,512]{1,0:T(8,128)(2,1)S(1)}, u32[]{:S(2)}, u32[]{:S(2)}) collective-permute-start(bf16[128,512]{1,0:T(8,128)(2,1)} %get-tuple-element.39), channel_id=1, source_target_pairs={{0,48},{16,32},{32,16},{48,0},{64,112},{80,96},{96,80},{112,64},{1... | collective-permute-start | bytes 393224 | tf_op jit(solution)/shard_map/ppermute | solution.py:368
  50.8 12.3 %collective-permute-start.6 = (bf16[128,512]{1,0:T(8,128)(2,1)}, bf16[128,512]{1,0:T(8,128)(2,1)S(1)}, u32[]{:S(2)}, u32[]{:S(2)}) collective-permute-start(bf16[128,512]{1,0:T(8,128)(2,1)} %get-tuple-element.40), channel_id=1, source_target_pairs={{0,64},{16,80},{32,96},{48,112},{64,0},{80,16},{96,32},{112,48},{1... | collective-permute-start | bytes 393224 | tf_op jit(solution)/shard_map/ppermute | solution.py:368
  50.9 12.9 %collective-permute-start.7 = (bf16[128,512]{1,0:T(8,128)(2,1)}, bf16[128,512]{1,0:T(8,128)(2,1)S(1)}, u32[]{:S(2)}, u32[]{:S(2)}) collective-permute-start(bf16[128,512]{1,0:T(8,128)(2,1)} %get-tuple-element.41), channel_id=1, source_target_pairs={{0,80},{16,64},{32,112},{48,96},{64,16},{80,0},{96,48},{112,32},{1... | collective-permute-start | bytes 393224 | tf_op jit(solution)/shard_map/ppermute | solution.py:368
  51.4 4.2 %copy-start.11 = (bf16[128,512]{1,0:T(8,128)(2,1)S(1)}, bf16[128,512]{1,0:T(8,128)(2,1)}, u32[]{:S(2)}) copy-start(bf16[128,512]{1,0:T(8,128)(2,1)} %get-tuple-element.42) | copy-start | bytes 393220
  51.4 7.7 %copy-start.10 = (bf16[128,512]{1,0:T(8,128)(2,1)S(1)}, bf16[128,512]{1,0:T(8,128)(2,1)}, u32[]{:S(2)}) copy-start(bf16[128,512]{1,0:T(8,128)(2,1)} %get-tuple-element.43) | copy-start | bytes 393220
  51.4 15.3 %copy-start.2 = (bf16[128,512]{1,0:T(8,128)(2,1)S(1)}, bf16[128,512]{1,0:T(8,128)(2,1)}, u32[]{:S(2)}) copy-start(bf16[128,512]{1,0:T(8,128)(2,1)} %get-tuple-element.36.refs_0_) | copy-start | bytes 393220
  51.8 1.0 copy-start.9
  52.7 31.1 %copy-start.12 = (s32[4]{0:T(128)S(1)}, s32[4]{0:T(128)}, u32[]{:S(2)}) copy-start(s32[4]{0:T(128)} %param.6) | copy-start | bytes 52
  52.7 32.4 %copy-start = (bf16[512,2048]{1,0:T(8,128)(2,1)S(1)}, bf16[512,2048]{1,0:T(8,128)(2,1)}, u32[]{:S(2)}) copy-start(bf16[512,2048]{1,0:T(8,128)(2,1)} %refs_6_.3) | copy-start | bytes 6291460
  55.7 8.7 %collective-permute-start.8 = (bf16[128,512]{1,0:T(8,128)(2,1)S(1)}, bf16[128,512]{1,0:T(8,128)(2,1)S(1)}, u32[]{:S(2)}, u32[]{:S(2)}) collective-permute-start(bf16[128,512]{1,0:T(8,128)(2,1)S(1)} %copy-done.11), channel_id=1, source_target_pairs={{0,96},{16,112},{32,64},{48,80},{64,32},{80,48},{96,0},{112,16},{1... | collective-permute-start | bytes 393224 | tf_op jit(solution)/shard_map/ppermute | solution.py:368
  59.2 7.5 %collective-permute-start.9 = (bf16[128,512]{1,0:T(8,128)(2,1)S(1)}, bf16[128,512]{1,0:T(8,128)(2,1)S(1)}, u32[]{:S(2)}, u32[]{:S(2)}) collective-permute-start(bf16[128,512]{1,0:T(8,128)(2,1)S(1)} %copy-done.10), channel_id=1, source_target_pairs={{0,112},{16,96},{32,80},{48,64},{64,48},{80,32},{96,16},{112,0},{1... | collective-permute-start | bytes 393224 | tf_op jit(solution)/shard_map/ppermute | solution.py:368
  63.1 13.8 %collective-permute-start.1 = (bf16[512,512]{1,0:T(8,128)(2,1)}, bf16[512,512]{1,0:T(8,128)(2,1)}, u32[]{:S(2)}, u32[]{:S(2)}) collective-permute-start(bf16[512,512]{1,0:T(8,128)(2,1)} %fusion.1.refs_0_), channel_id=1, source_target_pairs={{0,4},{4,0},{1,5},{5,1},{2,6},{6,2},{3,7},{7,3},{8,12},{12,8},{9,1... | collective-permute-start | bytes 1572872 | tf_op jit(solution)/shard_map/ppermute | solution.py:394
  66.7 0.9 copy-start.4
  68.5 0.9 copy-start.8
  69.4 21.8 %copy-start.1 = (bf16[512,512]{1,0:T(8,128)(2,1)S(1)}, bf16[512,512]{1,0:T(8,128)(2,1)}, u32[]{:S(2)}) copy-start(bf16[512,512]{1,0:T(8,128)(2,1)} %refs_7_.1) | copy-start | bytes 1572868
  70.5 13.3 %collective-permute-start.10 = (bf16[512,512]{1,0:T(8,128)(2,1)S(1)}, bf16[512,512]{1,0:T(8,128)(2,1)}, u32[]{:S(2)}, u32[]{:S(2)}) collective-permute-start(bf16[512,512]{1,0:T(8,128)(2,1)S(1)} %place.1.refs_4_), channel_id=1, source_target_pairs={{0,4},{4,0},{1,5},{5,1},{2,6},{6,2},{3,7},{7,3},{8,12},{12,8},{9,1... | collective-permute-start | bytes 1572872 | tf_op jit(solution)/shard_map/ppermute | solution.py:394
  70.6 14.5 %collective-permute-start = (bf16[512,512]{1,0:T(8,128)(2,1)}, bf16[512,512]{1,0:T(8,128)(2,1)}, u32[]{:S(2)}, u32[]{:S(2)}) collective-permute-start(bf16[512,512]{1,0:T(8,128)(2,1)} %fusion.1.refs_0_), channel_id=1, source_target_pairs={{0,1},{1,0},{2,3},{3,2},{4,5},{5,4},{6,7},{7,6},{8,9},{9,8},{10,11... | collective-permute-start | bytes 1572872 | tf_op jit(solution)/shard_map/ppermute | solution.py:395
  76.8 14.4 %collective-permute-start.2 = (bf16[512,512]{1,0:T(8,128)(2,1)}, bf16[512,512]{1,0:T(8,128)(2,1)}, u32[]{:S(2)}, u32[]{:S(2)}) collective-permute-start(bf16[512,512]{1,0:T(8,128)(2,1)} %collective-permute-done.1.refs_0_), channel_id=1, source_target_pairs={{0,1},{1,0},{2,3},{3,2},{4,5},{5,4},{6,7},{7,6},{8,9},{9,8},{10,11... | collective-permute-start | bytes 1572872 | tf_op jit(solution)/shard_map/ppermute | solution.py:396
  76.8 23.5 %collective-permute-start.12 = (bf16[512,512]{1,0:T(8,128)(2,1)S(1)}, bf16[512,512]{1,0:T(8,128)(2,1)}, u32[]{:S(2)}, u32[]{:S(2)}) collective-permute-start(bf16[512,512]{1,0:T(8,128)(2,1)S(1)} %place.1.refs_4_), channel_id=1, source_target_pairs={{0,1},{1,0},{2,3},{3,2},{4,5},{5,4},{6,7},{7,6},{8,9},{9,8},{10,11... | collective-permute-start | bytes 1572872 | tf_op jit(solution)/shard_map/ppermute | solution.py:395
  83.8 25.5 %collective-permute-start.11 = (bf16[512,512]{1,0:T(8,128)(2,1)}, bf16[512,512]{1,0:T(8,128)(2,1)}, u32[]{:S(2)}, u32[]{:S(2)}) collective-permute-start(bf16[512,512]{1,0:T(8,128)(2,1)} %collective-permute-done.10.refs_4_), channel_id=1, source_target_pairs={{0,1},{1,0},{2,3},{3,2},{4,5},{5,4},{6,7},{7,6},{8,9},{9,8},{10,11... | collective-permute-start | bytes 1572872 | tf_op jit(solution)/shard_map/ppermute | solution.py:396
  (4 other events, 2.9 us)

commit v6 on v5

--- a/solution.py
+++ b/solution.py
@@ -73,15 +73,20 @@
     lane = lax.broadcasted_iota(jnp.int32, (BUNCH, width), 1).astype(F32)
     slot = lax.broadcasted_iota(jnp.int32, (BUNCH, 1), 0)
     for k in range(owners):
-        o = who(k)
         eight = buf.at[pl.ds(k * CAP, ROW8)]
-        low = jnp.broadcast_to((ids_ref[pl.ds(o, 1), :] & 7).astype(F32), (8, CAP)).T[:, :1]
 
         def wait(j, _, k=k, eight=eight):
             pltpu.make_async_copy(eight, eight, sems.at[k]).wait()
             return 0
 
         lax.fori_loop(0, eights(k), wait, 0)
+    low8 = (ids_ref[...] & 7).astype(F32).T
+    for k in range(owners):
+        o = who(k)
+        if outs > 1:
+            low = jnp.broadcast_to((ids_ref[pl.ds(o, 1), :] & 7).astype(F32), (8, CAP)).T[:, :1]
+        else:
+            low = low8[:, k : k + 1]
         for b in range(CAP // BUNCH):
             want = (8 * slot).astype(F32) + low[b * BUNCH : (b + 1) * BUNCH]
             pick = (lane == want).astype(F32).astype(BF)
@@ -106,31 +111,6 @@
         compiler_params=pltpu.CompilerParams(vmem_limit_bytes=56 * 1024 * 1024),
         cost_estimate=cost(7),
     )(rows, count, rows, groups)
-
-
-def place_kernel(at_ref, *refs):
-    pieces, own_ref = refs[:-1], refs[-1]
-    rows = own_ref.shape[0]
-    at = jnp.broadcast_to(at_ref[...].astype(F32), (8, rows)).T[:, :1]
-    lane = lax.broadcasted_iota(jnp.int32, (rows, 2 * CAP), 1).astype(F32)
-    own = None
-    for j in range(len(pieces) // 2):
-        got = jnp.concatenate([pieces[2 * j][...], pieces[2 * j + 1][...]], axis=0)
-        part = nn((lane + 2.0 * CAP * j == at).astype(F32).astype(BF), got)
-        own = part if own is None else own + part
-    own_ref[...] = own.astype(BF)
-
-
-def place_call(at, pieces):
-    return pl.pallas_call(
-        place_kernel,
-        out_shape=pltpu.VMEM((at.shape[1], D), BF),
-        in_specs=[VM] * (1 + len(pieces)),
-        out_specs=VM,
-        compiler_params=PARAMS,
-        cost_estimate=cost(1.5),
-        name="place",
-    )(at, *pieces)
 
 
 def project(first, side, sc_ref, pieces, w_ref, k_ref, v_ref, q_ref, g_ref, x_ref, n_scr, nq_scr):
@@ -225,42 +205,31 @@
     lax.fori_loop(0, 4 // together, heads, 0)
 
 
-def near_kernel(chunk, sc_ref, *refs):
-    past = refs[: 4 * chunk]
-    p1, p2, w_ref, k_ref, v_ref, q_ref, g_ref, x_ref, o_ref, n_scr, nq_scr = refs[4 * chunk :]
-    project(2 * GRP * chunk, 0, sc_ref, (p1, p2), w_ref, k_ref, v_ref, q_ref, g_ref, x_ref, n_scr, nq_scr)
-    seen = [(past[2 * i], past[2 * i + 1], False) for i in range(2 * chunk)]
-    attend(sc_ref, [(q_ref, o_ref, seen + [(k_ref, v_ref, True)])], 2)
-
-
-def far_kernel(chunk, sc_ref, *refs):
-    past = refs[: 4 * chunk]
-    p1, p2, w_ref, wo_ref, kn, vn, qn, gn, xn, on = refs[4 * chunk : 4 * chunk + 10]
-    rest = refs[4 * chunk + 10 :]
-    if chunk:
-        first_ref, rest = rest[0], rest[1:]
-        out_ref, rest = rest[0], rest[1:]
-        kf, vf = rest[-2:]
-    else:
-        out_ref, kf, vf = rest[:3]
-        rest = rest[3:]
-    n_scr, nq_scr, qf, gf, xf, of, qx, kx, vx, ox = rest[:10]
-    project(2 * GRP * chunk, 1, sc_ref, (p1, p2), w_ref, kf, vf, qf, gf, xf, n_scr, nq_scr)
-    low = sc_ref[3] == 0
-
-    @pl.when(low)
-    def _():
-        qx[...], kx[...], vx[...] = qf[...], kn[...], vn[...]
-
-    @pl.when(jnp.logical_not(low))
-    def _():
-        qx[...], kx[...], vx[...] = qn[...], kf[...], vf[...]
-
-    seen = [(past[2 * i], past[2 * i + 1], False) for i in range(2 * chunk)]
-    attend(sc_ref, [(qf, of, seen + [(kf, vf, True)]), (qx, ox, [(kx, vx, False)])], 2)
-    if chunk:
-        out_ref[:512, :] = first_ref[...]
-    for side, (o_ref, g_ref, x_ref) in enumerate(((on, gn, xn), (of, gf, xf))):
+def near0_kernel(sc_ref, p1, p2, w_ref, *refs):
+    outs, held, (n_scr, nq_scr, sems) = refs[:6], refs[6:12], refs[12:]
+    k, v, q, g, x, o = held
+    copies = [pltpu.make_async_copy(src, dst, sems.at[i]) for i, (src, dst) in enumerate(zip(held, outs))]
+    project(0, 0, sc_ref, (p1, p2), w_ref, k, v, q, g, x, n_scr, nq_scr)
+    for c in copies[:5]:
+        c.start()
+    attend(sc_ref, [(q, o, [(k, v, True)])], 2)
+    copies[5].start()
+    for c in copies:
+        c.wait()
+
+
+def near1_kernel(sc_ref, p1, p2, w_ref, k_ref, v_ref, q_ref, g_ref, x_ref, o_ref, n_scr, nq_scr):
+    project(2 * GRP, 0, sc_ref, (p1, p2), w_ref, k_ref, v_ref, q_ref, g_ref, x_ref, n_scr, nq_scr)
+    attend(sc_ref, [(q_ref, o_ref, [(k_ref, v_ref, True)])], 2)
+
+
+def past_kernel(sc_ref, k0, v0, k1, v1, q_ref, before_ref, o_ref):
+    attend(sc_ref, [(q_ref, o_ref, [(k0, v0, False), (k1, v1, False)])], 2)
+    o_ref[...] = o_ref[...] + before_ref[...]
+
+
+def finish(chunk, sc_ref, wo_ref, ox, sides, out_ref):
+    for side, (o_ref, g_ref, x_ref) in enumerate(sides):
         o = o_ref[...] + jnp.where(sc_ref[3 + side] == 1, ox[...], 0.0)
         c = o - jnp.mean(o, axis=0, keepdims=True)
         var = jnp.mean(c * c, axis=0, keepdims=True)
@@ -272,52 +241,95 @@
             out_ref[pl.ds(at, 128), :] = out[128 * j : 128 * (j + 1)]
 
 
+def far_core(chunk, sc_ref, past, p1, p2, w_ref, wo_ref, kept, arrive, out_ref, kf, vf, scratch):
+    n_scr, nq_scr, qf, gf, xf, of, qx, kx, vx, ox = scratch
+    kn, vn, qn, gn, xn, on = kept
+    project(2 * GRP * chunk, 1, sc_ref, (p1, p2), w_ref, kf, vf, qf, gf, xf, n_scr, nq_scr)
+    for c in arrive:
+        c.wait()
+    low = sc_ref[3] == 0
+
+    @pl.when(low)
+    def _():
+        qx[...], kx[...], vx[...] = qf[...], kn[...], vn[...]
+
+    @pl.when(jnp.logical_not(low))
+    def _():
+        qx[...], kx[...], vx[...] = qn[...], kf[...], vf[...]
+
+    seen = [(past[2 * i], past[2 * i + 1], False) for i in range(2 * chunk)]
+    attend(sc_ref, [(qf, of, seen + [(kf, vf, True)]), (qx, ox, [(kx, vx, False)])], 2)
+    finish(chunk, sc_ref, wo_ref, ox, ((on, gn, xn), (of, gf, xf)), out_ref)
+
+
+def far0_kernel(sc_ref, p1, p2, w_ref, wo_ref, *refs):
+    sent, (out_ref, kn, vn, kf, vf), rest = refs[:6], refs[6:11], refs[11:]
+    kept = (kn, vn, *rest[:4])
+    sems = rest[-1]
+    arrive = [pltpu.make_async_copy(src, dst, sems.at[i]) for i, (src, dst) in enumerate(zip(sent, kept))]
+    for c in arrive:
+        c.start()
+    far_core(0, sc_ref, (), p1, p2, w_ref, wo_ref, kept, arrive, out_ref, kf, vf, rest[4:-1])
+
+
+def far1_kernel(sc_ref, *refs):
+    past, (p1, p2, w_ref, wo_ref), kept = refs[:4], refs[4:8], refs[8:14]
+    first_ref, out_ref = refs[14:16]
+    scratch, (kf, vf) = refs[16:26], refs[26:]
+    far_core(1, sc_ref, past, p1, p2, w_ref, wo_ref, kept, (), out_ref, kf, vf, scratch)
+    out_ref[:512, :] = first_ref[...]
+
+
 SIZES = [(GRP, D), (D, GRP), (D, 256), (D, 256), (256, D)]
-
-
-def near_call(chunk, sc, past, own, near, w_in):
-    inputs = [*past, own, near, w_in]
-    outs = pl.pallas_call(
-        functools.partial(near_kernel, chunk),
-        out_shape=[pltpu.VMEM(s, BF) for s in SIZES] + [pltpu.VMEM((D, 256), F32)],
-        in_specs=[SM] + [VM] * len(inputs),
-        out_specs=[VM] * 6,
-        scratch_shapes=[pltpu.VMEM((2, D, D), BF), pltpu.VMEM((256, D), BF)],
-        compiler_params=PARAMS,
-        cost_estimate=cost(6 + 6 * chunk),
-    )(sc, *inputs)
-    return outs
-
-
-def far_call(chunk, sc, past, far, diag, w_in, w_out, kept, first):
-    inputs = [*past, far, diag, w_in, w_out, *kept]
-    scratch = [
-        pltpu.VMEM((2, D, D), BF),
-        pltpu.VMEM((256, D), BF),
-        pltpu.VMEM((D, 256), BF),
-        pltpu.VMEM((D, 256), BF),
-        pltpu.VMEM((256, D), BF),
-        pltpu.VMEM((D, 256), F32),
-        pltpu.VMEM((D, 256), BF),
-        pltpu.VMEM((GRP, D), BF),
-        pltpu.VMEM((D, GRP), BF),
-        pltpu.VMEM((D, 256), F32),
-    ]
-    held = [pltpu.VMEM(s, BF) for s in SIZES[:2]]
-    if chunk:
-        inputs.append(first)
-        shapes, scratch = [jax.ShapeDtypeStruct((1024, D), BF)], scratch + held
-    else:
-        shapes = [pltpu.VMEM((512, D), BF)] + held
+HBM = pl.BlockSpec(memory_space=pltpu.HBM)
+SUMS = pltpu.VMEM((D, 256), F32)
+PROJECT = [pltpu.VMEM((2, D, D), BF), pltpu.VMEM((256, D), BF)]
+
+
+def held(some=slice(None)):
+    return [pltpu.VMEM(s, BF) for s in SIZES[some]]
+
+
+def call(kernel, us, inputs, in_specs, out_shape, out_specs, scratch):
     return pl.pallas_call(
-        functools.partial(far_kernel, chunk),
-        out_shape=shapes,
-        in_specs=[SM] + [VM] * len(inputs),
-        out_specs=[VM] * len(shapes),
+        kernel,
+        out_shape=out_shape,
+        in_specs=[SM] + in_specs,
+        out_specs=out_specs,
         scratch_shapes=scratch,
         compiler_params=PARAMS,
-        cost_estimate=cost(9 + 5 * chunk),
-    )(sc, *inputs)
+        cost_estimate=cost(us),
+    )(*inputs)
+
+
+def near0_call(sc, own, near, w_in):
+    shapes = [pltpu.HBM(s, BF) for s in SIZES] + [pltpu.HBM((D, 256), F32)]
+    scratch = held() + [SUMS] + PROJECT + [pltpu.SemaphoreType.DMA((6,))]
+    return call(near0_kernel, 6, (sc, own, near, w_in), [VM] * 3, shapes, [HBM] * 6, scratch)
+
+
+def near1_call(sc, own, near, w_in):
+    return call(near1_kernel, 5, (sc, own, near, w_in), [VM] * 3, held() + [SUMS], [VM] * 6, PROJECT)
+
+
+def past_call(sc, past, q, before):
+    return call(past_kernel, 5, (sc, *past, q, before), [VM] * 6, SUMS, VM, [])
+
+
+FAR = PROJECT + held(slice(2, 5)) + [SUMS, pltpu.VMEM((D, 256), BF)] + held(slice(0, 2)) + [SUMS]
+
+
+def far0_call(sc, far, diag, w_in, w_out, sent):
+    shapes = [pltpu.VMEM((512, D), BF)] + held(slice(0, 2)) * 2
+    scratch = held(slice(2, 5)) + [SUMS] + FAR + [pltpu.SemaphoreType.DMA((6,))]
+    inputs = (sc, far, diag, w_in, w_out, *sent)
+    return call(far0_kernel, 9, inputs, [VM] * 4 + [HBM] * 6, shapes, [VM] * 5, scratch)
+
+
+def far1_call(sc, past, far, diag, w_in, w_out, kept, first):
+    inputs = (sc, *past, far, diag, w_in, w_out, *kept, first)
+    shape = jax.ShapeDtypeStruct((1024, D), BF)
+    return call(far1_kernel, 11, inputs, [VM] * 15, shape, VM, FAR + held(slice(0, 2)))
 
 
 from jax.sharding import Mesh
@@ -325,7 +337,6 @@
 
 CTX = ("xh", "xl", "yh", "co")
 FLIP = [(0, 1), (1, 0)]
-EARLY, LATE = (7, 6, 5), (4, 2, 3, 1)
 
 
 def layer(item_ids, lengths, table, w_in, w_out):
@@ -358,51 +369,40 @@
         slot = lax.broadcasted_iota(jnp.int32, (owners, CAP, 2 * BLK), 1)
         rows = jnp.sum(jnp.where(rank[:, None, :] == slot, local[:, None, :], 0), axis=2)
         count = jnp.sum(here.astype(jnp.int32), axis=1)
-        if c == 0:
-            picked = gather_call(rows, count, groups, 1)[0].reshape(owners, CAP, D)
-            return lax.all_to_all(picked, "dp", 0, 0, tiled=True).reshape(owners * CAP, D)
-        picked = gather_call(rows, count, groups, owners)
-        return picked
-
-    def swap(picked, k):
-        return lax.ppermute(picked[k], "dp", [(i, i ^ k) for i in range(owners)])
-
-    def places(c):
+        picked = gather_call(rows, count, groups, 1)[0].reshape(owners, CAP, D)
+        return lax.all_to_all(picked, "dp", 0, 0, tiled=True).reshape(owners * CAP, D)
+
+    def place(c, got):
         own_ids = mine[2 * c : 2 * c + 2].reshape(2 * BLK)
         owner = own_ids // owned
         member = owner[None, :] == lax.broadcasted_iota(jnp.int32, (owners, 2 * BLK), 0)
-        rank = jnp.sum(jnp.where(member, ranks(member), 0), axis=0)
-        return rank + (owner if c == 0 else owner ^ me) * CAP
-
-    def place(c, got):
-        at = places(c)
-        if c:
-            return in_vmem(place_call(at[None], got))
+        at = jnp.sum(jnp.where(member, ranks(member), 0), axis=0) + owner * CAP
         pick = (at[:, None] == lax.broadcasted_iota(jnp.int32, (2 * BLK, owners * CAP), 1)).astype(BF)
         return nn(pick, got).astype(BF)
 
-    past, first = [], None
+    def vmem_all(arrays):
+        return [in_vmem(a) for a in arrays]
+
     for c in range(2):
         got = fetch(c)
-        if c:
-            early = [swap(got, k) for k in EARLY]
-            late = [swap(got, k) for k in LATE]
-            received = dict(zip(EARLY + LATE, early + late))
-            got = [got[0]] + [received[k] for k in range(1, owners)]
-            got = [in_vmem(a) for a in got]
         own = place(c, got)
         far = lax.ppermute(own, "xl", FLIP)
         near = lax.ppermute(own, "co", FLIP)
         diag = lax.ppermute(far, "co", FLIP)
-        pieces = [in_vmem(a) for a in (own, near, far, diag)]
-        kept = near_call(c, sc, past, *pieces[:2], w_in)
-        kept = [in_vmem(a) for a in kept]
-        done = far_call(c, sc, past, *pieces[2:], w_in, w_out, kept, first)
+        own, near, far, diag = vmem_all((own, near, far, diag))
         if c == 0:
-            first, k1, v1 = (in_vmem(a) for a in done)
-            past = [*kept[:2], k1, v1]
-    back = lax.all_to_all(done[0].reshape(16, PART, D), ("xh", "yh", "xl", "co"), 0, 0, tiled=True)
-    return back.reshape(4, BLK, D)
+            sent = near0_call(sc, own, near, w_in)
+            sent = [pltpu.with_memory_space_constraint(a, pltpu.HBM) for a in sent]
+            done = far0_call(sc, far, diag, w_in, w_out, sent)
+            first, *past = vmem_all(done)
+        else:
+            kept = near1_call(sc, own, near, w_in)
+            kept = vmem_all(kept)
+            total = past_call(sc, past, kept[2], kept[5])
+            kept[5] = in_vmem(total)
+            out = far1_call(sc, past, far, diag, w_in, w_out, kept, first)
+    back = lax.all_to_all(out.reshape(16, PART, D), ("xh", "yh", "xl", "co"), 0, 0, tiled=True)
+    return pltpu.with_memory_space_constraint(back.reshape(4, BLK, D), pltpu.HBM)
 
 
 def solution(mesh):

time: 146 us -> 147 us (level); the launches traced: 143 us -> 145 us
  waiting for transfers between devices: 23.7 us -> 33.9 us
  local copies, waits for them, and re-layouts: 8 us -> 2.37 us
  starting transfers between devices: 29.9 us -> 24.3 us
    all_to_all x1 -> x2, waiting for transfers between devices: 0.01 us -> 13.3 us  [fetch(): lax.all_to_all(picked, 'dp', 0, 0, tiled=True).reshape(owners * CAP, D)]
    ppermute x7 -> x0, starting transfers between devices: 11.8 us -> none  [swap(): return lax.ppermute(picked[k], 'dp', [(i, i ^ k) for i in range(owners)])]
    unnamed x33 -> x12, local copies, waits for them, and re-layouts: 6.63 us -> 1 us
    all_to_all x1 -> x2, starting transfers between devices: 6.32 us -> 10.6 us  [fetch(): lax.all_to_all(picked, 'dp', 0, 0, tiled=True).reshape(owners * CAP, D)]
    ppermute x7 -> x0, waiting for transfers between devices: 2.36 us -> none  [swap(): return lax.ppermute(picked[k], 'dp', [(i, i ^ k) for i in range(owners)])]
    ppermute x2, starting transfers between devices: 0.09 us -> 2.17 us  [layer(): far = lax.ppermute(own, 'xl', FLIP)]
    pallas_call x5, Pallas kernels: 37 us -> 38.5 us  [call(): pl.pallas_call(kernel, out_shape=out_shape, in_specs=[SM] + in_specs, out...]
    dot_general x5 -> x6, matrix products: 3.97 us -> 5.37 us  [nn(): return jnp.dot(a, b, preferred_element_type=F32)]
  transfers between devices with their start and end apart: 15 -> 9, of which waited for: 4 -> 4; matrix products, arithmetic and copies ran while one was open for 4% -> 5% of each run, Pallas kernels for 23% -> 24%
where the time goes in v6:
time: 147 us; the launch traced here: 145 us
  Pallas kernels  52.9 us (36%)
  waiting for transfers between devices  33.9 us (23%)
  starting transfers between devices  24.3 us (17%)
  blocking collectives  21.9 us (15%)
  matrix products  5.37 us (4%)
  other arithmetic  4.17 us (3%)
  local copies, waits for them, and re-layouts  2.37 us (2%)
    pallas_call x5, Pallas kernels, call(): pl.pallas_call(kernel, out_shape=out_shape, in_specs=[SM] + in_specs, out...  38.5 us
    all_to_all x1, blocking collectives, layer(): lax.all_to_all(out.reshape(16, PART, D), ('xh', 'yh', 'xl', 'co'), 0, 0,...  21.9 us
    pallas_call x2, Pallas kernels, gather_call(): pl.pallas_call(functools.partial(gather_kernel, owners, outs), out_shape=...  14.4 us
    all_to_all x2, waiting for transfers between devices, fetch(): lax.all_to_all(picked, 'dp', 0, 0, tiled=True).reshape(owners * CAP, D)  13.3 us
    ppermute x2, waiting for transfers between devices, layer(): far = lax.ppermute(own, 'xl', FLIP)  11.9 us
    all_to_all x1, starting transfers between devices, layer(): lax.all_to_all(send, ('dp', 'xh', 'yh'), 0, 0, tiled=True)  11 us
    all_to_all x2, starting transfers between devices, fetch(): lax.all_to_all(picked, 'dp', 0, 0, tiled=True).reshape(owners * CAP, D)  10.6 us
    all_to_all x1, waiting for transfers between devices, layer(): lax.all_to_all(send, ('dp', 'xh', 'yh'), 0, 0, tiled=True)  8.72 us
  transfers between devices with their start and end apart: 9, of which 4 were waited for; matrix products, arithmetic and copies ran while one was open for 5% of the time, Pallas kernels for 24%

profile of v6, /device:TPU:8, one launch (start us, length us, event | category | flops | bytes accessed | tf_op | source)
XLA Modules:
  0.0 145.2 jit_solution(13555694896069306926)
XLA Ops:
  1.4 11.0 %all-to-all-start = ((s32[32,1,256]{2,1,0:T(1,128)}), s32[32,1,256]{2,1,0:T(1,128)S(1)}, u32[]{:S(2)}, u32[]{:S(2)}) async-start(s32[32,1,256]{2,1,0:T(1,128)} %broadcast_in_dim.77), calls=%async_computation | async-start | bytes 65536 | tf_op jit(solution)/shard_map/all_to_all | solution.py:351
  12.4 8.7 %all-to-all-done = s32[32,1,256]{2,1,0:T(1,128)S(1)} async-done(((s32[32,1,256]{2,1,0:T(1,128)}), s32[32,1,256]{2,1,0:T(1,128)S(1)}, u32[]{:S(2)}, u32[]{:S(2)}) %all-to-all-start) | async-done | bytes 32800 | tf_op jit(solution)/shard_map/all_to_all | solution.py:351
  21.2 0.9 fusion.34
  22.4 0.9 select_reduce_fusion.1.rows_ref.ids_ref
  23.2 6.5 %shard_map.55 = bf16[1024,512]{1,0:T(8,128)(2,1)} custom-call(s32[8,128]{1,0:T(8,128)} %select_reduce_fusion.1.rows_ref.ids_ref, s32[8]{0:T(128)} %get-tuple-element.40.count_ref, s32[8,128]{1,0:T(8,128)} %select_reduce_fusion.1.rows_ref.ids_ref, bf16[2048,8,512]{2,1,0:T(8,128)(2,1)} %bitcast.22), custom_call_target="tpu_custom_call" | custom-call | flops 28000000 | tf_op jit(solution)/shard_map/pallas_call | solution.py:105
  29.8 5.9 %all-to-all-start.1 = ((bf16[8,128,512]{2,1,0:T(8,128)(2,1)}), bf16[8,128,512]{2,1,0:T(8,128)(2,1)S(1)}, u32[]{:S(2)}, u32[]{:S(2)}) async-start(bf16[8,128,512]{2,1,0:T(8,128)(2,1)} %bitcast.25), calls=%async_computation.1 | async-start | bytes 2097152 | tf_op jit(solution)/shard_map/all_to_all | solution.py:373
  36.0 0.9 select_reduce_fusion.rows_ref.ids_ref
  36.9 7.9 %shard_map.58 = bf16[1024,512]{1,0:T(8,128)(2,1)} custom-call(s32[8,128]{1,0:T(8,128)} %select_reduce_fusion.rows_ref.ids_ref, s32[8]{0:T(128)} %get-tuple-element.39.count_ref, s32[8,128]{1,0:T(8,128)} %select_reduce_fusion.rows_ref.ids_ref, bf16[2048,8,512]{2,1,0:T(8,128)(2,1)} %bitcast.23), custom_call_target="tpu_custom_call" | custom-call | flops 28000000 | tf_op jit(solution)/shard_map/pallas_call | solution.py:105
  44.8 2.9 %all-to-all-done.1 = bf16[8,128,512]{2,1,0:T(8,128)(2,1)S(1)} async-done(((bf16[8,128,512]{2,1,0:T(8,128)(2,1)}), bf16[8,128,512]{2,1,0:T(8,128)(2,1)S(1)}, u32[]{:S(2)}, u32[]{:S(2)}) %all-to-all-start.1) | async-done | bytes 1048608 | tf_op jit(solution)/shard_map/all_to_all | solution.py:373
  47.7 4.7 %all-to-all-start.2 = ((bf16[8,128,512]{2,1,0:T(8,128)(2,1)}), bf16[8,128,512]{2,1,0:T(8,128)(2,1)}, u32[]{:S(2)}, u32[]{:S(2)}) async-start(bf16[8,128,512]{2,1,0:T(8,128)(2,1)} %bitcast.24), calls=%async_computation.2 | async-start | bytes 2097152 | tf_op jit(solution)/shard_map/all_to_all | solution.py:373
  52.9 1.5 %fusion.3.p1 = bf16[512,512]{1,0:T(8,128)(2,1)} fusion(bf16[1024,512]{1,0:T(8,128)(2,1)S(1)} %bitcast.27, s32[512]{0:T(512)S(1)} %multiply_add_fusion.1), kind=kOutput, calls=%fused_computation.9 | convolution fusion | flops 537657344 | bytes 1574912 | tf_op jit(solution)/shard_map/dot_general | solution.py:41
  54.5 0.7 collective-permute-start
  55.2 10.4 %all-to-all-done.2 = bf16[8,128,512]{2,1,0:T(8,128)(2,1)} async-done(((bf16[8,128,512]{2,1,0:T(8,128)(2,1)}), bf16[8,128,512]{2,1,0:T(8,128)(2,1)}, u32[]{:S(2)}, u32[]{:S(2)}) %all-to-all-start.2) | async-done | bytes 1048608 | tf_op jit(solution)/shard_map/all_to_all | solution.py:373
  65.6 2.8 %fusion.2.p1 = bf16[512,512]{1,0:T(8,128)(2,1)} fusion(bf16[1024,512]{1,0:T(8,128)(2,1)} %bitcast.4, s32[512]{0:T(512)S(1)} %multiply_add_fusion), kind=kOutput, calls=%fused_computation.8 | convolution fusion | flops 537657344 | bytes 1574912 | tf_op jit(solution)/shard_map/dot_general | solution.py:41
  68.4 1.4 collective-permute-start.3
  70.4 11.9 %collective-permute-done.3.refs_4_ = bf16[512,512]{1,0:T(8,128)(2,1)} collective-permute-done((bf16[512,512]{1,0:T(8,128)(2,1)}, bf16[512,512]{1,0:T(8,128)(2,1)}, u32[]{:S(2)}, u32[]{:S(2)}) %collective-permute-start.3) | collective-permute-done | bytes 524320 | tf_op jit(solution)/shard_map/ppermute | solution.py:389
  82.3 0.7 fusion.53
  83.7 6.1 %shard_map.59 = (bf16[1024,512]{1,0:T(8,128)(2,1)S(1)}, bf16[512,1024]{1,0:T(8,128)(2,1)S(1)}, bf16[512,256]{1,0:T(8,128)(2,1)S(1)}, bf16[512,256]{1,0:T(8,128)(...) custom-call(s32[8]{0:T(128)S(1)} %compare_select_fusion.5.sc_ref, bf16[512,512]{1,0:T(8,128)(2,1)} %fusion.2.p1, ...), custom_call_target="tpu_custom_call" | custom-call | flops 20000000 | tf_op jit(solution)/shard_map/pallas_call | solution.py:294
  89.9 7.0 %shard_map.56 = (bf16[1024,512]{1,0:T(8,128)(2,1)}, bf16[512,1024]{1,0:T(8,128)(2,1)}, bf16[512,256]{1,0:T(8,128)(2,1)}, bf16[512,256]{1,0:T(8,128)(2,1)}, bf16[256,512]{1,0:T(8,128)(2,1)}, /*index=5*/f32[512,256]{1,0:T(8,128)}) custom-call(s32[8]{0:T(128)S(1)} %compare_select_fusion.5.sc_ref, bf16[512,512]{1,0:T(8,128)(2,1)} %fusion.3.p1, ...), custom_call_target="tpu_custom_call" | custom-call | flops 24000000 | tf_op jit(solution)/shard_map/pallas_call | solution.py:294
  96.9 9.6 %shard_map.57 = (bf16[512,512]{1,0:T(8,128)(2,1)S(1)}, bf16[1024,512]{1,0:T(8,128)(2,1)S(1)}, bf16[512,1024]{1,0:T(8,128)(2,1)S(1)}, bf16[1024,512]{1,0:T(8,128)(2,1)S(1)}, bf16[512,1024]{1,0:T(8,128)(2,1)S(1)}) custom-call(s32[8]{0:T(128)S(1)} %compare_select_fusion.5.sc_ref, bf16[512,512]{1,0:T(8,128)(2,1)S(1)} %collective-permute-done.p1, ...), custom_call_target="tpu_custom_call" | custom-call | flops 36000000 | tf_op jit(solution)/shard_map/pallas_call | solution.py:294
  106.5 4.1 %shard_map.60.refs_13_ = f32[512,256]{1,0:T(8,128)S(1)} custom-call(s32[8]{0:T(128)S(1)} %compare_select_fusion.5.sc_ref, bf16[1024,512]{1,0:T(8,128)(2,1)S(1)} %get-tuple-element.28.k0.refs_0_, bf16[512,1024]{1,0:T(8,128)(2,1)S(1)} %get-tuple-element.29.v0.refs_1_, bf16[1024,512]{1,0:T(8,128)(2,1)S(1)} %get-tuple-element.30.k1.refs_2_, ...), custom_call_target="tpu_custom_call" | custom-call | flops 20000000 | tf_op jit(solution)/shard_map/pallas_call | solution.py:294
  110.6 11.7 %shard_map.61 = bf16[1024,512]{1,0:T(8,128)(2,1)S(1)} custom-call(s32[8]{0:T(128)S(1)} %compare_select_fusion.5.sc_ref, bf16[1024,512]{1,0:T(8,128)(2,1)S(1)} %get-tuple-element.28.k0.refs_0_, bf16[512,1024]{1,0:T(8,128)(2,1)S(1)} %get-tuple-element.29.v0.refs_1_, bf16[1024,512]{1,0:T(8,128)(2,1)S(1)} %get-tuple-element.30.k1.refs_2_, ...), custom_call_target="tpu_custom_call" | custom-call | flops 44000000 | tf_op jit(solution)/shard_map/pallas_call | solution.py:294
  122.3 21.9 %all_to_all.20 = bf16[16,64,512]{2,1,0:T(8,128)(2,1)S(1)} all-to-all(bf16[16,64,512]{2,1,0:T(8,128)(2,1)S(1)} %bitcast.21), channel_id=1, replica_groups=mesh['dp'=8,'xh'=2,'xl'=2,'yh'=2,'co'=2] {'xh','yh','xl','co'}, dimensions={0} | all-to-all | bytes 2097152 | tf_op jit(solution)/shard_map/all_to_all | solution.py:404
  144.3 1.0 copy.12
  (34 shorter events, 3.8 us)
Async XLA Ops:
  1.4 19.8 %all-to-all-start = ((s32[32,1,256]{2,1,0:T(1,128)}), s32[32,1,256]{2,1,0:T(1,128)S(1)}, u32[]{:S(2)}, u32[]{:S(2)}) async-start(s32[32,1,256]{2,1,0:T(1,128)} %broadcast_in_dim.77), calls=%async_computation | async-start | bytes 65536 | tf_op jit(solution)/shard_map/all_to_all | solution.py:351
  29.8 17.9 %all-to-all-start.1 = ((bf16[8,128,512]{2,1,0:T(8,128)(2,1)}), bf16[8,128,512]{2,1,0:T(8,128)(2,1)S(1)}, u32[]{:S(2)}, u32[]{:S(2)}) async-start(bf16[8,128,512]{2,1,0:T(8,128)(2,1)} %bitcast.25), calls=%async_computation.1 | async-start | bytes 2097152 | tf_op jit(solution)/shard_map/all_to_all | solution.py:373
  47.7 17.9 %all-to-all-start.2 = ((bf16[8,128,512]{2,1,0:T(8,128)(2,1)}), bf16[8,128,512]{2,1,0:T(8,128)(2,1)}, u32[]{:S(2)}, u32[]{:S(2)}) async-start(bf16[8,128,512]{2,1,0:T(8,128)(2,1)} %bitcast.24), calls=%async_computation.2 | async-start | bytes 2097152 | tf_op jit(solution)/shard_map/all_to_all | solution.py:373
  54.5 27.8 %copy-start.2 = (s32[4]{0:T(128)S(1)}, s32[4]{0:T(128)}, u32[]{:S(2)}) copy-start(s32[4]{0:T(128)} %param.6) | copy-start | bytes 52
  54.5 29.2 %copy-start = (bf16[512,2048]{1,0:T(8,128)(2,1)S(1)}, bf16[512,2048]{1,0:T(8,128)(2,1)}, u32[]{:S(2)}) copy-start(bf16[512,2048]{1,0:T(8,128)(2,1)} %refs_6_.1) | copy-start | bytes 6291460
  54.5 15.9 %collective-permute-start = (bf16[512,512]{1,0:T(8,128)(2,1)}, bf16[512,512]{1,0:T(8,128)(2,1)S(1)}, u32[]{:S(2)}, u32[]{:S(2)}) collective-permute-start(bf16[512,512]{1,0:T(8,128)(2,1)} %fusion.3.p1), channel_id=1, source_target_pairs={{0,4},{4,0},{1,5},{5,1},{2,6},{6,2},{3,7},{7,3},{8,12},{12,8},{9,1... | collective-permute-start | bytes 1572872 | tf_op jit(solution)/shard_map/ppermute | solution.py:389
  68.4 13.9 %collective-permute-start.3 = (bf16[512,512]{1,0:T(8,128)(2,1)}, bf16[512,512]{1,0:T(8,128)(2,1)}, u32[]{:S(2)}, u32[]{:S(2)}) collective-permute-start(bf16[512,512]{1,0:T(8,128)(2,1)} %fusion.2.p1), channel_id=1, source_target_pairs={{0,4},{4,0},{1,5},{5,1},{2,6},{6,2},{3,7},{7,3},{8,12},{12,8},{9,1... | collective-permute-start | bytes 1572872 | tf_op jit(solution)/shard_map/ppermute | solution.py:389
  69.8 13.8 %collective-permute-start.5 = (bf16[512,512]{1,0:T(8,128)(2,1)}, bf16[512,512]{1,0:T(8,128)(2,1)}, u32[]{:S(2)}, u32[]{:S(2)}) collective-permute-start(bf16[512,512]{1,0:T(8,128)(2,1)} %fusion.2.p1), channel_id=1, source_target_pairs={{0,1},{1,0},{2,3},{3,2},{4,5},{5,4},{6,7},{7,6},{8,9},{9,8},{10,11... | collective-permute-start | bytes 1572872 | tf_op jit(solution)/shard_map/ppermute | solution.py:390
  69.8 20.0 %collective-permute-start.2 = (bf16[512,512]{1,0:T(8,128)(2,1)}, bf16[512,512]{1,0:T(8,128)(2,1)}, u32[]{:S(2)}, u32[]{:S(2)}) collective-permute-start(bf16[512,512]{1,0:T(8,128)(2,1)} %fusion.3.p1), channel_id=1, source_target_pairs={{0,1},{1,0},{2,3},{3,2},{4,5},{5,4},{6,7},{7,6},{8,9},{9,8},{10,11... | collective-permute-start | bytes 1572872 | tf_op jit(solution)/shard_map/ppermute | solution.py:390
  70.4 26.5 %collective-permute-start.1 = (bf16[512,512]{1,0:T(8,128)(2,1)S(1)}, bf16[512,512]{1,0:T(8,128)(2,1)S(1)}, u32[]{:S(2)}, u32[]{:S(2)}) collective-permute-start(bf16[512,512]{1,0:T(8,128)(2,1)S(1)} %collective-permute-done.p1), channel_id=1, source_target_pairs={{0,1},{1,0},{2,3},{3,2},{4,5},{5,4},{6,7},{7,6},{8,9},{9,8},{10,11... | collective-permute-start | bytes 1572872 | tf_op jit(solution)/shard_map/ppermute | solution.py:391
  82.3 28.4 %collective-permute-start.4 = (bf16[512,512]{1,0:T(8,128)(2,1)}, bf16[512,512]{1,0:T(8,128)(2,1)}, u32[]{:S(2)}, u32[]{:S(2)}) collective-permute-start(bf16[512,512]{1,0:T(8,128)(2,1)} %collective-permute-done.3.refs_4_), channel_id=1, source_target_pairs={{0,1},{1,0},{2,3},{3,2},{4,5},{5,4},{6,7},{7,6},{8,9},{9,8},{10,11... | collective-permute-start | bytes 1572872 | tf_op jit(solution)/shard_map/ppermute | solution.py:391
  89.8 7.1 %copy-start.1 = (bf16[512,512]{1,0:T(8,128)(2,1)S(1)}, bf16[512,512]{1,0:T(8,128)(2,1)}, u32[]{:S(2)}) copy-start(bf16[512,512]{1,0:T(8,128)(2,1)} %refs_7_.1) | copy-start | bytes 1572868

commit v7 on v6

--- a/solution.py
+++ b/solution.py
@@ -17,7 +17,7 @@
 BUNCH = 32
 VM = pl.BlockSpec(memory_space=pltpu.VMEM)
 SM = pl.BlockSpec(memory_space=pltpu.SMEM)
-ANY = pl.BlockSpec(memory_space=pl.ANY)
+HBM = pl.BlockSpec(memory_space=pltpu.HBM)
 PARAMS = pltpu.CompilerParams(vmem_limit_bytes=16 * 1024 * 1024)
 
 
@@ -105,12 +105,42 @@
     return pl.pallas_call(
         functools.partial(gather_kernel, owners, outs),
         out_shape=[shape] * outs,
-        in_specs=[SM, SM, VM, pl.BlockSpec(memory_space=pltpu.HBM)],
+        in_specs=[SM, SM, VM, HBM],
         out_specs=[VM] * outs,
         scratch_shapes=[pltpu.VMEM((owners * CAP, 8, D), BF), pltpu.SemaphoreType.DMA((owners,))],
         compiler_params=pltpu.CompilerParams(vmem_limit_bytes=56 * 1024 * 1024),
         cost_estimate=cost(7),
     )(rows, count, rows, groups)
+
+
+def place_kernel(at_ref, got_ref, own_ref, buf, sems):
+    rows = own_ref.shape[0]
+    parts = [pl.ds(2 * CAP * j, 2 * CAP) for j in range(4)]
+    copies = [pltpu.make_async_copy(got_ref.at[p], buf.at[p], sems.at[j]) for j, p in enumerate(parts)]
+    for c in copies:
+        c.start()
+    at = jnp.broadcast_to(at_ref[...].astype(F32), (8, rows)).T[:, :1]
+    lane = lax.broadcasted_iota(jnp.int32, (rows, 2 * CAP), 1).astype(F32)
+    own = None
+    for j, c in enumerate(copies):
+        pick = (lane + 2.0 * CAP * j == at).astype(F32).astype(BF)
+        c.wait()
+        part = nn(pick, buf[2 * CAP * j : 2 * CAP * (j + 1), :])
+        own = part if own is None else own + part
+    own_ref[...] = own.astype(BF)
+
+
+def place_call(at, got):
+    return pl.pallas_call(
+        place_kernel,
+        out_shape=pltpu.VMEM((at.shape[1], D), BF),
+        in_specs=[VM, HBM],
+        out_specs=VM,
+        scratch_shapes=[pltpu.VMEM(got.shape, BF), pltpu.SemaphoreType.DMA((4,))],
+        compiler_params=PARAMS,
+        cost_estimate=cost(1.5),
+        name="place",
+    )(at, got)
 
 
 def project(first, side, sc_ref, pieces, w_ref, k_ref, v_ref, q_ref, g_ref, x_ref, n_scr, nq_scr):
@@ -281,7 +311,6 @@
 
 
 SIZES = [(GRP, D), (D, GRP), (D, 256), (D, 256), (256, D)]
-HBM = pl.BlockSpec(memory_space=pltpu.HBM)
 SUMS = pltpu.VMEM((D, 256), F32)
 PROJECT = [pltpu.VMEM((2, D, D), BF), pltpu.VMEM((256, D), BF)]
 
@@ -377,8 +406,7 @@
         owner = own_ids // owned
         member = owner[None, :] == lax.broadcasted_iota(jnp.int32, (owners, 2 * BLK), 0)
         at = jnp.sum(jnp.where(member, ranks(member), 0), axis=0) + owner * CAP
-        pick = (at[:, None] == lax.broadcasted_iota(jnp.int32, (2 * BLK, owners * CAP), 1)).astype(BF)
-        return nn(pick, got).astype(BF)
+        return place_call(at[None], pltpu.with_memory_space_constraint(got, pltpu.HBM))
 
     def vmem_all(arrays):
         return [in_vmem(a) for a in arrays]
@@ -402,7 +430,7 @@
             kept[5] = in_vmem(total)
             out = far1_call(sc, past, far, diag, w_in, w_out, kept, first)
     back = lax.all_to_all(out.reshape(16, PART, D), ("xh", "yh", "xl", "co"), 0, 0, tiled=True)
-    return pltpu.with_memory_space_constraint(back.reshape(4, BLK, D), pltpu.HBM)
+    return back.reshape(4, BLK, D)
 
 
 def solution(mesh):

time: 147 us -> 146 us (level)
  Pallas kernels: 52.9 us -> 57.3 us
  matrix products: 5.37 us -> 1.04 us
    dot_general x6 -> x4, matrix products: 5.37 us -> 1.04 us  [nn(): return jnp.dot(a, b, preferred_element_type=F32)]
    pallas_call x0 -> x2, Pallas kernels: none -> 4.01 us  [place_call(): pl.pallas_call(place_kernel, out_shape=pltpu.VMEM((at.shape[1], D), BF),...]
  transfers between devices with their start and end apart: 9 -> 9, of which waited for: 4 -> 4; matrix products, arithmetic and copies ran while one was open for 5% -> 2% of each run, Pallas kernels for 24% -> 27%
where the time goes in v7:
time: 146 us; the launch traced here: 145 us
  Pallas kernels  57.3 us (39%)
  waiting for transfers between devices  33.1 us (23%)
  starting transfers between devices  24.5 us (17%)
  blocking collectives  21.9 us (15%)
  other arithmetic  4.05 us (3%)
  local copies, waits for them, and re-layouts  2.39 us (2%)
    pallas_call x5, Pallas kernels, call(): pl.pallas_call(kernel, out_shape=out_shape, in_specs=[SM] + in_specs, out...  38.9 us
    all_to_all x1, blocking collectives, layer(): lax.all_to_all(out.reshape(16, PART, D), ('xh', 'yh', 'xl', 'co'), 0, 0,...  21.9 us
    pallas_call x2, Pallas kernels, gather_call(): pl.pallas_call(functools.partial(gather_kernel, owners, outs), out_shape=...  14.4 us
    all_to_all x2, waiting for transfers between devices, fetch(): lax.all_to_all(picked, 'dp', 0, 0, tiled=True).reshape(owners * CAP, D)  12.7 us
    ppermute x2, waiting for transfers between devices, layer(): far = lax.ppermute(own, 'xl', FLIP)  11.7 us
    all_to_all x1, starting transfers between devices, layer(): lax.all_to_all(send, ('dp', 'xh', 'yh'), 0, 0, tiled=True)  11 us
    all_to_all x2, starting transfers between devices, fetch(): lax.all_to_all(picked, 'dp', 0, 0, tiled=True).reshape(owners * CAP, D)  10.6 us
    all_to_all x1, waiting for transfers between devices, layer(): lax.all_to_all(send, ('dp', 'xh', 'yh'), 0, 0, tiled=True)  8.74 us
  transfers between devices with their start and end apart: 9, of which 4 were waited for; matrix products, arithmetic and copies ran while one was open for 2% of the time, Pallas kernels for 27%

profile of v7, /device:TPU:8, one launch (start us, length us, event | category | flops | bytes accessed | tf_op | source)
XLA Modules:
  0.0 144.6 jit_solution(9747042650450376481)
XLA Ops:
  0.0 0.7 broadcast_in_dim.76
  1.4 11.0 %all-to-all-start = ((s32[32,1,256]{2,1,0:T(1,128)}), s32[32,1,256]{2,1,0:T(1,128)S(1)}, u32[]{:S(2)}, u32[]{:S(2)}) async-start(s32[32,1,256]{2,1,0:T(1,128)} %broadcast_in_dim.77), calls=%async_computation | async-start | bytes 65536 | tf_op jit(solution)/shard_map/all_to_all | solution.py:380
  12.4 8.7 %all-to-all-done = s32[32,1,256]{2,1,0:T(1,128)S(1)} async-done(((s32[32,1,256]{2,1,0:T(1,128)}), s32[32,1,256]{2,1,0:T(1,128)S(1)}, u32[]{:S(2)}, u32[]{:S(2)}) %all-to-all-start) | async-done | bytes 32800 | tf_op jit(solution)/shard_map/all_to_all | solution.py:380
  21.3 0.9 fusion.28
  22.4 0.9 select_reduce_fusion.1.rows_ref.ids_ref
  23.3 6.5 %shard_map.55 = bf16[1024,512]{1,0:T(8,128)(2,1)} custom-call(s32[8,128]{1,0:T(8,128)} %select_reduce_fusion.1.rows_ref.ids_ref, s32[8]{0:T(128)} %get-tuple-element.40.count_ref, s32[8,128]{1,0:T(8,128)} %select_reduce_fusion.1.rows_ref.ids_ref, bf16[2048,8,512]{2,1,0:T(8,128)(2,1)} %bitcast.28), custom_call_target="tpu_custom_call" | custom-call | flops 28000000 | tf_op jit(solution)/shard_map/pallas_call | solution.py:105
  29.8 5.9 %all-to-all-start.1 = ((bf16[8,128,512]{2,1,0:T(8,128)(2,1)}), bf16[8,128,512]{2,1,0:T(8,128)(2,1)S(1)}, u32[]{:S(2)}, u32[]{:S(2)}) async-start(bf16[8,128,512]{2,1,0:T(8,128)(2,1)} %bitcast.31), calls=%async_computation.1 | async-start | bytes 2097152 | tf_op jit(solution)/shard_map/all_to_all | solution.py:402
  36.0 0.9 select_reduce_fusion.rows_ref.ids_ref
  36.9 7.9 %shard_map.58 = bf16[1024,512]{1,0:T(8,128)(2,1)} custom-call(s32[8,128]{1,0:T(8,128)} %select_reduce_fusion.rows_ref.ids_ref, s32[8]{0:T(128)} %get-tuple-element.39.count_ref, s32[8,128]{1,0:T(8,128)} %select_reduce_fusion.rows_ref.ids_ref, bf16[2048,8,512]{2,1,0:T(8,128)(2,1)} %bitcast.29), custom_call_target="tpu_custom_call" | custom-call | flops 28000000 | tf_op jit(solution)/shard_map/pallas_call | solution.py:105
  44.8 2.9 %all-to-all-done.1 = bf16[8,128,512]{2,1,0:T(8,128)(2,1)S(1)} async-done(((bf16[8,128,512]{2,1,0:T(8,128)(2,1)}), bf16[8,128,512]{2,1,0:T(8,128)(2,1)S(1)}, u32[]{:S(2)}, u32[]{:S(2)}) %all-to-all-start.1) | async-done | bytes 1048608 | tf_op jit(solution)/shard_map/all_to_all | solution.py:402
  47.7 4.7 %all-to-all-start.2 = ((bf16[8,128,512]{2,1,0:T(8,128)(2,1)}), bf16[8,128,512]{2,1,0:T(8,128)(2,1)}, u32[]{:S(2)}, u32[]{:S(2)}) async-start(bf16[8,128,512]{2,1,0:T(8,128)(2,1)} %bitcast.30), calls=%async_computation.2 | async-start | bytes 2097152 | tf_op jit(solution)/shard_map/all_to_all | solution.py:402
  53.0 2.1 %place.2.p1 = bf16[512,512]{1,0:T(8,128)(2,1)S(1)} custom-call(s32[1,512]{1,0:T(1,128)S(1)} %multiply_add_fusion.1.at_ref, bf16[1024,512]{1,0:T(8,128)(2,1)} %bitcast.32), custom_call_target="tpu_custom_call" | custom-call | flops 6000000 | tf_op jit(solution)/shard_map/place/pallas_call | solution.py:134
  55.1 0.8 collective-permute-start
  55.9 9.7 %all-to-all-done.2 = bf16[8,128,512]{2,1,0:T(8,128)(2,1)} async-done(((bf16[8,128,512]{2,1,0:T(8,128)(2,1)}), bf16[8,128,512]{2,1,0:T(8,128)(2,1)}, u32[]{:S(2)}, u32[]{:S(2)}) %all-to-all-start.2) | async-done | bytes 1048608 | tf_op jit(solution)/shard_map/all_to_all | solution.py:402
  65.7 1.9 %place.3.p1 = bf16[512,512]{1,0:T(8,128)(2,1)S(1)} custom-call(s32[1,512]{1,0:T(1,128)S(1)} %multiply_add_fusion.at_ref, bf16[1024,512]{1,0:T(8,128)(2,1)} %bitcast.6.got_ref), custom_call_target="tpu_custom_call" | custom-call | flops 6000000 | tf_op jit(solution)/shard_map/place/pallas_call | solution.py:134
  67.6 1.5 %collective-permute-start.3 = (bf16[512,512]{1,0:T(8,128)(2,1)S(1)}, bf16[512,512]{1,0:T(8,128)(2,1)}, u32[]{:S(2)}, u32[]{:S(2)}) collective-permute-start(bf16[512,512]{1,0:T(8,128)(2,1)S(1)} %place.3.p1), channel_id=1, source_target_pairs={{0,4},{4,0},{1,5},{5,1},{2,6},{6,2},{3,7},{7,3},{8,12},{12,8},{9,1... | collective-permute-start | bytes 1572872 | tf_op jit(solution)/shard_map/ppermute | solution.py:417
  69.7 11.7 %collective-permute-done.3.refs_4_ = bf16[512,512]{1,0:T(8,128)(2,1)} collective-permute-done((bf16[512,512]{1,0:T(8,128)(2,1)S(1)}, bf16[512,512]{1,0:T(8,128)(2,1)}, u32[]{:S(2)}, u32[]{:S(2)}) %collective-permute-start.3) | collective-permute-done | bytes 524320 | tf_op jit(solution)/shard_map/ppermute | solution.py:417
  82.7 6.0 %shard_map.59 = (bf16[1024,512]{1,0:T(8,128)(2,1)S(1)}, bf16[512,1024]{1,0:T(8,128)(2,1)S(1)}, bf16[512,256]{1,0:T(8,128)(2,1)S(1)}, bf16[512,256]{1,0:T(8,128)(...) custom-call(s32[8]{0:T(128)S(1)} %compare_select_fusion.11.sc_ref, bf16[512,512]{1,0:T(8,128)(2,1)S(1)} %place.3.p1, ...), custom_call_target="tpu_custom_call" | custom-call | flops 20000000 | tf_op jit(solution)/shard_map/pallas_call | solution.py:323
  88.7 6.9 %shard_map.56 = (bf16[1024,512]{1,0:T(8,128)(2,1)}, bf16[512,1024]{1,0:T(8,128)(2,1)}, bf16[512,256]{1,0:T(8,128)(2,1)}, bf16[512,256]{1,0:T(8,128)(2,1)}, bf16[256,512]{1,0:T(8,128)(2,1)}, /*index=5*/f32[512,256]{1,0:T(8,128)}) custom-call(s32[8]{0:T(128)S(1)} %compare_select_fusion.11.sc_ref, bf16[512,512]{1,0:T(8,128)(2,1)S(1)} %place.2.p1, ...), custom_call_target="tpu_custom_call" | custom-call | flops 24000000 | tf_op jit(solution)/shard_map/pallas_call | solution.py:323
  95.6 10.2 %shard_map.57 = (bf16[512,512]{1,0:T(8,128)(2,1)S(1)}, bf16[1024,512]{1,0:T(8,128)(2,1)S(1)}, bf16[512,1024]{1,0:T(8,128)(2,1)S(1)}, bf16[1024,512]{1,0:T(8,128)(2,1)S(1)}, bf16[512,1024]{1,0:T(8,128)(2,1)S(1)}) custom-call(s32[8]{0:T(128)S(1)} %compare_select_fusion.11.sc_ref, bf16[512,512]{1,0:T(8,128)(2,1)} %collective-permute-done.p1, ...), custom_call_target="tpu_custom_call" | custom-call | flops 36000000 | tf_op jit(solution)/shard_map/pallas_call | solution.py:323
  105.8 4.1 %shard_map.60.refs_13_ = f32[512,256]{1,0:T(8,128)S(1)} custom-call(s32[8]{0:T(128)S(1)} %compare_select_fusion.11.sc_ref, bf16[1024,512]{1,0:T(8,128)(2,1)S(1)} %get-tuple-element.28.k0.refs_0_, bf16[512,1024]{1,0:T(8,128)(2,1)S(1)} %get-tuple-element.29.v0.refs_1_, bf16[1024,512]{1,0:T(8,128)(2,1)S(1)} %get-tuple-element.30.k1.refs_2_, ...), custom_call_target="tpu_custom_call" | custom-call | flops 20000000 | tf_op jit(solution)/shard_map/pallas_call | solution.py:323
  110.0 11.7 %shard_map.61 = bf16[1024,512]{1,0:T(8,128)(2,1)S(1)} custom-call(s32[8]{0:T(128)S(1)} %compare_select_fusion.11.sc_ref, bf16[1024,512]{1,0:T(8,128)(2,1)S(1)} %get-tuple-element.28.k0.refs_0_, bf16[512,1024]{1,0:T(8,128)(2,1)S(1)} %get-tuple-element.29.v0.refs_1_, bf16[1024,512]{1,0:T(8,128)(2,1)S(1)} %get-tuple-element.30.k1.refs_2_, ...), custom_call_target="tpu_custom_call" | custom-call | flops 44000000 | tf_op jit(solution)/shard_map/pallas_call | solution.py:323
  121.7 21.9 %all_to_all.20 = bf16[16,64,512]{2,1,0:T(8,128)(2,1)S(1)} all-to-all(bf16[16,64,512]{2,1,0:T(8,128)(2,1)S(1)} %bitcast.27), channel_id=1, replica_groups=mesh['dp'=8,'xh'=2,'xl'=2,'yh'=2,'co'=2] {'xh','yh','xl','co'}, dimensions={0} | all-to-all | bytes 2097152 | tf_op jit(solution)/shard_map/all_to_all | solution.py:432
  143.6 1.0 copy.14
  (37 shorter events, 3.7 us)
Async XLA Ops:
  1.4 19.8 %all-to-all-start = ((s32[32,1,256]{2,1,0:T(1,128)}), s32[32,1,256]{2,1,0:T(1,128)S(1)}, u32[]{:S(2)}, u32[]{:S(2)}) async-start(s32[32,1,256]{2,1,0:T(1,128)} %broadcast_in_dim.77), calls=%async_computation | async-start | bytes 65536 | tf_op jit(solution)/shard_map/all_to_all | solution.py:380
  29.8 17.9 %all-to-all-start.1 = ((bf16[8,128,512]{2,1,0:T(8,128)(2,1)}), bf16[8,128,512]{2,1,0:T(8,128)(2,1)S(1)}, u32[]{:S(2)}, u32[]{:S(2)}) async-start(bf16[8,128,512]{2,1,0:T(8,128)(2,1)} %bitcast.31), calls=%async_computation.1 | async-start | bytes 2097152 | tf_op jit(solution)/shard_map/all_to_all | solution.py:402
  47.7 5.3 %copy-start.2 = (bf16[8,128,512]{2,1,0:T(8,128)(2,1)}, bf16[8,128,512]{2,1,0:T(8,128)(2,1)S(1)}, u32[]{:S(2)}) copy-start(bf16[8,128,512]{2,1,0:T(8,128)(2,1)S(1)} %all-to-all-done.1) | copy-start | bytes 3145732
  47.7 17.9 %all-to-all-start.2 = ((bf16[8,128,512]{2,1,0:T(8,128)(2,1)}), bf16[8,128,512]{2,1,0:T(8,128)(2,1)}, u32[]{:S(2)}, u32[]{:S(2)}) async-start(bf16[8,128,512]{2,1,0:T(8,128)(2,1)} %bitcast.30), calls=%async_computation.2 | async-start | bytes 2097152 | tf_op jit(solution)/shard_map/all_to_all | solution.py:402
  52.7 28.7 %copy-start.3 = (s32[4]{0:T(128)S(1)}, s32[4]{0:T(128)}, u32[]{:S(2)}) copy-start(s32[4]{0:T(128)} %param.6) | copy-start | bytes 52
  52.7 30.0 %copy-start = (bf16[512,2048]{1,0:T(8,128)(2,1)S(1)}, bf16[512,2048]{1,0:T(8,128)(2,1)}, u32[]{:S(2)}) copy-start(bf16[512,2048]{1,0:T(8,128)(2,1)} %refs_6_.1) | copy-start | bytes 6291460
  55.1 14.5 %collective-permute-start = (bf16[512,512]{1,0:T(8,128)(2,1)S(1)}, bf16[512,512]{1,0:T(8,128)(2,1)}, u32[]{:S(2)}, u32[]{:S(2)}) collective-permute-start(bf16[512,512]{1,0:T(8,128)(2,1)S(1)} %place.2.p1), channel_id=1, source_target_pairs={{0,4},{4,0},{1,5},{5,1},{2,6},{6,2},{3,7},{7,3},{8,12},{12,8},{9,1... | collective-permute-start | bytes 1572872 | tf_op jit(solution)/shard_map/ppermute | solution.py:417
  67.6 13.7 %collective-permute-start.3 = (bf16[512,512]{1,0:T(8,128)(2,1)S(1)}, bf16[512,512]{1,0:T(8,128)(2,1)}, u32[]{:S(2)}, u32[]{:S(2)}) collective-permute-start(bf16[512,512]{1,0:T(8,128)(2,1)S(1)} %place.3.p1), channel_id=1, source_target_pairs={{0,4},{4,0},{1,5},{5,1},{2,6},{6,2},{3,7},{7,3},{8,12},{12,8},{9,1... | collective-permute-start | bytes 1572872 | tf_op jit(solution)/shard_map/ppermute | solution.py:417
  69.1 13.5 %collective-permute-start.5 = (bf16[512,512]{1,0:T(8,128)(2,1)S(1)}, bf16[512,512]{1,0:T(8,128)(2,1)}, u32[]{:S(2)}, u32[]{:S(2)}) collective-permute-start(bf16[512,512]{1,0:T(8,128)(2,1)S(1)} %place.3.p1), channel_id=1, source_target_pairs={{0,1},{1,0},{2,3},{3,2},{4,5},{5,4},{6,7},{7,6},{8,9},{9,8},{10,11... | collective-permute-start | bytes 1572872 | tf_op jit(solution)/shard_map/ppermute | solution.py:418
  69.1 19.5 %collective-permute-start.2 = (bf16[512,512]{1,0:T(8,128)(2,1)S(1)}, bf16[512,512]{1,0:T(8,128)(2,1)}, u32[]{:S(2)}, u32[]{:S(2)}) collective-permute-start(bf16[512,512]{1,0:T(8,128)(2,1)S(1)} %place.2.p1), channel_id=1, source_target_pairs={{0,1},{1,0},{2,3},{3,2},{4,5},{5,4},{6,7},{7,6},{8,9},{9,8},{10,11... | collective-permute-start | bytes 1572872 | tf_op jit(solution)/shard_map/ppermute | solution.py:418
  69.7 25.9 %collective-permute-start.1 = (bf16[512,512]{1,0:T(8,128)(2,1)}, bf16[512,512]{1,0:T(8,128)(2,1)}, u32[]{:S(2)}, u32[]{:S(2)}) collective-permute-start(bf16[512,512]{1,0:T(8,128)(2,1)} %collective-permute-done.p1), channel_id=1, source_target_pairs={{0,1},{1,0},{2,3},{3,2},{4,5},{5,4},{6,7},{7,6},{8,9},{9,8},{10,11... | collective-permute-start | bytes 1572872 | tf_op jit(solution)/shard_map/ppermute | solution.py:419
  81.3 28.6 %collective-permute-start.4 = (bf16[512,512]{1,0:T(8,128)(2,1)}, bf16[512,512]{1,0:T(8,128)(2,1)}, u32[]{:S(2)}, u32[]{:S(2)}) collective-permute-start(bf16[512,512]{1,0:T(8,128)(2,1)} %collective-permute-done.3.refs_4_), channel_id=1, source_target_pairs={{0,1},{1,0},{2,3},{3,2},{4,5},{5,4},{6,7},{7,6},{8,9},{9,8},{10,11... | collective-permute-start | bytes 1572872 | tf_op jit(solution)/shard_map/ppermute | solution.py:419
  88.7 6.9 %copy-start.1 = (bf16[512,512]{1,0:T(8,128)(2,1)S(1)}, bf16[512,512]{1,0:T(8,128)(2,1)}, u32[]{:S(2)}) copy-start(bf16[512,512]{1,0:T(8,128)(2,1)} %refs_7_.1) | copy-start | bytes 1572868

commit v8 on v7

--- a/solution.py
+++ b/solution.py
@@ -113,7 +113,8 @@
     )(rows, count, rows, groups)
 
 
-def place_kernel(at_ref, got_ref, own_ref, buf, sems):
+def place_kernel(at_ref, length_ref, got_ref, own_ref, kept_ref, buf, sems):
+    kept_ref[...] = length_ref[...]
     rows = own_ref.shape[0]
     parts = [pl.ds(2 * CAP * j, 2 * CAP) for j in range(4)]
     copies = [pltpu.make_async_copy(got_ref.at[p], buf.at[p], sems.at[j]) for j, p in enumerate(parts)]
@@ -130,17 +131,23 @@
     own_ref[...] = own.astype(BF)
 
 
-def place_call(at, got):
+def place_call(at, length, got):
     return pl.pallas_call(
         place_kernel,
-        out_shape=pltpu.VMEM((at.shape[1], D), BF),
-        in_specs=[VM, HBM],
-        out_specs=VM,
+        out_shape=[pltpu.VMEM((at.shape[1], D), BF), pltpu.VMEM(length.shape, jnp.int32)],
+        in_specs=[VM, VM, HBM],
+        out_specs=[VM, VM],
         scratch_shapes=[pltpu.VMEM(got.shape, BF), pltpu.SemaphoreType.DMA((4,))],
         compiler_params=PARAMS,
         cost_estimate=cost(1.5),
         name="place",
-    )(at, got)
+    )(at, length, got)
+
+
+def scalars(length_ref=None):
+    xl, co = lax.axis_index("xl"), lax.axis_index("co")
+    length = None if length_ref is None else length_ref[0:1, 0:1]
+    return length, PART * (2 * xl + co), co, xl, 1 - xl
 
 
 def project(first, side, sc_ref, pieces, w_ref, k_ref, v_ref, q_ref, g_ref, x_ref, n_scr, nq_scr):
@@ -235,7 +242,8 @@
     lax.fori_loop(0, 4 // together, heads, 0)
 
 
-def near0_kernel(sc_ref, p1, p2, w_ref, *refs):
+def near0_kernel(length_ref, p1, p2, w_ref, *refs):
+    sc_ref = scalars(length_ref)
     outs, held, (n_scr, nq_scr, sems) = refs[:6], refs[6:12], refs[12:]
     k, v, q, g, x, o = held
     copies = [pltpu.make_async_copy(src, dst, sems.at[i]) for i, (src, dst) in enumerate(zip(held, outs))]
@@ -248,12 +256,14 @@
         c.wait()
 
 
-def near1_kernel(sc_ref, p1, p2, w_ref, k_ref, v_ref, q_ref, g_ref, x_ref, o_ref, n_scr, nq_scr):
+def near1_kernel(length_ref, p1, p2, w_ref, k_ref, v_ref, q_ref, g_ref, x_ref, o_ref, n_scr, nq_scr):
+    sc_ref = scalars(length_ref)
     project(2 * GRP, 0, sc_ref, (p1, p2), w_ref, k_ref, v_ref, q_ref, g_ref, x_ref, n_scr, nq_scr)
     attend(sc_ref, [(q_ref, o_ref, [(k_ref, v_ref, True)])], 2)
 
 
-def past_kernel(sc_ref, k0, v0, k1, v1, q_ref, before_ref, o_ref):
+def past_kernel(k0, v0, k1, v1, q_ref, before_ref, o_ref):
+    sc_ref = scalars()
     attend(sc_ref, [(q_ref, o_ref, [(k0, v0, False), (k1, v1, False)])], 2)
     o_ref[...] = o_ref[...] + before_ref[...]
 
@@ -292,7 +302,8 @@
     finish(chunk, sc_ref, wo_ref, ox, ((on, gn, xn), (of, gf, xf)), out_ref)
 
 
-def far0_kernel(sc_ref, p1, p2, w_ref, wo_ref, *refs):
+def far0_kernel(length_ref, p1, p2, w_ref, wo_ref, *refs):
+    sc_ref = scalars(length_ref)
     sent, (out_ref, kn, vn, kf, vf), rest = refs[:6], refs[6:11], refs[11:]
     kept = (kn, vn, *rest[:4])
     sems = rest[-1]
@@ -302,7 +313,8 @@
     far_core(0, sc_ref, (), p1, p2, w_ref, wo_ref, kept, arrive, out_ref, kf, vf, rest[4:-1])
 
 
-def far1_kernel(sc_ref, *refs):
+def far1_kernel(length_ref, *refs):
+    sc_ref = scalars(length_ref)
     past, (p1, p2, w_ref, wo_ref), kept = refs[:4], refs[4:8], refs[8:14]
     first_ref, out_ref = refs[14:16]
     scratch, (kf, vf) = refs[16:26], refs[26:]
@@ -323,7 +335,7 @@
     return pl.pallas_call(
         kernel,
         out_shape=out_shape,
-        in_specs=[SM] + in_specs,
+        in_specs=in_specs,
         out_specs=out_specs,
         scratch_shapes=scratch,
         compiler_params=PARAMS,
@@ -331,34 +343,34 @@
     )(*inputs)
 
 
-def near0_call(sc, own, near, w_in):
+def near0_call(length, own, near, w_in):
     shapes = [pltpu.HBM(s, BF) for s in SIZES] + [pltpu.HBM((D, 256), F32)]
     scratch = held() + [SUMS] + PROJECT + [pltpu.SemaphoreType.DMA((6,))]
-    return call(near0_kernel, 6, (sc, own, near, w_in), [VM] * 3, shapes, [HBM] * 6, scratch)
-
-
-def near1_call(sc, own, near, w_in):
-    return call(near1_kernel, 5, (sc, own, near, w_in), [VM] * 3, held() + [SUMS], [VM] * 6, PROJECT)
-
-
-def past_call(sc, past, q, before):
-    return call(past_kernel, 5, (sc, *past, q, before), [VM] * 6, SUMS, VM, [])
+    return call(near0_kernel, 6, (length, own, near, w_in), [VM] * 4, shapes, [HBM] * 6, scratch)
+
+
+def near1_call(length, own, near, w_in):
+    return call(near1_kernel, 5, (length, own, near, w_in), [VM] * 4, held() + [SUMS], [VM] * 6, PROJECT)
+
+
+def past_call(past, q, before):
+    return call(past_kernel, 5, (*past, q, before), [VM] * 6, SUMS, VM, [])
 
 
 FAR = PROJECT + held(slice(2, 5)) + [SUMS, pltpu.VMEM((D, 256), BF)] + held(slice(0, 2)) + [SUMS]
 
 
-def far0_call(sc, far, diag, w_in, w_out, sent):
+def far0_call(length, far, diag, w_in, w_out, sent):
     shapes = [pltpu.VMEM((512, D), BF)] + held(slice(0, 2)) * 2
     scratch = held(slice(2, 5)) + [SUMS] + FAR + [pltpu.SemaphoreType.DMA((6,))]
-    inputs = (sc, far, diag, w_in, w_out, *sent)
-    return call(far0_kernel, 9, inputs, [VM] * 4 + [HBM] * 6, shapes, [VM] * 5, scratch)
-
-
-def far1_call(sc, past, far, diag, w_in, w_out, kept, first):
-    inputs = (sc, *past, far, diag, w_in, w_out, *kept, first)
+    inputs = (length, far, diag, w_in, w_out, *sent)
+    return call(far0_kernel, 9, inputs, [VM] * 5 + [HBM] * 6, shapes, [VM] * 5, scratch)
+
+
+def far1_call(length, past, far, diag, w_in, w_out, kept, first):
+    inputs = (length, *past, far, diag, w_in, w_out, *kept, first)
     shape = jax.ShapeDtypeStruct((1024, D), BF)
-    return call(far1_kernel, 11, inputs, [VM] * 15, shape, VM, FAR + held(slice(0, 2)))
+    return call(far1_kernel, 11, inputs, [VM] * 16, shape, VM, FAR + held(slice(0, 2)))
 
 
 from jax.sharding import Mesh
@@ -371,7 +383,7 @@
 def layer(item_ids, lengths, table, w_in, w_out):
     owned = table.shape[0]
     me = lax.axis_index("dp")
-    xh, xl, yh, co = (lax.axis_index(a) for a in CTX)
+    xh, _, yh, _ = (lax.axis_index(a) for a in CTX)
     owners = lax.axis_size("dp")
     w_in, w_out = in_vmem(w_in), in_vmem(w_out)
     groups = table.reshape(-1, 8, D)
@@ -382,10 +394,7 @@
     user = 2 * xh + yh
     length = jnp.sum(jnp.where(lax.iota(jnp.int32, 4) == user, lengths, 0))
     upto = jnp.triu(jnp.ones((2 * BLK, 2 * BLK), BF))
-    slots = lax.iota(jnp.int32, 8)
-    sc = jnp.zeros((8,), jnp.int32)
-    for i, value in enumerate((length, PART * (2 * xl + co), co, xl, 1 - xl)):
-        sc = jnp.where(slots == i, value, sc)
+    length = jnp.broadcast_to(length, (8, 128))
 
     def ranks(member):
         return nn(member.astype(BF), upto).astype(jnp.int32) - 1
@@ -406,29 +415,30 @@
         owner = own_ids // owned
         member = owner[None, :] == lax.broadcasted_iota(jnp.int32, (owners, 2 * BLK), 0)
         at = jnp.sum(jnp.where(member, ranks(member), 0), axis=0) + owner * CAP
-        return place_call(at[None], pltpu.with_memory_space_constraint(got, pltpu.HBM))
+        return place_call(at[None], length, pltpu.with_memory_space_constraint(got, pltpu.HBM))
 
     def vmem_all(arrays):
         return [in_vmem(a) for a in arrays]
 
     for c in range(2):
         got = fetch(c)
-        own = place(c, got)
+        own, kept_length = place(c, got)
         far = lax.ppermute(own, "xl", FLIP)
         near = lax.ppermute(own, "co", FLIP)
         diag = lax.ppermute(far, "co", FLIP)
-        own, near, far, diag = vmem_all((own, near, far, diag))
+        own, near, far, diag, kept_length = vmem_all((own, near, far, diag, kept_length))
         if c == 0:
-            sent = near0_call(sc, own, near, w_in)
+            sent = near0_call(kept_length, own, near, w_in)
             sent = [pltpu.with_memory_space_constraint(a, pltpu.HBM) for a in sent]
-            done = far0_call(sc, far, diag, w_in, w_out, sent)
+            far0, diag0 = far, diag
+        else:
+            done = far0_call(kept_length, far0, diag0, w_in, w_out, sent)
             first, *past = vmem_all(done)
-        else:
-            kept = near1_call(sc, own, near, w_in)
+            kept = near1_call(kept_length, own, near, w_in)
             kept = vmem_all(kept)
-            total = past_call(sc, past, kept[2], kept[5])
+            total = past_call(past, kept[2], kept[5])
             kept[5] = in_vmem(total)
-            out = far1_call(sc, past, far, diag, w_in, w_out, kept, first)
+            out = far1_call(kept_length, past, far, diag, w_in, w_out, kept, first)
     back = lax.all_to_all(out.reshape(16, PART, D), ("xh", "yh", "xl", "co"), 0, 0, tiled=True)
     return back.reshape(4, BLK, D)
 

time: 146 us -> 140 us (0.959)
  Pallas kernels: 57.3 us -> 52.3 us
    pallas_call x7, Pallas kernels: 42.9 us -> 37.9 us  [the longest x5 34.1 us: call(): pl.pallas_call(kernel, out_shape=out_shape, in_specs=in_specs, out_specs=...]
  transfers between devices with their start and end apart: 9 -> 9, of which waited for: 4 -> 4; matrix products, arithmetic and copies ran while one was open for 2% -> 2% of each run, Pallas kernels for 27% -> 26%
where the time goes in v8:
time: 140 us; the launch traced here: 138 us
  Pallas kernels  52.3 us (37%)
  waiting for transfers between devices  31.9 us (23%)
  starting transfers between devices  24.5 us (18%)
  blocking collectives  21.9 us (16%)
  other arithmetic  3.47 us (2%)
  local copies, waits for them, and re-layouts  3.03 us (2%)
    pallas_call x5, Pallas kernels, call(): pl.pallas_call(kernel, out_shape=out_shape, in_specs=in_specs, out_specs=...  34.1 us
    all_to_all x1, blocking collectives, layer(): lax.all_to_all(out.reshape(16, PART, D), ('xh', 'yh', 'xl', 'co'), 0, 0,...  21.9 us
    pallas_call x2, Pallas kernels, gather_call(): pl.pallas_call(functools.partial(gather_kernel, owners, outs), out_shape=...  14.4 us
    ppermute x2, waiting for transfers between devices, layer(): far = lax.ppermute(own, 'xl', FLIP)  11.6 us
    all_to_all x2, waiting for transfers between devices, fetch(): lax.all_to_all(picked, 'dp', 0, 0, tiled=True).reshape(owners * CAP, D)  11.6 us
    all_to_all x1, starting transfers between devices, layer(): lax.all_to_all(send, ('dp', 'xh', 'yh'), 0, 0, tiled=True)  11 us
    all_to_all x2, starting transfers between devices, fetch(): lax.all_to_all(picked, 'dp', 0, 0, tiled=True).reshape(owners * CAP, D)  10.6 us
    all_to_all x1, waiting for transfers between devices, layer(): lax.all_to_all(send, ('dp', 'xh', 'yh'), 0, 0, tiled=True)  8.74 us
  transfers between devices with their start and end apart: 9, of which 4 were waited for; matrix products, arithmetic and copies ran while one was open for 2% of the time, Pallas kernels for 26%

profile of v8, /device:TPU:8, one launch (start us, length us, event | category | flops | bytes accessed | tf_op | source)
XLA Modules:
  0.0 138.3 jit_solution(2715785724957520051)
XLA Ops:
  0.0 0.7 broadcast_in_dim.57
  1.4 11.0 %all-to-all-start = ((s32[32,1,256]{2,1,0:T(1,128)}), s32[32,1,256]{2,1,0:T(1,128)S(1)}, u32[]{:S(2)}, u32[]{:S(2)}) async-start(s32[32,1,256]{2,1,0:T(1,128)} %broadcast_in_dim.58), calls=%async_computation | async-start | bytes 65536 | tf_op jit(solution)/shard_map/all_to_all | solution.py:392
  12.4 8.7 %all-to-all-done = s32[32,1,256]{2,1,0:T(1,128)S(1)} async-done(((s32[32,1,256]{2,1,0:T(1,128)}), s32[32,1,256]{2,1,0:T(1,128)S(1)}, u32[]{:S(2)}, u32[]{:S(2)}) %all-to-all-start) | async-done | bytes 32800 | tf_op jit(solution)/shard_map/all_to_all | solution.py:392
  21.3 0.9 fusion.28
  22.4 0.9 select_reduce_fusion.rows_ref.ids_ref
  23.3 6.6 %shard_map.56 = bf16[1024,512]{1,0:T(8,128)(2,1)} custom-call(s32[8,128]{1,0:T(8,128)} %select_reduce_fusion.rows_ref.ids_ref, s32[8]{0:T(128)} %get-tuple-element.47.count_ref, s32[8,128]{1,0:T(8,128)} %select_reduce_fusion.rows_ref.ids_ref, bf16[2048,8,512]{2,1,0:T(8,128)(2,1)} %bitcast.28), custom_call_target="tpu_custom_call" | custom-call | flops 28000000 | tf_op jit(solution)/shard_map/pallas_call | solution.py:105
  29.9 5.9 %all-to-all-start.2 = ((bf16[8,128,512]{2,1,0:T(8,128)(2,1)}), bf16[8,128,512]{2,1,0:T(8,128)(2,1)S(1)}, u32[]{:S(2)}, u32[]{:S(2)}) async-start(bf16[8,128,512]{2,1,0:T(8,128)(2,1)} %bitcast.30), calls=%async_computation.2 | async-start | bytes 2097152 | tf_op jit(solution)/shard_map/all_to_all | solution.py:411
  36.7 0.9 select_reduce_fusion.1.rows_ref.ids_ref
  37.6 7.9 %shard_map.55 = bf16[1024,512]{1,0:T(8,128)(2,1)} custom-call(s32[8,128]{1,0:T(8,128)} %select_reduce_fusion.1.rows_ref.ids_ref, s32[8]{0:T(128)} %get-tuple-element.48.count_ref, s32[8,128]{1,0:T(8,128)} %select_reduce_fusion.1.rows_ref.ids_ref, bf16[2048,8,512]{2,1,0:T(8,128)(2,1)} %bitcast.29), custom_call_target="tpu_custom_call" | custom-call | flops 28000000 | tf_op jit(solution)/shard_map/pallas_call | solution.py:105
  45.5 2.3 %all-to-all-done.2 = bf16[8,128,512]{2,1,0:T(8,128)(2,1)S(1)} async-done(((bf16[8,128,512]{2,1,0:T(8,128)(2,1)}), bf16[8,128,512]{2,1,0:T(8,128)(2,1)S(1)}, u32[]{:S(2)}, u32[]{:S(2)}) %all-to-all-start.2) | async-done | bytes 1048608 | tf_op jit(solution)/shard_map/all_to_all | solution.py:411
  47.8 4.7 %all-to-all-start.1 = ((bf16[8,128,512]{2,1,0:T(8,128)(2,1)}), bf16[8,128,512]{2,1,0:T(8,128)(2,1)}, u32[]{:S(2)}, u32[]{:S(2)}) async-start(bf16[8,128,512]{2,1,0:T(8,128)(2,1)} %bitcast.31), calls=%async_computation.1 | async-start | bytes 2097152 | tf_op jit(solution)/shard_map/all_to_all | solution.py:411
  53.7 1.9 %place.3 = (bf16[512,512]{1,0:T(8,128)(2,1)S(1)}, s32[8,128]{1,0:T(8,128)S(1)}) custom-call(s32[1,512]{1,0:T(1,128)S(1)} %multiply_add_fusion.at_ref, s32[8,128]{1,0:T(8,128)S(1)} %broadcast_in_dim.63.length_ref, bf16[1024,512]{1,0:T(8,128)(2,1)} %bitcast.32), custom_call_target="tpu_custom_call" | custom-call | flops 6000000 | tf_op jit(solution)/shard_map/place/pallas_call | solution.py:135
  55.7 0.8 collective-permute-start
  56.5 9.2 %all-to-all-done.1 = bf16[8,128,512]{2,1,0:T(8,128)(2,1)} async-done(((bf16[8,128,512]{2,1,0:T(8,128)(2,1)}), bf16[8,128,512]{2,1,0:T(8,128)(2,1)}, u32[]{:S(2)}, u32[]{:S(2)}) %all-to-all-start.1) | async-done | bytes 1048608 | tf_op jit(solution)/shard_map/all_to_all | solution.py:411
  65.7 1.9 %place.2 = (bf16[512,512]{1,0:T(8,128)(2,1)S(1)}, s32[8,128]{1,0:T(8,128)S(1)}) custom-call(s32[1,512]{1,0:T(1,128)S(1)} %multiply_add_fusion.1.at_ref, s32[8,128]{1,0:T(8,128)S(1)} %broadcast_in_dim.63.length_ref, bf16[1024,512]{1,0:T(8,128)(2,1)} %bitcast.3.got_ref), custom_call_target="tpu_custom_call" | custom-call | flops 6000000 | tf_op jit(solution)/shard_map/place/pallas_call | solution.py:135
  67.7 1.5 %collective-permute-start.3 = (bf16[512,512]{1,0:T(8,128)(2,1)S(1)}, bf16[512,512]{1,0:T(8,128)(2,1)S(1)}, u32[]{:S(2)}, u32[]{:S(2)}) collective-permute-start(bf16[512,512]{1,0:T(8,128)(2,1)S(1)} %get-tuple-element.39.p1), channel_id=1, source_target_pairs={{0,4},{4,0},{1,5},{5,1},{2,6},{6,2},{3,7},{7,3},{8,12},{12,8},{9,1... | collective-permute-start | bytes 1572872 | tf_op jit(solution)/shard_map/ppermute | solution.py:426
  69.7 11.6 %collective-permute-done.3.refs_4_ = bf16[512,512]{1,0:T(8,128)(2,1)S(1)} collective-permute-done((bf16[512,512]{1,0:T(8,128)(2,1)S(1)}, bf16[512,512]{1,0:T(8,128)(2,1)S(1)}, u32[]{:S(2)}, u32[]{:S(2)}) %collective-permute-start.3) | collective-permute-done | bytes 524320 | tf_op jit(solution)/shard_map/ppermute | solution.py:426
  81.3 4.9 %shard_map.59 = (bf16[1024,512]{1,0:T(8,128)(2,1)S(1)}, bf16[512,1024]{1,0:T(8,128)(2,1)S(1)}, bf16[512,256]{1,0:T(8,128)(2,1)S(1)}, bf16[512,256]{1,0:T(8,128)(...) custom-call(s32[8,128]{1,0:T(8,128)S(1)} %get-tuple-element.26.length_ref, ...), custom_call_target="tpu_custom_call" | custom-call | flops 20000000 | tf_op jit(solution)/shard_map/pallas_call | solution.py:335
  86.2 5.8 %shard_map.57 = (bf16[1024,512]{1,0:T(8,128)(2,1)}, bf16[512,1024]{1,0:T(8,128)(2,1)}, bf16[512,256]{1,0:T(8,128)(2,1)}, bf16[512,256]{1,0:T(8,128)(2,1)}, bf16[256,512]{1,0:T(8,128)(2,1)}, /*index=5*/f32[512,256]{1,0:T(8,128)}) custom-call(s32[8,128]{1,0:T(8,128)S(1)} %get-tuple-element.28.length_ref, bf16[512,512]{1,0:T(8,128)(2,1)S(1)} %get-tuple-element.27.p1, ...), custom_call_target="tpu_custom_call" | custom-call | flops 24000000 | tf_op jit(solution)/shard_map/pallas_call | solution.py:335
  92.0 9.5 %shard_map.58 = (bf16[512,512]{1,0:T(8,128)(2,1)S(1)}, bf16[1024,512]{1,0:T(8,128)(2,1)S(1)}, bf16[512,1024]{1,0:T(8,128)(2,1)S(1)}, bf16[1024,512]{1,0:T(8,128)(2,1)S(1)}, bf16[512,1024]{1,0:T(8,128)(2,1)S(1)}) custom-call(s32[8,128]{1,0:T(8,128)S(1)} %get-tuple-element.26.length_ref, bf16[512,512]{1,0:T(8,128)(2,1)S(1)} %collective-permute-done.p1, ...), custom_call_target="tpu_custom_call" | custom-call | flops 36000000 | tf_op jit(solution)/shard_map/pallas_call | solution.py:335
  101.5 3.6 %shard_map.60.refs_13_ = f32[512,256]{1,0:T(8,128)S(1)} custom-call(bf16[1024,512]{1,0:T(8,128)(2,1)S(1)} %get-tuple-element.35.k0.refs_0_, bf16[512,1024]{1,0:T(8,128)(2,1)S(1)} %get-tuple-element.36.v0.refs_1_, bf16[1024,512]{1,0:T(8,128)(2,1)S(1)} %get-tuple-element.37.k1.refs_2_, bf16[512,1024]{1,0:T(8,128)(2,1)S(1)} %get-tuple-element.38.v1.refs_3_, ...), custom_call_target="tpu_custom_call" | custom-call | flops 20000000 | tf_op jit(solution)/shard_map/pallas_call | solution.py:335
  105.1 10.4 %shard_map.61 = bf16[1024,512]{1,0:T(8,128)(2,1)S(1)} custom-call(s32[8,128]{1,0:T(8,128)S(1)} %get-tuple-element.26.length_ref, bf16[1024,512]{1,0:T(8,128)(2,1)S(1)} %get-tuple-element.35.k0.refs_0_, bf16[512,1024]{1,0:T(8,128)(2,1)S(1)} %get-tuple-element.36.v0.refs_1_, bf16[1024,512]{1,0:T(8,128)(2,1)S(1)} %get-tuple-element.37.k1.refs_2_, ...), custom_call_target="tpu_custom_call" | custom-call | flops 44000000 | tf_op jit(solution)/shard_map/pallas_call | solution.py:335
  115.4 21.9 %all_to_all.20 = bf16[16,64,512]{2,1,0:T(8,128)(2,1)S(1)} all-to-all(bf16[16,64,512]{2,1,0:T(8,128)(2,1)S(1)} %bitcast.27), channel_id=1, replica_groups=mesh['dp'=8,'xh'=2,'xl'=2,'yh'=2,'co'=2] {'xh','yh','xl','co'}, dimensions={0} | all-to-all | bytes 2097152 | tf_op jit(solution)/shard_map/all_to_all | solution.py:442
  137.4 1.0 copy.14
  (37 shorter events, 3.7 us)
Async XLA Ops:
  1.4 19.8 %all-to-all-start = ((s32[32,1,256]{2,1,0:T(1,128)}), s32[32,1,256]{2,1,0:T(1,128)S(1)}, u32[]{:S(2)}, u32[]{:S(2)}) async-start(s32[32,1,256]{2,1,0:T(1,128)} %broadcast_in_dim.58), calls=%async_computation | async-start | bytes 65536 | tf_op jit(solution)/shard_map/all_to_all | solution.py:392
  29.9 5.9 %copy-start.3 = (s32[4]{0:T(128)S(1)}, s32[4]{0:T(128)}, u32[]{:S(2)}) copy-start(s32[4]{0:T(128)} %param.6) | copy-start | bytes 52
  29.9 17.9 %all-to-all-start.2 = ((bf16[8,128,512]{2,1,0:T(8,128)(2,1)}), bf16[8,128,512]{2,1,0:T(8,128)(2,1)S(1)}, u32[]{:S(2)}, u32[]{:S(2)}) async-start(bf16[8,128,512]{2,1,0:T(8,128)(2,1)} %bitcast.30), calls=%async_computation.2 | async-start | bytes 2097152 | tf_op jit(solution)/shard_map/all_to_all | solution.py:411
  47.8 5.3 %copy-start.2 = (bf16[8,128,512]{2,1,0:T(8,128)(2,1)}, bf16[8,128,512]{2,1,0:T(8,128)(2,1)S(1)}, u32[]{:S(2)}) copy-start(bf16[8,128,512]{2,1,0:T(8,128)(2,1)S(1)} %all-to-all-done.2) | copy-start | bytes 3145732
  47.8 17.9 %all-to-all-start.1 = ((bf16[8,128,512]{2,1,0:T(8,128)(2,1)}), bf16[8,128,512]{2,1,0:T(8,128)(2,1)}, u32[]{:S(2)}, u32[]{:S(2)}) async-start(bf16[8,128,512]{2,1,0:T(8,128)(2,1)} %bitcast.31), calls=%async_computation.1 | async-start | bytes 2097152 | tf_op jit(solution)/shard_map/all_to_all | solution.py:411
  52.5 28.8 %copy-start = (bf16[512,2048]{1,0:T(8,128)(2,1)S(1)}, bf16[512,2048]{1,0:T(8,128)(2,1)}, u32[]{:S(2)}) copy-start(bf16[512,2048]{1,0:T(8,128)(2,1)} %refs_6_.1) | copy-start | bytes 6291460
  55.7 14.0 %collective-permute-start = (bf16[512,512]{1,0:T(8,128)(2,1)S(1)}, bf16[512,512]{1,0:T(8,128)(2,1)S(1)}, u32[]{:S(2)}, u32[]{:S(2)}) collective-permute-start(bf16[512,512]{1,0:T(8,128)(2,1)S(1)} %get-tuple-element.27.p1), channel_id=1, source_target_pairs={{0,4},{4,0},{1,5},{5,1},{2,6},{6,2},{3,7},{7,3},{8,12},{12,8},{9,1... | collective-permute-start | bytes 1572872 | tf_op jit(solution)/shard_map/ppermute | solution.py:426
  67.7 13.6 %collective-permute-start.3 = (bf16[512,512]{1,0:T(8,128)(2,1)S(1)}, bf16[512,512]{1,0:T(8,128)(2,1)S(1)}, u32[]{:S(2)}, u32[]{:S(2)}) collective-permute-start(bf16[512,512]{1,0:T(8,128)(2,1)S(1)} %get-tuple-element.39.p1), channel_id=1, source_target_pairs={{0,4},{4,0},{1,5},{5,1},{2,6},{6,2},{3,7},{7,3},{8,12},{12,8},{9,1... | collective-permute-start | bytes 1572872 | tf_op jit(solution)/shard_map/ppermute | solution.py:426
  69.2 12.1 %collective-permute-start.5 = (bf16[512,512]{1,0:T(8,128)(2,1)S(1)}, bf16[512,512]{1,0:T(8,128)(2,1)S(1)}, u32[]{:S(2)}, u32[]{:S(2)}) collective-permute-start(bf16[512,512]{1,0:T(8,128)(2,1)S(1)} %get-tuple-element.39.p1), channel_id=1, source_target_pairs={{0,1},{1,0},{2,3},{3,2},{4,5},{5,4},{6,7},{7,6},{8,9},{9,8},{10,11... | collective-permute-start | bytes 1572872 | tf_op jit(solution)/shard_map/ppermute | solution.py:427
  69.2 17.0 %collective-permute-start.2 = (bf16[512,512]{1,0:T(8,128)(2,1)S(1)}, bf16[512,512]{1,0:T(8,128)(2,1)S(1)}, u32[]{:S(2)}, u32[]{:S(2)}) collective-permute-start(bf16[512,512]{1,0:T(8,128)(2,1)S(1)} %get-tuple-element.27.p1), channel_id=1, source_target_pairs={{0,1},{1,0},{2,3},{3,2},{4,5},{5,4},{6,7},{7,6},{8,9},{9,8},{10,11... | collective-permute-start | bytes 1572872 | tf_op jit(solution)/shard_map/ppermute | solution.py:427
  69.7 22.3 %collective-permute-start.1 = (bf16[512,512]{1,0:T(8,128)(2,1)S(1)}, bf16[512,512]{1,0:T(8,128)(2,1)S(1)}, u32[]{:S(2)}, u32[]{:S(2)}) collective-permute-start(bf16[512,512]{1,0:T(8,128)(2,1)S(1)} %collective-permute-done.p1), channel_id=1, source_target_pairs={{0,1},{1,0},{2,3},{3,2},{4,5},{5,4},{6,7},{7,6},{8,9},{9,8},{10,11... | collective-permute-start | bytes 1572872 | tf_op jit(solution)/shard_map/ppermute | solution.py:428
  81.3 23.8 %collective-permute-start.4 = (bf16[512,512]{1,0:T(8,128)(2,1)S(1)}, bf16[512,512]{1,0:T(8,128)(2,1)S(1)}, u32[]{:S(2)}, u32[]{:S(2)}) collective-permute-start(bf16[512,512]{1,0:T(8,128)(2,1)S(1)} %collective-permute-done.3.refs_4_), channel_id=1, source_target_pairs={{0,1},{1,0},{2,3},{3,2},{4,5},{5,4},{6,7},{7,6},{8,9},{9,8},{10,11... | collective-permute-start | bytes 1572872 | tf_op jit(solution)/shard_map/ppermute | solution.py:428
  86.2 5.8 %copy-start.1 = (bf16[512,512]{1,0:T(8,128)(2,1)S(1)}, bf16[512,512]{1,0:T(8,128)(2,1)}, u32[]{:S(2)}) copy-start(bf16[512,512]{1,0:T(8,128)(2,1)} %refs_7_.1) | copy-start | bytes 1572868

commit v9 on v8

--- a/solution.py
+++ b/solution.py
@@ -113,31 +113,20 @@
     )(rows, count, rows, groups)
 
 
-def place_kernel(at_ref, length_ref, got_ref, own_ref, kept_ref, buf, sems):
+def place_kernel(at_ref, length_ref, got_ref, own_ref, kept_ref):
     kept_ref[...] = length_ref[...]
     rows = own_ref.shape[0]
-    parts = [pl.ds(2 * CAP * j, 2 * CAP) for j in range(4)]
-    copies = [pltpu.make_async_copy(got_ref.at[p], buf.at[p], sems.at[j]) for j, p in enumerate(parts)]
-    for c in copies:
-        c.start()
     at = jnp.broadcast_to(at_ref[...].astype(F32), (8, rows)).T[:, :1]
-    lane = lax.broadcasted_iota(jnp.int32, (rows, 2 * CAP), 1).astype(F32)
-    own = None
-    for j, c in enumerate(copies):
-        pick = (lane + 2.0 * CAP * j == at).astype(F32).astype(BF)
-        c.wait()
-        part = nn(pick, buf[2 * CAP * j : 2 * CAP * (j + 1), :])
-        own = part if own is None else own + part
-    own_ref[...] = own.astype(BF)
+    lane = lax.broadcasted_iota(jnp.int32, (rows, got_ref.shape[0]), 1).astype(F32)
+    own_ref[...] = nn((lane == at).astype(F32).astype(BF), got_ref[...]).astype(BF)
 
 
 def place_call(at, length, got):
     return pl.pallas_call(
         place_kernel,
         out_shape=[pltpu.VMEM((at.shape[1], D), BF), pltpu.VMEM(length.shape, jnp.int32)],
-        in_specs=[VM, VM, HBM],
+        in_specs=[VM] * 3,
         out_specs=[VM, VM],
-        scratch_shapes=[pltpu.VMEM(got.shape, BF), pltpu.SemaphoreType.DMA((4,))],
         compiler_params=PARAMS,
         cost_estimate=cost(1.5),
         name="place",
@@ -389,12 +378,12 @@
     groups = table.reshape(-1, 8, D)
 
     send = jnp.broadcast_to(item_ids[None, :, None], (owners, 4, 1, BLK)).reshape(owners * 4, 1, BLK)
-    wanted = lax.all_to_all(send, ("dp", "xh", "yh"), 0, 0, tiled=True).reshape(owners, 4, BLK)
+    wanted = lax.all_to_all(send, ("dp", "xh", "yh"), 0, 0, tiled=True)
+    wanted = wanted.reshape(owners, 4, BLK)
     mine = lax.dynamic_index_in_dim(wanted, me, 0, keepdims=False)
-    user = 2 * xh + yh
-    length = jnp.sum(jnp.where(lax.iota(jnp.int32, 4) == user, lengths, 0))
     upto = jnp.triu(jnp.ones((2 * BLK, 2 * BLK), BF))
-    length = jnp.broadcast_to(length, (8, 128))
+    users = lax.broadcasted_iota(jnp.int32, (4, 8, 128), 0)
+    length = jnp.sum(jnp.where(users == 2 * xh + yh, lengths[:, None, None], 0), axis=0)
 
     def ranks(member):
         return nn(member.astype(BF), upto).astype(jnp.int32) - 1
@@ -415,7 +404,7 @@
         owner = own_ids // owned
         member = owner[None, :] == lax.broadcasted_iota(jnp.int32, (owners, 2 * BLK), 0)
         at = jnp.sum(jnp.where(member, ranks(member), 0), axis=0) + owner * CAP
-        return place_call(at[None], length, pltpu.with_memory_space_constraint(got, pltpu.HBM))
+        return place_call(at[None], length, in_vmem(got))
 
     def vmem_all(arrays):
         return [in_vmem(a) for a in arrays]

time: 140 us -> 141 us (level)
    all_to_all x2, waiting for transfers between devices: 11.6 us -> 13 us  [fetch(): lax.all_to_all(picked, 'dp', 0, 0, tiled=True).reshape(owners * CAP, D)]
  transfers between devices with their start and end apart: 9 -> 9, of which waited for: 4 -> 4; matrix products, arithmetic and copies ran while one was open for 2% -> 1% of each run, Pallas kernels for 26% -> 26%
where the time goes in v9:
time: 141 us; the launch traced here: 140 us
  Pallas kernels  53.5 us (38%)
  waiting for transfers between devices  33.3 us (24%)
  starting transfers between devices  24.4 us (17%)
  blocking collectives  21.9 us (16%)
  other arithmetic  2.86 us (2%)
  local copies, waits for them, and re-layouts  2.38 us (2%)
    pallas_call x5, Pallas kernels, call(): pl.pallas_call(kernel, out_shape=out_shape, in_specs=in_specs, out_specs=...  35.1 us
    all_to_all x1, blocking collectives, layer(): lax.all_to_all(out.reshape(16, PART, D), ('xh', 'yh', 'xl', 'co'), 0, 0,...  21.9 us
    pallas_call x2, Pallas kernels, gather_call(): pl.pallas_call(functools.partial(gather_kernel, owners, outs), out_shape=...  14.4 us
    all_to_all x2, waiting for transfers between devices, fetch(): lax.all_to_all(picked, 'dp', 0, 0, tiled=True).reshape(owners * CAP, D)  13 us
    ppermute x2, waiting for transfers between devices, layer(): far = lax.ppermute(own, 'xl', FLIP)  11.6 us
    all_to_all x1, starting transfers between devices, layer(): wanted = lax.all_to_all(send, ('dp', 'xh', 'yh'), 0, 0, tiled=True)  11 us
    all_to_all x2, starting transfers between devices, fetch(): lax.all_to_all(picked, 'dp', 0, 0, tiled=True).reshape(owners * CAP, D)  10.6 us
    all_to_all x1, waiting for transfers between devices, layer(): wanted = lax.all_to_all(send, ('dp', 'xh', 'yh'), 0, 0, tiled=True)  8.74 us
  transfers between devices with their start and end apart: 9, of which 4 were waited for; matrix products, arithmetic and copies ran while one was open for 1% of the time, Pallas kernels for 26%

profile of v9, /device:TPU:8, one launch (start us, length us, event | category | flops | bytes accessed | tf_op | source)
XLA Modules:
  0.0 139.7 jit_solution(4656343096098750840)
XLA Ops:
  0.0 0.7 broadcast_in_dim.63
  1.4 11.0 %all-to-all-start = ((s32[32,1,256]{2,1,0:T(1,128)}), s32[32,1,256]{2,1,0:T(1,128)S(1)}, u32[]{:S(2)}, u32[]{:S(2)}) async-start(s32[32,1,256]{2,1,0:T(1,128)} %broadcast_in_dim.64), calls=%async_computation | async-start | bytes 65536 | tf_op jit(solution)/shard_map/all_to_all | solution.py:381
  12.4 8.7 %all-to-all-done = s32[32,1,256]{2,1,0:T(1,128)S(1)} async-done(((s32[32,1,256]{2,1,0:T(1,128)}), s32[32,1,256]{2,1,0:T(1,128)S(1)}, u32[]{:S(2)}, u32[]{:S(2)}) %all-to-all-start) | async-done | bytes 32800 | tf_op jit(solution)/shard_map/all_to_all | solution.py:381
  21.3 0.9 fusion.28
  22.4 0.9 select_reduce_fusion.rows_ref.ids_ref
  23.3 6.6 %shard_map.56 = bf16[1024,512]{1,0:T(8,128)(2,1)} custom-call(s32[8,128]{1,0:T(8,128)} %select_reduce_fusion.rows_ref.ids_ref, s32[8]{0:T(128)} %get-tuple-element.47.count_ref, s32[8,128]{1,0:T(8,128)} %select_reduce_fusion.rows_ref.ids_ref, bf16[2048,8,512]{2,1,0:T(8,128)(2,1)} %bitcast.29), custom_call_target="tpu_custom_call" | custom-call | flops 28000000 | tf_op jit(solution)/shard_map/pallas_call | solution.py:105
  29.9 5.9 %all-to-all-start.2 = ((bf16[8,128,512]{2,1,0:T(8,128)(2,1)}), bf16[8,128,512]{2,1,0:T(8,128)(2,1)S(1)}, u32[]{:S(2)}, u32[]{:S(2)}) async-start(bf16[8,128,512]{2,1,0:T(8,128)(2,1)} %bitcast.31), calls=%async_computation.2 | async-start | bytes 2097152 | tf_op jit(solution)/shard_map/all_to_all | solution.py:400
  36.2 0.9 select_reduce_fusion.1.rows_ref.ids_ref
  37.0 7.9 %shard_map.55 = bf16[1024,512]{1,0:T(8,128)(2,1)} custom-call(s32[8,128]{1,0:T(8,128)} %select_reduce_fusion.1.rows_ref.ids_ref, s32[8]{0:T(128)} %get-tuple-element.48.count_ref, s32[8,128]{1,0:T(8,128)} %select_reduce_fusion.1.rows_ref.ids_ref, bf16[2048,8,512]{2,1,0:T(8,128)(2,1)} %bitcast.30), custom_call_target="tpu_custom_call" | custom-call | flops 28000000 | tf_op jit(solution)/shard_map/pallas_call | solution.py:105
  44.9 2.9 %all-to-all-done.2 = bf16[8,128,512]{2,1,0:T(8,128)(2,1)S(1)} async-done(((bf16[8,128,512]{2,1,0:T(8,128)(2,1)}), bf16[8,128,512]{2,1,0:T(8,128)(2,1)S(1)}, u32[]{:S(2)}, u32[]{:S(2)}) %all-to-all-start.2) | async-done | bytes 1048608 | tf_op jit(solution)/shard_map/all_to_all | solution.py:400
  47.8 4.7 %all-to-all-start.1 = ((bf16[8,128,512]{2,1,0:T(8,128)(2,1)}), bf16[8,128,512]{2,1,0:T(8,128)(2,1)}, u32[]{:S(2)}, u32[]{:S(2)}) async-start(bf16[8,128,512]{2,1,0:T(8,128)(2,1)} %bitcast.32), calls=%async_computation.1 | async-start | bytes 2097152 | tf_op jit(solution)/shard_map/all_to_all | solution.py:400
  53.0 1.8 %place.3 = (bf16[512,512]{1,0:T(8,128)(2,1)}, s32[8,128]{1,0:T(8,128)S(1)}) custom-call(s32[1,512]{1,0:T(1,128)S(1)} %multiply_add_fusion.at_ref, s32[8,128]{1,0:T(8,128)S(1)} %select_reduce_fusion.2.length_ref, bf16[1024,512]{1,0:T(8,128)(2,1)S(1)} %bitcast.28), custom_call_target="tpu_custom_call" | custom-call | flops 6000000 | tf_op jit(solution)/shard_map/place/pallas_call | solution.py:125
  54.8 0.7 collective-permute-start
  55.6 10.1 %all-to-all-done.1 = bf16[8,128,512]{2,1,0:T(8,128)(2,1)} async-done(((bf16[8,128,512]{2,1,0:T(8,128)(2,1)}), bf16[8,128,512]{2,1,0:T(8,128)(2,1)}, u32[]{:S(2)}, u32[]{:S(2)}) %all-to-all-start.1) | async-done | bytes 1048608 | tf_op jit(solution)/shard_map/all_to_all | solution.py:400
  65.7 2.2 %place.2 = (bf16[512,512]{1,0:T(8,128)(2,1)S(1)}, s32[8,128]{1,0:T(8,128)S(1)}) custom-call(s32[1,512]{1,0:T(1,128)S(1)} %multiply_add_fusion.1.at_ref, s32[8,128]{1,0:T(8,128)S(1)} %select_reduce_fusion.2.length_ref, bf16[1024,512]{1,0:T(8,128)(2,1)} %bitcast.3.got_ref), custom_call_target="tpu_custom_call" | custom-call | flops 6000000 | tf_op jit(solution)/shard_map/place/pallas_call | solution.py:125
  67.9 1.5 %collective-permute-start.3 = (bf16[512,512]{1,0:T(8,128)(2,1)S(1)}, bf16[512,512]{1,0:T(8,128)(2,1)S(1)}, u32[]{:S(2)}, u32[]{:S(2)}) collective-permute-start(bf16[512,512]{1,0:T(8,128)(2,1)S(1)} %get-tuple-element.39.p1), channel_id=1, source_target_pairs={{0,4},{4,0},{1,5},{5,1},{2,6},{6,2},{3,7},{7,3},{8,12},{12,8},{9,1... | collective-permute-start | bytes 1572872 | tf_op jit(solution)/shard_map/ppermute | solution.py:415
  70.0 11.6 %collective-permute-done.3.refs_4_ = bf16[512,512]{1,0:T(8,128)(2,1)S(1)} collective-permute-done((bf16[512,512]{1,0:T(8,128)(2,1)S(1)}, bf16[512,512]{1,0:T(8,128)(2,1)S(1)}, u32[]{:S(2)}, u32[]{:S(2)}) %collective-permute-start.3) | collective-permute-done | bytes 524320 | tf_op jit(solution)/shard_map/ppermute | solution.py:415
  81.6 4.9 %shard_map.59 = (bf16[1024,512]{1,0:T(8,128)(2,1)S(1)}, bf16[512,1024]{1,0:T(8,128)(2,1)S(1)}, bf16[512,256]{1,0:T(8,128)(2,1)S(1)}, bf16[512,256]{1,0:T(8,128)(...) custom-call(s32[8,128]{1,0:T(8,128)S(1)} %get-tuple-element.26.length_ref, ...), custom_call_target="tpu_custom_call" | custom-call | flops 20000000 | tf_op jit(solution)/shard_map/pallas_call | solution.py:324
  86.5 6.9 %shard_map.57 = (bf16[1024,512]{1,0:T(8,128)(2,1)}, bf16[512,1024]{1,0:T(8,128)(2,1)}, bf16[512,256]{1,0:T(8,128)(2,1)}, bf16[512,256]{1,0:T(8,128)(2,1)}, bf16[256,512]{1,0:T(8,128)(2,1)}, /*index=5*/f32[512,256]{1,0:T(8,128)}) custom-call(s32[8,128]{1,0:T(8,128)S(1)} %get-tuple-element.28.length_ref, bf16[512,512]{1,0:T(8,128)(2,1)} %get-tuple-element.27.p1, ...), custom_call_target="tpu_custom_call" | custom-call | flops 24000000 | tf_op jit(solution)/shard_map/pallas_call | solution.py:324
  93.4 9.4 %shard_map.58 = (bf16[512,512]{1,0:T(8,128)(2,1)S(1)}, bf16[1024,512]{1,0:T(8,128)(2,1)S(1)}, bf16[512,1024]{1,0:T(8,128)(2,1)S(1)}, bf16[1024,512]{1,0:T(8,128)(2,1)S(1)}, bf16[512,1024]{1,0:T(8,128)(2,1)S(1)}) custom-call(s32[8,128]{1,0:T(8,128)S(1)} %get-tuple-element.26.length_ref, bf16[512,512]{1,0:T(8,128)(2,1)S(1)} %collective-permute-done.p1, ...), custom_call_target="tpu_custom_call" | custom-call | flops 36000000 | tf_op jit(solution)/shard_map/pallas_call | solution.py:324
  102.8 3.6 %shard_map.60.refs_13_ = f32[512,256]{1,0:T(8,128)S(1)} custom-call(bf16[1024,512]{1,0:T(8,128)(2,1)S(1)} %get-tuple-element.35.k0.refs_0_, bf16[512,1024]{1,0:T(8,128)(2,1)S(1)} %get-tuple-element.36.v0.refs_1_, bf16[1024,512]{1,0:T(8,128)(2,1)S(1)} %get-tuple-element.37.k1.refs_2_, bf16[512,1024]{1,0:T(8,128)(2,1)S(1)} %get-tuple-element.38.v1.refs_3_, ...), custom_call_target="tpu_custom_call" | custom-call | flops 20000000 | tf_op jit(solution)/shard_map/pallas_call | solution.py:324
  106.4 10.4 %shard_map.61 = bf16[1024,512]{1,0:T(8,128)(2,1)S(1)} custom-call(s32[8,128]{1,0:T(8,128)S(1)} %get-tuple-element.26.length_ref, bf16[1024,512]{1,0:T(8,128)(2,1)S(1)} %get-tuple-element.35.k0.refs_0_, bf16[512,1024]{1,0:T(8,128)(2,1)S(1)} %get-tuple-element.36.v0.refs_1_, bf16[1024,512]{1,0:T(8,128)(2,1)S(1)} %get-tuple-element.37.k1.refs_2_, ...), custom_call_target="tpu_custom_call" | custom-call | flops 44000000 | tf_op jit(solution)/shard_map/pallas_call | solution.py:324
  116.8 21.9 %all_to_all.20 = bf16[16,64,512]{2,1,0:T(8,128)(2,1)S(1)} all-to-all(bf16[16,64,512]{2,1,0:T(8,128)(2,1)S(1)} %bitcast.27), channel_id=1, replica_groups=mesh['dp'=8,'xh'=2,'xl'=2,'yh'=2,'co'=2] {'xh','yh','xl','co'}, dimensions={0} | all-to-all | bytes 2097152 | tf_op jit(solution)/shard_map/all_to_all | solution.py:431
  138.7 1.0 copy.14
  (35 shorter events, 2.5 us)
Async XLA Ops:
  1.4 19.8 %all-to-all-start = ((s32[32,1,256]{2,1,0:T(1,128)}), s32[32,1,256]{2,1,0:T(1,128)S(1)}, u32[]{:S(2)}, u32[]{:S(2)}) async-start(s32[32,1,256]{2,1,0:T(1,128)} %broadcast_in_dim.64), calls=%async_computation | async-start | bytes 65536 | tf_op jit(solution)/shard_map/all_to_all | solution.py:381
  29.9 5.9 %copy-start.2 = (s32[4]{0:T(128)S(1)}, s32[4]{0:T(128)}, u32[]{:S(2)}) copy-start(s32[4]{0:T(128)} %param.6) | copy-start | bytes 52
  29.9 17.9 %all-to-all-start.2 = ((bf16[8,128,512]{2,1,0:T(8,128)(2,1)}), bf16[8,128,512]{2,1,0:T(8,128)(2,1)S(1)}, u32[]{:S(2)}, u32[]{:S(2)}) async-start(bf16[8,128,512]{2,1,0:T(8,128)(2,1)} %bitcast.31), calls=%async_computation.2 | async-start | bytes 2097152 | tf_op jit(solution)/shard_map/all_to_all | solution.py:400
  47.8 17.9 %all-to-all-start.1 = ((bf16[8,128,512]{2,1,0:T(8,128)(2,1)}), bf16[8,128,512]{2,1,0:T(8,128)(2,1)}, u32[]{:S(2)}, u32[]{:S(2)}) async-start(bf16[8,128,512]{2,1,0:T(8,128)(2,1)} %bitcast.32), calls=%async_computation.1 | async-start | bytes 2097152 | tf_op jit(solution)/shard_map/all_to_all | solution.py:400
  52.4 29.1 %copy-start = (bf16[512,2048]{1,0:T(8,128)(2,1)S(1)}, bf16[512,2048]{1,0:T(8,128)(2,1)}, u32[]{:S(2)}) copy-start(bf16[512,2048]{1,0:T(8,128)(2,1)} %refs_6_.1) | copy-start | bytes 6291460
  54.8 15.1 %collective-permute-start = (bf16[512,512]{1,0:T(8,128)(2,1)}, bf16[512,512]{1,0:T(8,128)(2,1)S(1)}, u32[]{:S(2)}, u32[]{:S(2)}) collective-permute-start(bf16[512,512]{1,0:T(8,128)(2,1)} %get-tuple-element.27.p1), channel_id=1, source_target_pairs={{0,4},{4,0},{1,5},{5,1},{2,6},{6,2},{3,7},{7,3},{8,12},{12,8},{9,1... | collective-permute-start | bytes 1572872 | tf_op jit(solution)/shard_map/ppermute | solution.py:415
  67.9 13.6 %collective-permute-start.3 = (bf16[512,512]{1,0:T(8,128)(2,1)S(1)}, bf16[512,512]{1,0:T(8,128)(2,1)S(1)}, u32[]{:S(2)}, u32[]{:S(2)}) collective-permute-start(bf16[512,512]{1,0:T(8,128)(2,1)S(1)} %get-tuple-element.39.p1), channel_id=1, source_target_pairs={{0,4},{4,0},{1,5},{5,1},{2,6},{6,2},{3,7},{7,3},{8,12},{12,8},{9,1... | collective-permute-start | bytes 1572872 | tf_op jit(solution)/shard_map/ppermute | solution.py:415
  69.4 12.1 %collective-permute-start.5 = (bf16[512,512]{1,0:T(8,128)(2,1)S(1)}, bf16[512,512]{1,0:T(8,128)(2,1)S(1)}, u32[]{:S(2)}, u32[]{:S(2)}) collective-permute-start(bf16[512,512]{1,0:T(8,128)(2,1)S(1)} %get-tuple-element.39.p1), channel_id=1, source_target_pairs={{0,1},{1,0},{2,3},{3,2},{4,5},{5,4},{6,7},{7,6},{8,9},{9,8},{10,11... | collective-permute-start | bytes 1572872 | tf_op jit(solution)/shard_map/ppermute | solution.py:416
  69.4 17.0 %collective-permute-start.2 = (bf16[512,512]{1,0:T(8,128)(2,1)}, bf16[512,512]{1,0:T(8,128)(2,1)S(1)}, u32[]{:S(2)}, u32[]{:S(2)}) collective-permute-start(bf16[512,512]{1,0:T(8,128)(2,1)} %get-tuple-element.27.p1), channel_id=1, source_target_pairs={{0,1},{1,0},{2,3},{3,2},{4,5},{5,4},{6,7},{7,6},{8,9},{9,8},{10,11... | collective-permute-start | bytes 1572872 | tf_op jit(solution)/shard_map/ppermute | solution.py:416
  70.0 23.4 %collective-permute-start.1 = (bf16[512,512]{1,0:T(8,128)(2,1)S(1)}, bf16[512,512]{1,0:T(8,128)(2,1)S(1)}, u32[]{:S(2)}, u32[]{:S(2)}) collective-permute-start(bf16[512,512]{1,0:T(8,128)(2,1)S(1)} %collective-permute-done.p1), channel_id=1, source_target_pairs={{0,1},{1,0},{2,3},{3,2},{4,5},{5,4},{6,7},{7,6},{8,9},{9,8},{10,11... | collective-permute-start | bytes 1572872 | tf_op jit(solution)/shard_map/ppermute | solution.py:417
  81.5 24.8 %collective-permute-start.4 = (bf16[512,512]{1,0:T(8,128)(2,1)S(1)}, bf16[512,512]{1,0:T(8,128)(2,1)S(1)}, u32[]{:S(2)}, u32[]{:S(2)}) collective-permute-start(bf16[512,512]{1,0:T(8,128)(2,1)S(1)} %collective-permute-done.3.refs_4_), channel_id=1, source_target_pairs={{0,1},{1,0},{2,3},{3,2},{4,5},{5,4},{6,7},{7,6},{8,9},{9,8},{10,11... | collective-permute-start | bytes 1572872 | tf_op jit(solution)/shard_map/ppermute | solution.py:417
  86.4 6.9 %copy-start.1 = (bf16[512,512]{1,0:T(8,128)(2,1)S(1)}, bf16[512,512]{1,0:T(8,128)(2,1)}, u32[]{:S(2)}) copy-start(bf16[512,512]{1,0:T(8,128)(2,1)} %refs_7_.1) | copy-start | bytes 1572868

commit v10 on v9

--- a/solution.py
+++ b/solution.py
@@ -231,12 +231,12 @@
     lax.fori_loop(0, 4 // together, heads, 0)
 
 
-def near0_kernel(length_ref, p1, p2, w_ref, *refs):
+def early_kernel(side, length_ref, p1, p2, w_ref, *refs):
     sc_ref = scalars(length_ref)
     outs, held, (n_scr, nq_scr, sems) = refs[:6], refs[6:12], refs[12:]
     k, v, q, g, x, o = held
     copies = [pltpu.make_async_copy(src, dst, sems.at[i]) for i, (src, dst) in enumerate(zip(held, outs))]
-    project(0, 0, sc_ref, (p1, p2), w_ref, k, v, q, g, x, n_scr, nq_scr)
+    project(0, side, sc_ref, (p1, p2), w_ref, k, v, q, g, x, n_scr, nq_scr)
     for c in copies[:5]:
         c.start()
     attend(sc_ref, [(q, o, [(k, v, True)])], 2)
@@ -245,10 +245,33 @@
         c.wait()
 
 
-def near1_kernel(length_ref, p1, p2, w_ref, k_ref, v_ref, q_ref, g_ref, x_ref, o_ref, n_scr, nq_scr):
+def middle_kernel(length_ref, p1, p2, w_ref, wo_hbm, *refs):
     sc_ref = scalars(length_ref)
-    project(2 * GRP, 0, sc_ref, (p1, p2), w_ref, k_ref, v_ref, q_ref, g_ref, x_ref, n_scr, nq_scr)
-    attend(sc_ref, [(q_ref, o_ref, [(k_ref, v_ref, True)])], 2)
+    sent, (k1, v1, q1, g1, x1, o1), refs = refs[:12], refs[12:18], refs[18:]
+    (out_ref, kn, vn, kf, vf), refs = refs[:5], refs[5:]
+    qn, gn, xn, on, qf, gf, xf, of, wo_ref, qx, kx, vx, ox, n_scr, nq_scr, sems = refs
+    landed = (kn, vn, qn, gn, xn, on, kf, vf, qf, gf, xf, of, wo_ref)
+    copies = [pltpu.make_async_copy(src, dst, sems.at[i]) for i, (src, dst) in enumerate(zip((*sent, wo_hbm), landed))]
+    for c in copies:
+        c.start()
+    project(2 * GRP, 0, sc_ref, (p1, p2), w_ref, k1, v1, q1, g1, x1, n_scr, nq_scr)
+    for c in copies:
+        c.wait()
+    cross(sc_ref, (qn, kn, vn), (qf, kf, vf), (qx, kx, vx))
+    attend(sc_ref, [(q1, o1, [(k1, v1, True)]), (qx, ox, [(kx, vx, False)])], 2)
+    finish(0, sc_ref, wo_ref, ox, ((on, gn, xn), (of, gf, xf)), out_ref)
+
+
+def cross(sc_ref, near, far, to):
+    low = sc_ref[3] == 0
+
+    @pl.when(low)
+    def _():
+        to[0][...], to[1][...], to[2][...] = far[0][...], near[1][...], near[2][...]
+
+    @pl.when(jnp.logical_not(low))
+    def _():
+        to[0][...], to[1][...], to[2][...] = near[0][...], far[1][...], far[2][...]
 
 
 def past_kernel(k0, v0, k1, v1, q_ref, before_ref, o_ref):
@@ -270,44 +293,20 @@
             out_ref[pl.ds(at, 128), :] = out[128 * j : 128 * (j + 1)]
 
 
-def far_core(chunk, sc_ref, past, p1, p2, w_ref, wo_ref, kept, arrive, out_ref, kf, vf, scratch):
-    n_scr, nq_scr, qf, gf, xf, of, qx, kx, vx, ox = scratch
-    kn, vn, qn, gn, xn, on = kept
-    project(2 * GRP * chunk, 1, sc_ref, (p1, p2), w_ref, kf, vf, qf, gf, xf, n_scr, nq_scr)
-    for c in arrive:
-        c.wait()
-    low = sc_ref[3] == 0
-
-    @pl.when(low)
-    def _():
-        qx[...], kx[...], vx[...] = qf[...], kn[...], vn[...]
-
-    @pl.when(jnp.logical_not(low))
-    def _():
-        qx[...], kx[...], vx[...] = qn[...], kf[...], vf[...]
-
-    seen = [(past[2 * i], past[2 * i + 1], False) for i in range(2 * chunk)]
-    attend(sc_ref, [(qf, of, seen + [(kf, vf, True)]), (qx, ox, [(kx, vx, False)])], 2)
-    finish(chunk, sc_ref, wo_ref, ox, ((on, gn, xn), (of, gf, xf)), out_ref)
-
-
-def far0_kernel(length_ref, p1, p2, w_ref, wo_ref, *refs):
-    sc_ref = scalars(length_ref)
-    sent, (out_ref, kn, vn, kf, vf), rest = refs[:6], refs[6:11], refs[11:]
-    kept = (kn, vn, *rest[:4])
-    sems = rest[-1]
-    arrive = [pltpu.make_async_copy(src, dst, sems.at[i]) for i, (src, dst) in enumerate(zip(sent, kept))]
-    for c in arrive:
-        c.start()
-    far_core(0, sc_ref, (), p1, p2, w_ref, wo_ref, kept, arrive, out_ref, kf, vf, rest[4:-1])
-
-
 def far1_kernel(length_ref, *refs):
     sc_ref = scalars(length_ref)
-    past, (p1, p2, w_ref, wo_ref), kept = refs[:4], refs[4:8], refs[8:14]
+    past, (p1, p2, w_ref, wo_hbm), kept = refs[:4], refs[4:8], refs[8:14]
     first_ref, out_ref = refs[14:16]
-    scratch, (kf, vf) = refs[16:26], refs[26:]
-    far_core(1, sc_ref, past, p1, p2, w_ref, wo_ref, kept, (), out_ref, kf, vf, scratch)
+    n_scr, nq_scr, qf, gf, xf, of, qx, kx, vx, ox, kf, vf, wo_ref, sem = refs[16:]
+    kn, vn, qn, gn, xn, on = kept
+    copy = pltpu.make_async_copy(wo_hbm, wo_ref, sem)
+    copy.start()
+    project(2 * GRP, 1, sc_ref, (p1, p2), w_ref, kf, vf, qf, gf, xf, n_scr, nq_scr)
+    copy.wait()
+    cross(sc_ref, (qn, kn, vn), (qf, kf, vf), (qx, kx, vx))
+    seen = [(past[0], past[1], False), (past[2], past[3], False)]
+    attend(sc_ref, [(qf, of, seen + [(kf, vf, True)]), (qx, ox, [(kx, vx, False)])], 2)
+    finish(1, sc_ref, wo_ref, ox, ((on, gn, xn), (of, gf, xf)), out_ref)
     out_ref[:512, :] = first_ref[...]
 
 
@@ -332,34 +331,33 @@
     )(*inputs)
 
 
-def near0_call(length, own, near, w_in):
+def early_call(side, length, p1, p2, w_in):
     shapes = [pltpu.HBM(s, BF) for s in SIZES] + [pltpu.HBM((D, 256), F32)]
     scratch = held() + [SUMS] + PROJECT + [pltpu.SemaphoreType.DMA((6,))]
-    return call(near0_kernel, 6, (length, own, near, w_in), [VM] * 4, shapes, [HBM] * 6, scratch)
-
-
-def near1_call(length, own, near, w_in):
-    return call(near1_kernel, 5, (length, own, near, w_in), [VM] * 4, held() + [SUMS], [VM] * 6, PROJECT)
+    kernel = functools.partial(early_kernel, side)
+    return call(kernel, 6, (length, p1, p2, w_in), [VM] * 4, shapes, [HBM] * 6, scratch)
+
+
+SQUARE = pltpu.VMEM((D, D), BF)
+CROSS = [pltpu.VMEM((D, 256), BF)] + held(slice(0, 2)) + [SUMS]
+
+
+def middle_call(length, own, near, w_in, w_out, sent):
+    shapes = held() + [SUMS, SQUARE] + held(slice(0, 2)) * 2
+    scratch = (held(slice(2, 5)) + [SUMS]) * 2 + [SQUARE] + CROSS + PROJECT + [pltpu.SemaphoreType.DMA((13,))]
+    inputs = (length, own, near, w_in, w_out, *sent)
+    return call(middle_kernel, 9, inputs, [VM] * 4 + [HBM] * 13, shapes, [VM] * 11, scratch)
 
 
 def past_call(past, q, before):
     return call(past_kernel, 5, (*past, q, before), [VM] * 6, SUMS, VM, [])
 
 
-FAR = PROJECT + held(slice(2, 5)) + [SUMS, pltpu.VMEM((D, 256), BF)] + held(slice(0, 2)) + [SUMS]
-
-
-def far0_call(length, far, diag, w_in, w_out, sent):
-    shapes = [pltpu.VMEM((512, D), BF)] + held(slice(0, 2)) * 2
-    scratch = held(slice(2, 5)) + [SUMS] + FAR + [pltpu.SemaphoreType.DMA((6,))]
-    inputs = (length, far, diag, w_in, w_out, *sent)
-    return call(far0_kernel, 9, inputs, [VM] * 5 + [HBM] * 6, shapes, [VM] * 5, scratch)
-
-
 def far1_call(length, past, far, diag, w_in, w_out, kept, first):
     inputs = (length, *past, far, diag, w_in, w_out, *kept, first)
-    shape = jax.ShapeDtypeStruct((1024, D), BF)
-    return call(far1_kernel, 11, inputs, [VM] * 16, shape, VM, FAR + held(slice(0, 2)))
+    specs = [VM] * 8 + [HBM] + [VM] * 7
+    scratch = PROJECT + held(slice(2, 5)) + [SUMS] + CROSS + held(slice(0, 2)) + [SQUARE, pltpu.SemaphoreType.DMA]
+    return call(far1_kernel, 11, inputs, specs, jax.ShapeDtypeStruct((1024, D), BF), VM, scratch)
 
 
 from jax.sharding import Mesh
@@ -374,7 +372,8 @@
     me = lax.axis_index("dp")
     xh, _, yh, _ = (lax.axis_index(a) for a in CTX)
     owners = lax.axis_size("dp")
-    w_in, w_out = in_vmem(w_in), in_vmem(w_out)
+    w_in = in_vmem(w_in)
+    w_out = pltpu.with_memory_space_constraint(w_out, pltpu.HBM)
     groups = table.reshape(-1, 8, D)
 
     send = jnp.broadcast_to(item_ids[None, :, None], (owners, 4, 1, BLK)).reshape(owners * 4, 1, BLK)
@@ -417,14 +416,13 @@
         diag = lax.ppermute(far, "co", FLIP)
         own, near, far, diag, kept_length = vmem_all((own, near, far, diag, kept_length))
         if c == 0:
-            sent = near0_call(kept_length, own, near, w_in)
+            sent = early_call(0, kept_length, own, near, w_in)
+            sent += early_call(1, kept_length, far, diag, w_in)
             sent = [pltpu.with_memory_space_constraint(a, pltpu.HBM) for a in sent]
-            far0, diag0 = far, diag
         else:
-            done = far0_call(kept_length, far0, diag0, w_in, w_out, sent)
-            first, *past = vmem_all(done)
-            kept = near1_call(kept_length, own, near, w_in)
-            kept = vmem_all(kept)
+            done = middle_call(kept_length, own, near, w_in, w_out, sent)
+            done = vmem_all(done)
+            kept, first, past = done[:6], done[6], done[7:]
             total = past_call(past, kept[2], kept[5])
             kept[5] = in_vmem(total)
             out = far1_call(kept_length, past, far, diag, w_in, w_out, kept, first)

time: 141 us -> 144 us (1.021)
  Pallas kernels: 53.5 us -> 56 us
    pallas_call x5, Pallas kernels: 35.1 us -> 37.6 us  [call(): pl.pallas_call(kernel, out_shape=out_shape, in_specs=in_specs, out_specs=...]
  transfers between devices with their start and end apart: 9 -> 9, of which waited for: 4 -> 4; matrix products, arithmetic and copies ran while one was open for 1% -> 1% of each run, Pallas kernels for 26% -> 27%
where the time goes in v10:
time: 144 us; the launch traced here: 142 us
  Pallas kernels  56 us (39%)
  waiting for transfers between devices  33.3 us (23%)
  starting transfers between devices  24.4 us (17%)
  blocking collectives  21.9 us (15%)
  other arithmetic  2.86 us (2%)
  local copies, waits for them, and re-layouts  2.38 us (2%)
    pallas_call x5, Pallas kernels, call(): pl.pallas_call(kernel, out_shape=out_shape, in_specs=in_specs, out_specs=...  37.6 us
    all_to_all x1, blocking collectives, layer(): lax.all_to_all(out.reshape(16, PART, D), ('xh', 'yh', 'xl', 'co'), 0, 0,...  21.9 us
    pallas_call x2, Pallas kernels, gather_call(): pl.pallas_call(functools.partial(gather_kernel, owners, outs), out_shape=...  14.4 us
    all_to_all x2, waiting for transfers between devices, fetch(): lax.all_to_all(picked, 'dp', 0, 0, tiled=True).reshape(owners * CAP, D)  13 us
    ppermute x2, waiting for transfers between devices, layer(): far = lax.ppermute(own, 'xl', FLIP)  11.6 us
    all_to_all x1, starting transfers between devices, layer(): wanted = lax.all_to_all(send, ('dp', 'xh', 'yh'), 0, 0, tiled=True)  11 us
    all_to_all x2, starting transfers between devices, fetch(): lax.all_to_all(picked, 'dp', 0, 0, tiled=True).reshape(owners * CAP, D)  10.6 us
    all_to_all x1, waiting for transfers between devices, layer(): wanted = lax.all_to_all(send, ('dp', 'xh', 'yh'), 0, 0, tiled=True)  8.74 us
  transfers between devices with their start and end apart: 9, of which 4 were waited for; matrix products, arithmetic and copies ran while one was open for 1% of the time, Pallas kernels for 27%

profile of v10, /device:TPU:8, one launch (start us, length us, event | category | flops | bytes accessed | tf_op | source)
XLA Modules:
  0.0 142.1 jit_solution(7074534067286164880)
XLA Ops:
  0.0 0.7 broadcast_in_dim.63
  1.4 11.0 %all-to-all-start = ((s32[32,1,256]{2,1,0:T(1,128)}), s32[32,1,256]{2,1,0:T(1,128)S(1)}, u32[]{:S(2)}, u32[]{:S(2)}) async-start(s32[32,1,256]{2,1,0:T(1,128)} %broadcast_in_dim.64), calls=%async_computation | async-start | bytes 65536 | tf_op jit(solution)/shard_map/all_to_all | solution.py:380
  12.4 8.7 %all-to-all-done = s32[32,1,256]{2,1,0:T(1,128)S(1)} async-done(((s32[32,1,256]{2,1,0:T(1,128)}), s32[32,1,256]{2,1,0:T(1,128)S(1)}, u32[]{:S(2)}, u32[]{:S(2)}) %all-to-all-start) | async-done | bytes 32800 | tf_op jit(solution)/shard_map/all_to_all | solution.py:380
  21.3 0.9 fusion.28
  22.4 0.9 select_reduce_fusion.rows_ref.ids_ref
  23.3 6.6 %shard_map.56 = bf16[1024,512]{1,0:T(8,128)(2,1)} custom-call(s32[8,128]{1,0:T(8,128)} %select_reduce_fusion.rows_ref.ids_ref, s32[8]{0:T(128)} %get-tuple-element.59.count_ref, s32[8,128]{1,0:T(8,128)} %select_reduce_fusion.rows_ref.ids_ref, bf16[2048,8,512]{2,1,0:T(8,128)(2,1)} %bitcast.29), custom_call_target="tpu_custom_call" | custom-call | flops 28000000 | tf_op jit(solution)/shard_map/pallas_call | solution.py:105
  29.9 5.9 %all-to-all-start.2 = ((bf16[8,128,512]{2,1,0:T(8,128)(2,1)}), bf16[8,128,512]{2,1,0:T(8,128)(2,1)S(1)}, u32[]{:S(2)}, u32[]{:S(2)}) async-start(bf16[8,128,512]{2,1,0:T(8,128)(2,1)} %bitcast.31), calls=%async_computation.2 | async-start | bytes 2097152 | tf_op jit(solution)/shard_map/all_to_all | solution.py:399
  36.2 0.9 select_reduce_fusion.1.rows_ref.ids_ref
  37.0 7.9 %shard_map.55 = bf16[1024,512]{1,0:T(8,128)(2,1)} custom-call(s32[8,128]{1,0:T(8,128)} %select_reduce_fusion.1.rows_ref.ids_ref, s32[8]{0:T(128)} %get-tuple-element.60.count_ref, s32[8,128]{1,0:T(8,128)} %select_reduce_fusion.1.rows_ref.ids_ref, bf16[2048,8,512]{2,1,0:T(8,128)(2,1)} %bitcast.30), custom_call_target="tpu_custom_call" | custom-call | flops 28000000 | tf_op jit(solution)/shard_map/pallas_call | solution.py:105
  44.9 2.9 %all-to-all-done.2 = bf16[8,128,512]{2,1,0:T(8,128)(2,1)S(1)} async-done(((bf16[8,128,512]{2,1,0:T(8,128)(2,1)}), bf16[8,128,512]{2,1,0:T(8,128)(2,1)S(1)}, u32[]{:S(2)}, u32[]{:S(2)}) %all-to-all-start.2) | async-done | bytes 1048608 | tf_op jit(solution)/shard_map/all_to_all | solution.py:399
  47.8 4.7 %all-to-all-start.1 = ((bf16[8,128,512]{2,1,0:T(8,128)(2,1)}), bf16[8,128,512]{2,1,0:T(8,128)(2,1)}, u32[]{:S(2)}, u32[]{:S(2)}) async-start(bf16[8,128,512]{2,1,0:T(8,128)(2,1)} %bitcast.32), calls=%async_computation.1 | async-start | bytes 2097152 | tf_op jit(solution)/shard_map/all_to_all | solution.py:399
  53.0 1.8 %place.3 = (bf16[512,512]{1,0:T(8,128)(2,1)}, s32[8,128]{1,0:T(8,128)S(1)}) custom-call(s32[1,512]{1,0:T(1,128)S(1)} %multiply_add_fusion.at_ref, s32[8,128]{1,0:T(8,128)S(1)} %select_reduce_fusion.2.length_ref, bf16[1024,512]{1,0:T(8,128)(2,1)S(1)} %bitcast.28), custom_call_target="tpu_custom_call" | custom-call | flops 6000000 | tf_op jit(solution)/shard_map/place/pallas_call | solution.py:125
  54.8 0.7 collective-permute-start.2
  55.6 10.1 %all-to-all-done.1 = bf16[8,128,512]{2,1,0:T(8,128)(2,1)} async-done(((bf16[8,128,512]{2,1,0:T(8,128)(2,1)}), bf16[8,128,512]{2,1,0:T(8,128)(2,1)}, u32[]{:S(2)}, u32[]{:S(2)}) %all-to-all-start.1) | async-done | bytes 1048608 | tf_op jit(solution)/shard_map/all_to_all | solution.py:399
  65.7 2.2 %place.2 = (bf16[512,512]{1,0:T(8,128)(2,1)S(1)}, s32[8,128]{1,0:T(8,128)S(1)}) custom-call(s32[1,512]{1,0:T(1,128)S(1)} %multiply_add_fusion.1.at_ref, s32[8,128]{1,0:T(8,128)S(1)} %select_reduce_fusion.2.length_ref, bf16[1024,512]{1,0:T(8,128)(2,1)} %bitcast.3.got_ref), custom_call_target="tpu_custom_call" | custom-call | flops 6000000 | tf_op jit(solution)/shard_map/place/pallas_call | solution.py:125
  67.9 1.5 %collective-permute-start.4 = (bf16[512,512]{1,0:T(8,128)(2,1)S(1)}, bf16[512,512]{1,0:T(8,128)(2,1)S(1)}, u32[]{:S(2)}, u32[]{:S(2)}) collective-permute-start(bf16[512,512]{1,0:T(8,128)(2,1)S(1)} %get-tuple-element.33.p1), channel_id=1, source_target_pairs={{0,4},{4,0},{1,5},{5,1},{2,6},{6,2},{3,7},{7,3},{8,12},{12,8},{9,1... | collective-permute-start | bytes 1572872 | tf_op jit(solution)/shard_map/ppermute | solution.py:414
  70.0 11.6 %collective-permute-done.4.refs_4_ = bf16[512,512]{1,0:T(8,128)(2,1)S(1)} collective-permute-done((bf16[512,512]{1,0:T(8,128)(2,1)S(1)}, bf16[512,512]{1,0:T(8,128)(2,1)S(1)}, u32[]{:S(2)}, u32[]{:S(2)}) %collective-permute-start.4) | collective-permute-done | bytes 524320 | tf_op jit(solution)/shard_map/ppermute | solution.py:414
  81.6 6.8 %shard_map.57 = (bf16[1024,512]{1,0:T(8,128)(2,1)}, bf16[512,1024]{1,0:T(8,128)(2,1)}, bf16[512,256]{1,0:T(8,128)(2,1)}, bf16[512,256]{1,0:T(8,128)(2,1)}, bf16[256,512]{1,0:T(8,128)(2,1)}, /*index=5*/f32[512,256]{1,0:T(8,128)}) custom-call(s32[8,128]{1,0:T(8,128)S(1)} %get-tuple-element.34.length_ref, bf16[512,512]{1,0:T(8,128)(2,1)} %get-tuple-element.35.p1, ...), custom_call_target="tpu_custom_call" | custom-call | flops 24000000 | tf_op jit(solution)/shard_map/pallas_call | solution.py:323
  88.4 5.8 %shard_map.58 = (bf16[1024,512]{1,0:T(8,128)(2,1)}, bf16[512,1024]{1,0:T(8,128)(2,1)}, bf16[512,256]{1,0:T(8,128)(2,1)}, bf16[512,256]{1,0:T(8,128)(2,1)}, bf16[256,512]{1,0:T(8,128)(2,1)}, /*index=5*/f32[512,256]{1,0:T(8,128)}) custom-call(s32[8,128]{1,0:T(8,128)S(1)} %get-tuple-element.34.length_ref, bf16[512,512]{1,0:T(8,128)(2,1)S(1)} %collective-permute-done.2.p1, ...), custom_call_target="tpu_custom_call" | custom-call | flops 24000000 | tf_op jit(solution)/shard_map/pallas_call | solution.py:323
  94.2 10.3 %shard_map.59 = (bf16[1024,512]{1,0:T(8,128)(2,1)S(1)}, bf16[512,1024]{1,0:T(8,128)(2,1)S(1)}, bf16[512,256]{1,0:T(8,128)(2,1)S(1)}, bf16[512,256]{1,0:T(8,128)(...) custom-call(s32[8,128]{1,0:T(8,128)S(1)} %get-tuple-element.32.lengt, ...), custom_call_target="tpu_custom_call" | custom-call | flops 36000000 | tf_op jit(solution)/shard_map/pallas_call | solution.py:323
  104.5 3.6 %shard_map.60.refs_13_ = f32[512,256]{1,0:T(8,128)S(1)} custom-call(bf16[1024,512]{1,0:T(8,128)(2,1)S(1)} %get-tuple-element.48.k0.refs_0_, bf16[512,1024]{1,0:T(8,128)(2,1)S(1)} %get-tuple-element.49.v0.refs_1_, bf16[1024,512]{1,0:T(8,128)(2,1)S(1)} %get-tuple-element.50.k1.refs_2_, bf16[512,1024]{1,0:T(8,128)(2,1)S(1)} %get-tuple-element.51.v1.refs_3_, ...), custom_call_target="tpu_custom_call" | custom-call | flops 20000000 | tf_op jit(solution)/shard_map/pallas_call | solution.py:323
  108.1 11.1 %shard_map.61 = bf16[1024,512]{1,0:T(8,128)(2,1)S(1)} custom-call(s32[8,128]{1,0:T(8,128)S(1)} %get-tuple-element.32.length_ref, bf16[1024,512]{1,0:T(8,128)(2,1)S(1)} %get-tuple-element.48.k0.refs_0_, bf16[512,1024]{1,0:T(8,128)(2,1)S(1)} %get-tuple-element.49.v0.refs_1_, bf16[1024,512]{1,0:T(8,128)(2,1)S(1)} %get-tuple-element.50.k1.refs_2_, ...), custom_call_target="tpu_custom_call" | custom-call | flops 44000000 | tf_op jit(solution)/shard_map/pallas_call | solution.py:323
  119.2 21.9 %all_to_all.20 = bf16[16,64,512]{2,1,0:T(8,128)(2,1)S(1)} all-to-all(bf16[16,64,512]{2,1,0:T(8,128)(2,1)S(1)} %bitcast.27), channel_id=1, replica_groups=mesh['dp'=8,'xh'=2,'xl'=2,'yh'=2,'co'=2] {'xh','yh','xl','co'}, dimensions={0} | all-to-all | bytes 2097152 | tf_op jit(solution)/shard_map/all_to_all | solution.py:429
  141.2 1.0 copy.14
  (33 shorter events, 2.5 us)
Async XLA Ops:
  1.4 19.8 %all-to-all-start = ((s32[32,1,256]{2,1,0:T(1,128)}), s32[32,1,256]{2,1,0:T(1,128)S(1)}, u32[]{:S(2)}, u32[]{:S(2)}) async-start(s32[32,1,256]{2,1,0:T(1,128)} %broadcast_in_dim.64), calls=%async_computation | async-start | bytes 65536 | tf_op jit(solution)/shard_map/all_to_all | solution.py:380
  29.9 5.9 %copy-start.1 = (s32[4]{0:T(128)S(1)}, s32[4]{0:T(128)}, u32[]{:S(2)}) copy-start(s32[4]{0:T(128)} %param.6) | copy-start | bytes 52
  29.9 17.9 %all-to-all-start.2 = ((bf16[8,128,512]{2,1,0:T(8,128)(2,1)}), bf16[8,128,512]{2,1,0:T(8,128)(2,1)S(1)}, u32[]{:S(2)}, u32[]{:S(2)}) async-start(bf16[8,128,512]{2,1,0:T(8,128)(2,1)} %bitcast.31), calls=%async_computation.2 | async-start | bytes 2097152 | tf_op jit(solution)/shard_map/all_to_all | solution.py:399
  47.8 17.9 %all-to-all-start.1 = ((bf16[8,128,512]{2,1,0:T(8,128)(2,1)}), bf16[8,128,512]{2,1,0:T(8,128)(2,1)}, u32[]{:S(2)}, u32[]{:S(2)}) async-start(bf16[8,128,512]{2,1,0:T(8,128)(2,1)} %bitcast.32), calls=%async_computation.1 | async-start | bytes 2097152 | tf_op jit(solution)/shard_map/all_to_all | solution.py:399
  52.4 29.1 %copy-start = (bf16[512,2048]{1,0:T(8,128)(2,1)S(1)}, bf16[512,2048]{1,0:T(8,128)(2,1)}, u32[]{:S(2)}) copy-start(bf16[512,2048]{1,0:T(8,128)(2,1)} %refs_6_.1) | copy-start | bytes 6291460
  54.8 14.6 %collective-permute-start.2 = (bf16[512,512]{1,0:T(8,128)(2,1)}, bf16[512,512]{1,0:T(8,128)(2,1)S(1)}, u32[]{:S(2)}, u32[]{:S(2)}) collective-permute-start(bf16[512,512]{1,0:T(8,128)(2,1)} %get-tuple-element.35.p1), channel_id=1, source_target_pairs={{0,4},{4,0},{1,5},{5,1},{2,6},{6,2},{3,7},{7,3},{8,12},{12,8},{9,1... | collective-permute-start | bytes 1572872 | tf_op jit(solution)/shard_map/ppermute | solution.py:414
  67.9 13.6 %collective-permute-start.4 = (bf16[512,512]{1,0:T(8,128)(2,1)S(1)}, bf16[512,512]{1,0:T(8,128)(2,1)S(1)}, u32[]{:S(2)}, u32[]{:S(2)}) collective-permute-start(bf16[512,512]{1,0:T(8,128)(2,1)S(1)} %get-tuple-element.33.p1), channel_id=1, source_target_pairs={{0,4},{4,0},{1,5},{5,1},{2,6},{6,2},{3,7},{7,3},{8,12},{12,8},{9,1... | collective-permute-start | bytes 1572872 | tf_op jit(solution)/shard_map/ppermute | solution.py:414
  69.4 12.1 %collective-permute-start.1 = (bf16[512,512]{1,0:T(8,128)(2,1)}, bf16[512,512]{1,0:T(8,128)(2,1)S(1)}, u32[]{:S(2)}, u32[]{:S(2)}) collective-permute-start(bf16[512,512]{1,0:T(8,128)(2,1)} %get-tuple-element.35.p1), channel_id=1, source_target_pairs={{0,1},{1,0},{2,3},{3,2},{4,5},{5,4},{6,7},{7,6},{8,9},{9,8},{10,11... | collective-permute-start | bytes 1572872 | tf_op jit(solution)/shard_map/ppermute | solution.py:415
  69.4 18.9 %collective-permute-start.3 = (bf16[512,512]{1,0:T(8,128)(2,1)S(1)}, bf16[512,512]{1,0:T(8,128)(2,1)S(1)}, u32[]{:S(2)}, u32[]{:S(2)}) collective-permute-start(bf16[512,512]{1,0:T(8,128)(2,1)S(1)} %collective-permute-done.2.p1), channel_id=1, source_target_pairs={{0,1},{1,0},{2,3},{3,2},{4,5},{5,4},{6,7},{7,6},{8,9},{9,8},{10,11... | collective-permute-start | bytes 1572872 | tf_op jit(solution)/shard_map/ppermute | solution.py:416
  70.0 24.2 %collective-permute-start = (bf16[512,512]{1,0:T(8,128)(2,1)S(1)}, bf16[512,512]{1,0:T(8,128)(2,1)S(1)}, u32[]{:S(2)}, u32[]{:S(2)}) collective-permute-start(bf16[512,512]{1,0:T(8,128)(2,1)S(1)} %get-tuple-element.33.p1), channel_id=1, source_target_pairs={{0,1},{1,0},{2,3},{3,2},{4,5},{5,4},{6,7},{7,6},{8,9},{9,8},{10,11... | collective-permute-start | bytes 1572872 | tf_op jit(solution)/shard_map/ppermute | solution.py:415
  81.5 26.6 %collective-permute-start.5 = (bf16[512,512]{1,0:T(8,128)(2,1)S(1)}, bf16[512,512]{1,0:T(8,128)(2,1)S(1)}, u32[]{:S(2)}, u32[]{:S(2)}) collective-permute-start(bf16[512,512]{1,0:T(8,128)(2,1)S(1)} %collective-permute-done.4.refs_4_), channel_id=1, source_target_pairs={{0,1},{1,0},{2,3},{3,2},{4,5},{5,4},{6,7},{7,6},{8,9},{9,8},{10,11... | collective-permute-start | bytes 1572872 | tf_op jit(solution)/shard_map/ppermute | solution.py:416

commit v11 on v10

--- a/solution.py
+++ b/solution.py
@@ -295,14 +295,11 @@
 
 def far1_kernel(length_ref, *refs):
     sc_ref = scalars(length_ref)
-    past, (p1, p2, w_ref, wo_hbm), kept = refs[:4], refs[4:8], refs[8:14]
+    past, (p1, p2, w_ref, wo_ref), kept = refs[:4], refs[4:8], refs[8:14]
     first_ref, out_ref = refs[14:16]
-    n_scr, nq_scr, qf, gf, xf, of, qx, kx, vx, ox, kf, vf, wo_ref, sem = refs[16:]
+    n_scr, nq_scr, qf, gf, xf, of, qx, kx, vx, ox, kf, vf = refs[16:]
     kn, vn, qn, gn, xn, on = kept
-    copy = pltpu.make_async_copy(wo_hbm, wo_ref, sem)
-    copy.start()
     project(2 * GRP, 1, sc_ref, (p1, p2), w_ref, kf, vf, qf, gf, xf, n_scr, nq_scr)
-    copy.wait()
     cross(sc_ref, (qn, kn, vn), (qf, kf, vf), (qx, kx, vx))
     seen = [(past[0], past[1], False), (past[2], past[3], False)]
     attend(sc_ref, [(qf, of, seen + [(kf, vf, True)]), (qx, ox, [(kx, vx, False)])], 2)
@@ -355,9 +352,8 @@
 
 def far1_call(length, past, far, diag, w_in, w_out, kept, first):
     inputs = (length, *past, far, diag, w_in, w_out, *kept, first)
-    specs = [VM] * 8 + [HBM] + [VM] * 7
-    scratch = PROJECT + held(slice(2, 5)) + [SUMS] + CROSS + held(slice(0, 2)) + [SQUARE, pltpu.SemaphoreType.DMA]
-    return call(far1_kernel, 11, inputs, specs, jax.ShapeDtypeStruct((1024, D), BF), VM, scratch)
+    scratch = PROJECT + held(slice(2, 5)) + [SUMS] + CROSS + held(slice(0, 2))
+    return call(far1_kernel, 11, inputs, [VM] * 16, jax.ShapeDtypeStruct((1024, D), BF), VM, scratch)
 
 
 from jax.sharding import Mesh
@@ -373,7 +369,7 @@
     xh, _, yh, _ = (lax.axis_index(a) for a in CTX)
     owners = lax.axis_size("dp")
     w_in = in_vmem(w_in)
-    w_out = pltpu.with_memory_space_constraint(w_out, pltpu.HBM)
+    w_out, w_far = pltpu.with_memory_space_constraint(w_out, pltpu.HBM), in_vmem(w_out)
     groups = table.reshape(-1, 8, D)
 
     send = jnp.broadcast_to(item_ids[None, :, None], (owners, 4, 1, BLK)).reshape(owners * 4, 1, BLK)
@@ -425,7 +421,7 @@
             kept, first, past = done[:6], done[6], done[7:]
             total = past_call(past, kept[2], kept[5])
             kept[5] = in_vmem(total)
-            out = far1_call(kept_length, past, far, diag, w_in, w_out, kept, first)
+            out = far1_call(kept_length, past, far, diag, w_in, w_far, kept, first)
     back = lax.all_to_all(out.reshape(16, PART, D), ("xh", "yh", "xl", "co"), 0, 0, tiled=True)
     return back.reshape(4, BLK, D)
 

time: 144 us -> 143 us (level)
  no operation moved by 1% of the time
where the time goes in v11:
time: 143 us; the launch traced here: 141 us
  Pallas kernels  55.3 us (39%)
  waiting for transfers between devices  33.3 us (23%)
  starting transfers between devices  24.4 us (17%)
  blocking collectives  21.9 us (15%)
  other arithmetic  2.86 us (2%)
  local copies, waits for them, and re-layouts  2.38 us (2%)
    pallas_call x5, Pallas kernels, call(): pl.pallas_call(kernel, out_shape=out_shape, in_specs=in_specs, out_specs=...  36.9 us
    all_to_all x1, blocking collectives, layer(): lax.all_to_all(out.reshape(16, PART, D), ('xh', 'yh', 'xl', 'co'), 0, 0,...  21.9 us
    pallas_call x2, Pallas kernels, gather_call(): pl.pallas_call(functools.partial(gather_kernel, owners, outs), out_shape=...  14.4 us
    all_to_all x2, waiting for transfers between devices, fetch(): lax.all_to_all(picked, 'dp', 0, 0, tiled=True).reshape(owners * CAP, D)  13 us
    ppermute x2, waiting for transfers between devices, layer(): far = lax.ppermute(own, 'xl', FLIP)  11.6 us
    all_to_all x1, starting transfers between devices, layer(): wanted = lax.all_to_all(send, ('dp', 'xh', 'yh'), 0, 0, tiled=True)  11 us
    all_to_all x2, starting transfers between devices, fetch(): lax.all_to_all(picked, 'dp', 0, 0, tiled=True).reshape(owners * CAP, D)  10.6 us
    all_to_all x1, waiting for transfers between devices, layer(): wanted = lax.all_to_all(send, ('dp', 'xh', 'yh'), 0, 0, tiled=True)  8.74 us
  transfers between devices with their start and end apart: 9, of which 4 were waited for; matrix products, arithmetic and copies ran while one was open for 1% of the time, Pallas kernels for 27%

profile of v11, /device:TPU:8, one launch (start us, length us, event | category | flops | bytes accessed | tf_op | source)
XLA Modules:
  0.0 141.4 jit_solution(11324551795372175865)
XLA Ops:
  0.0 0.7 broadcast_in_dim.63
  1.4 11.0 %all-to-all-start = ((s32[32,1,256]{2,1,0:T(1,128)}), s32[32,1,256]{2,1,0:T(1,128)S(1)}, u32[]{:S(2)}, u32[]{:S(2)}) async-start(s32[32,1,256]{2,1,0:T(1,128)} %broadcast_in_dim.64), calls=%async_computation | async-start | bytes 65536 | tf_op jit(solution)/shard_map/all_to_all | solution.py:376
  12.4 8.7 %all-to-all-done = s32[32,1,256]{2,1,0:T(1,128)S(1)} async-done(((s32[32,1,256]{2,1,0:T(1,128)}), s32[32,1,256]{2,1,0:T(1,128)S(1)}, u32[]{:S(2)}, u32[]{:S(2)}) %all-to-all-start) | async-done | bytes 32800 | tf_op jit(solution)/shard_map/all_to_all | solution.py:376
  21.3 0.9 fusion.28
  22.4 0.9 select_reduce_fusion.rows_ref.ids_ref
  23.3 6.6 %shard_map.56 = bf16[1024,512]{1,0:T(8,128)(2,1)} custom-call(s32[8,128]{1,0:T(8,128)} %select_reduce_fusion.rows_ref.ids_ref, s32[8]{0:T(128)} %get-tuple-element.59.count_ref, s32[8,128]{1,0:T(8,128)} %select_reduce_fusion.rows_ref.ids_ref, bf16[2048,8,512]{2,1,0:T(8,128)(2,1)} %bitcast.29), custom_call_target="tpu_custom_call" | custom-call | flops 28000000 | tf_op jit(solution)/shard_map/pallas_call | solution.py:105
  29.9 5.9 %all-to-all-start.2 = ((bf16[8,128,512]{2,1,0:T(8,128)(2,1)}), bf16[8,128,512]{2,1,0:T(8,128)(2,1)S(1)}, u32[]{:S(2)}, u32[]{:S(2)}) async-start(bf16[8,128,512]{2,1,0:T(8,128)(2,1)} %bitcast.31), calls=%async_computation.2 | async-start | bytes 2097152 | tf_op jit(solution)/shard_map/all_to_all | solution.py:395
  36.2 0.9 select_reduce_fusion.1.rows_ref.ids_ref
  37.0 7.9 %shard_map.55 = bf16[1024,512]{1,0:T(8,128)(2,1)} custom-call(s32[8,128]{1,0:T(8,128)} %select_reduce_fusion.1.rows_ref.ids_ref, s32[8]{0:T(128)} %get-tuple-element.60.count_ref, s32[8,128]{1,0:T(8,128)} %select_reduce_fusion.1.rows_ref.ids_ref, bf16[2048,8,512]{2,1,0:T(8,128)(2,1)} %bitcast.30), custom_call_target="tpu_custom_call" | custom-call | flops 28000000 | tf_op jit(solution)/shard_map/pallas_call | solution.py:105
  44.9 2.9 %all-to-all-done.2 = bf16[8,128,512]{2,1,0:T(8,128)(2,1)S(1)} async-done(((bf16[8,128,512]{2,1,0:T(8,128)(2,1)}), bf16[8,128,512]{2,1,0:T(8,128)(2,1)S(1)}, u32[]{:S(2)}, u32[]{:S(2)}) %all-to-all-start.2) | async-done | bytes 1048608 | tf_op jit(solution)/shard_map/all_to_all | solution.py:395
  47.8 4.7 %all-to-all-start.1 = ((bf16[8,128,512]{2,1,0:T(8,128)(2,1)}), bf16[8,128,512]{2,1,0:T(8,128)(2,1)}, u32[]{:S(2)}, u32[]{:S(2)}) async-start(bf16[8,128,512]{2,1,0:T(8,128)(2,1)} %bitcast.32), calls=%async_computation.1 | async-start | bytes 2097152 | tf_op jit(solution)/shard_map/all_to_all | solution.py:395
  53.0 1.8 %place.3 = (bf16[512,512]{1,0:T(8,128)(2,1)}, s32[8,128]{1,0:T(8,128)S(1)}) custom-call(s32[1,512]{1,0:T(1,128)S(1)} %multiply_add_fusion.at_ref, s32[8,128]{1,0:T(8,128)S(1)} %select_reduce_fusion.2.length_ref, bf16[1024,512]{1,0:T(8,128)(2,1)S(1)} %bitcast.28), custom_call_target="tpu_custom_call" | custom-call | flops 6000000 | tf_op jit(solution)/shard_map/place/pallas_call | solution.py:125
  54.8 0.7 collective-permute-start.2
  55.6 10.1 %all-to-all-done.1 = bf16[8,128,512]{2,1,0:T(8,128)(2,1)} async-done(((bf16[8,128,512]{2,1,0:T(8,128)(2,1)}), bf16[8,128,512]{2,1,0:T(8,128)(2,1)}, u32[]{:S(2)}, u32[]{:S(2)}) %all-to-all-start.1) | async-done | bytes 1048608 | tf_op jit(solution)/shard_map/all_to_all | solution.py:395
  65.7 2.2 %place.2 = (bf16[512,512]{1,0:T(8,128)(2,1)S(1)}, s32[8,128]{1,0:T(8,128)S(1)}) custom-call(s32[1,512]{1,0:T(1,128)S(1)} %multiply_add_fusion.1.at_ref, s32[8,128]{1,0:T(8,128)S(1)} %select_reduce_fusion.2.length_ref, bf16[1024,512]{1,0:T(8,128)(2,1)} %bitcast.3.got_ref), custom_call_target="tpu_custom_call" | custom-call | flops 6000000 | tf_op jit(solution)/shard_map/place/pallas_call | solution.py:125
  67.9 1.5 %collective-permute-start.4 = (bf16[512,512]{1,0:T(8,128)(2,1)S(1)}, bf16[512,512]{1,0:T(8,128)(2,1)S(1)}, u32[]{:S(2)}, u32[]{:S(2)}) collective-permute-start(bf16[512,512]{1,0:T(8,128)(2,1)S(1)} %get-tuple-element.33.p1), channel_id=1, source_target_pairs={{0,4},{4,0},{1,5},{5,1},{2,6},{6,2},{3,7},{7,3},{8,12},{12,8},{9,1... | collective-permute-start | bytes 1572872 | tf_op jit(solution)/shard_map/ppermute | solution.py:410
  70.0 11.6 %collective-permute-done.4.refs_4_ = bf16[512,512]{1,0:T(8,128)(2,1)S(1)} collective-permute-done((bf16[512,512]{1,0:T(8,128)(2,1)S(1)}, bf16[512,512]{1,0:T(8,128)(2,1)S(1)}, u32[]{:S(2)}, u32[]{:S(2)}) %collective-permute-start.4) | collective-permute-done | bytes 524320 | tf_op jit(solution)/shard_map/ppermute | solution.py:410
  81.6 6.8 %shard_map.57 = (bf16[1024,512]{1,0:T(8,128)(2,1)}, bf16[512,1024]{1,0:T(8,128)(2,1)}, bf16[512,256]{1,0:T(8,128)(2,1)}, bf16[512,256]{1,0:T(8,128)(2,1)}, bf16[256,512]{1,0:T(8,128)(2,1)}, /*index=5*/f32[512,256]{1,0:T(8,128)}) custom-call(s32[8,128]{1,0:T(8,128)S(1)} %get-tuple-element.34.length_ref, bf16[512,512]{1,0:T(8,128)(2,1)} %get-tuple-element.35.p1, ...), custom_call_target="tpu_custom_call" | custom-call | flops 24000000 | tf_op jit(solution)/shard_map/pallas_call | solution.py:320
  88.4 5.8 %shard_map.58 = (bf16[1024,512]{1,0:T(8,128)(2,1)}, bf16[512,1024]{1,0:T(8,128)(2,1)}, bf16[512,256]{1,0:T(8,128)(2,1)}, bf16[512,256]{1,0:T(8,128)(2,1)}, bf16[256,512]{1,0:T(8,128)(2,1)}, /*index=5*/f32[512,256]{1,0:T(8,128)}) custom-call(s32[8,128]{1,0:T(8,128)S(1)} %get-tuple-element.34.length_ref, bf16[512,512]{1,0:T(8,128)(2,1)S(1)} %collective-permute-done.2.p1, ...), custom_call_target="tpu_custom_call" | custom-call | flops 24000000 | tf_op jit(solution)/shard_map/pallas_call | solution.py:320
  94.2 10.3 %shard_map.59 = (bf16[1024,512]{1,0:T(8,128)(2,1)S(1)}, bf16[512,1024]{1,0:T(8,128)(2,1)S(1)}, bf16[512,256]{1,0:T(8,128)(2,1)S(1)}, bf16[512,256]{1,0:T(8,128)(...) custom-call(s32[8,128]{1,0:T(8,128)S(1)} %get-tuple-element.32.lengt, ...), custom_call_target="tpu_custom_call" | custom-call | flops 36000000 | tf_op jit(solution)/shard_map/pallas_call | solution.py:320
  104.5 3.6 %shard_map.60.refs_13_ = f32[512,256]{1,0:T(8,128)S(1)} custom-call(bf16[1024,512]{1,0:T(8,128)(2,1)S(1)} %get-tuple-element.48.k0.refs_0_, bf16[512,1024]{1,0:T(8,128)(2,1)S(1)} %get-tuple-element.49.v0.refs_1_, bf16[1024,512]{1,0:T(8,128)(2,1)S(1)} %get-tuple-element.50.k1.refs_2_, bf16[512,1024]{1,0:T(8,128)(2,1)S(1)} %get-tuple-element.51.v1.refs_3_, ...), custom_call_target="tpu_custom_call" | custom-call | flops 20000000 | tf_op jit(solution)/shard_map/pallas_call | solution.py:320
  108.1 10.4 %shard_map.61 = bf16[1024,512]{1,0:T(8,128)(2,1)S(1)} custom-call(s32[8,128]{1,0:T(8,128)S(1)} %get-tuple-element.32.length_ref, bf16[1024,512]{1,0:T(8,128)(2,1)S(1)} %get-tuple-element.48.k0.refs_0_, bf16[512,1024]{1,0:T(8,128)(2,1)S(1)} %get-tuple-element.49.v0.refs_1_, bf16[1024,512]{1,0:T(8,128)(2,1)S(1)} %get-tuple-element.50.k1.refs_2_, ...), custom_call_target="tpu_custom_call" | custom-call | flops 44000000 | tf_op jit(solution)/shard_map/pallas_call | solution.py:320
  118.5 21.9 %all_to_all.20 = bf16[16,64,512]{2,1,0:T(8,128)(2,1)S(1)} all-to-all(bf16[16,64,512]{2,1,0:T(8,128)(2,1)S(1)} %bitcast.27), channel_id=1, replica_groups=mesh['dp'=8,'xh'=2,'xl'=2,'yh'=2,'co'=2] {'xh','yh','xl','co'}, dimensions={0} | all-to-all | bytes 2097152 | tf_op jit(solution)/shard_map/all_to_all | solution.py:425
  140.4 1.0 copy.14
  (35 shorter events, 2.5 us)
Async XLA Ops:
  1.4 19.8 %all-to-all-start = ((s32[32,1,256]{2,1,0:T(1,128)}), s32[32,1,256]{2,1,0:T(1,128)S(1)}, u32[]{:S(2)}, u32[]{:S(2)}) async-start(s32[32,1,256]{2,1,0:T(1,128)} %broadcast_in_dim.64), calls=%async_computation | async-start | bytes 65536 | tf_op jit(solution)/shard_map/all_to_all | solution.py:376
  29.9 5.9 %copy-start.2 = (s32[4]{0:T(128)S(1)}, s32[4]{0:T(128)}, u32[]{:S(2)}) copy-start(s32[4]{0:T(128)} %param.6) | copy-start | bytes 52
  29.9 17.9 %all-to-all-start.2 = ((bf16[8,128,512]{2,1,0:T(8,128)(2,1)}), bf16[8,128,512]{2,1,0:T(8,128)(2,1)S(1)}, u32[]{:S(2)}, u32[]{:S(2)}) async-start(bf16[8,128,512]{2,1,0:T(8,128)(2,1)} %bitcast.31), calls=%async_computation.2 | async-start | bytes 2097152 | tf_op jit(solution)/shard_map/all_to_all | solution.py:395
  47.8 17.9 %all-to-all-start.1 = ((bf16[8,128,512]{2,1,0:T(8,128)(2,1)}), bf16[8,128,512]{2,1,0:T(8,128)(2,1)}, u32[]{:S(2)}, u32[]{:S(2)}) async-start(bf16[8,128,512]{2,1,0:T(8,128)(2,1)} %bitcast.32), calls=%async_computation.1 | async-start | bytes 2097152 | tf_op jit(solution)/shard_map/all_to_all | solution.py:395
  52.4 29.1 %copy-start = (bf16[512,2048]{1,0:T(8,128)(2,1)S(1)}, bf16[512,2048]{1,0:T(8,128)(2,1)}, u32[]{:S(2)}) copy-start(bf16[512,2048]{1,0:T(8,128)(2,1)} %refs_6_.1) | copy-start | bytes 6291460
  54.8 14.6 %collective-permute-start.2 = (bf16[512,512]{1,0:T(8,128)(2,1)}, bf16[512,512]{1,0:T(8,128)(2,1)S(1)}, u32[]{:S(2)}, u32[]{:S(2)}) collective-permute-start(bf16[512,512]{1,0:T(8,128)(2,1)} %get-tuple-element.35.p1), channel_id=1, source_target_pairs={{0,4},{4,0},{1,5},{5,1},{2,6},{6,2},{3,7},{7,3},{8,12},{12,8},{9,1... | collective-permute-start | bytes 1572872 | tf_op jit(solution)/shard_map/ppermute | solution.py:410
  67.9 13.6 %collective-permute-start.4 = (bf16[512,512]{1,0:T(8,128)(2,1)S(1)}, bf16[512,512]{1,0:T(8,128)(2,1)S(1)}, u32[]{:S(2)}, u32[]{:S(2)}) collective-permute-start(bf16[512,512]{1,0:T(8,128)(2,1)S(1)} %get-tuple-element.33.p1), channel_id=1, source_target_pairs={{0,4},{4,0},{1,5},{5,1},{2,6},{6,2},{3,7},{7,3},{8,12},{12,8},{9,1... | collective-permute-start | bytes 1572872 | tf_op jit(solution)/shard_map/ppermute | solution.py:410
  69.4 12.1 %collective-permute-start.1 = (bf16[512,512]{1,0:T(8,128)(2,1)}, bf16[512,512]{1,0:T(8,128)(2,1)S(1)}, u32[]{:S(2)}, u32[]{:S(2)}) collective-permute-start(bf16[512,512]{1,0:T(8,128)(2,1)} %get-tuple-element.35.p1), channel_id=1, source_target_pairs={{0,1},{1,0},{2,3},{3,2},{4,5},{5,4},{6,7},{7,6},{8,9},{9,8},{10,11... | collective-permute-start | bytes 1572872 | tf_op jit(solution)/shard_map/ppermute | solution.py:411
  69.4 18.9 %collective-permute-start.3 = (bf16[512,512]{1,0:T(8,128)(2,1)S(1)}, bf16[512,512]{1,0:T(8,128)(2,1)S(1)}, u32[]{:S(2)}, u32[]{:S(2)}) collective-permute-start(bf16[512,512]{1,0:T(8,128)(2,1)S(1)} %collective-permute-done.2.p1), channel_id=1, source_target_pairs={{0,1},{1,0},{2,3},{3,2},{4,5},{5,4},{6,7},{7,6},{8,9},{9,8},{10,11... | collective-permute-start | bytes 1572872 | tf_op jit(solution)/shard_map/ppermute | solution.py:412
  70.0 24.2 %collective-permute-start = (bf16[512,512]{1,0:T(8,128)(2,1)S(1)}, bf16[512,512]{1,0:T(8,128)(2,1)S(1)}, u32[]{:S(2)}, u32[]{:S(2)}) collective-permute-start(bf16[512,512]{1,0:T(8,128)(2,1)S(1)} %get-tuple-element.33.p1), channel_id=1, source_target_pairs={{0,1},{1,0},{2,3},{3,2},{4,5},{5,4},{6,7},{7,6},{8,9},{9,8},{10,11... | collective-permute-start | bytes 1572872 | tf_op jit(solution)/shard_map/ppermute | solution.py:411
  81.5 26.6 %collective-permute-start.5 = (bf16[512,512]{1,0:T(8,128)(2,1)S(1)}, bf16[512,512]{1,0:T(8,128)(2,1)S(1)}, u32[]{:S(2)}, u32[]{:S(2)}) collective-permute-start(bf16[512,512]{1,0:T(8,128)(2,1)S(1)} %collective-permute-done.4.refs_4_), channel_id=1, source_target_pairs={{0,1},{1,0},{2,3},{3,2},{4,5},{5,4},{6,7},{7,6},{8,9},{9,8},{10,11... | collective-permute-start | bytes 1572872 | tf_op jit(solution)/shard_map/ppermute | solution.py:412
  104.5 3.6 %copy-start.1 = (bf16[512,512]{1,0:T(8,128)(2,1)S(1)}, bf16[512,512]{1,0:T(8,128)(2,1)}, u32[]{:S(2)}) copy-start(bf16[512,512]{1,0:T(8,128)(2,1)} %refs_7_.1) | copy-start | bytes 1572868
